TPU v7x, 16 devices: a 4x2x1 block of a 4x4x8 slice. The times are simulated.
16 devices in a mesh: dp: 2 (over y, z), tp: 8 (over x, core).
Axes of the slice: x: 4, y: 2, z: 1, core: 2. Of those that a mesh axis runs over, the one named last changes fastest.
The devices are a block of a 4x4x8 slice.
Arguments:
- query: bfloat16 [128, 32, 128], P('dp', 'tp'), parts along dimension 0
- k_cache: bfloat16 [128, 1024, 8, 128], P('dp', None, 'tp'), parts along dimension 0
- v_cache: bfloat16 [128, 1024, 8, 128], P('dp', None, 'tp'), parts along dimension 0
- k_new: bfloat16 [128, 8, 128], P('dp', 'tp'), parts along dimension 0
- v_new: bfloat16 [128, 8, 128], P('dp', 'tp'), parts along dimension 0
- lens: int32 [128], P('dp'), parts along dimension 0
Outputs:
- output 1: bfloat16 [128, 32, 128], P('dp', 'tp'), parts along dimension 0
- output 2: bfloat16 [128, 1024, 8, 128], P('dp', 'tp'), parts along dimension 0
- output 3: bfloat16 [128, 1024, 8, 128], P('dp', 'tp'), parts along dimension 0
There are 2 independent parts. A program takes and returns all parts, laid end to end along the dimension named above; each array names one.
All inputs are finite; a program needn't handle non-finite values.
Results may differ from a plain program's by a relative error of at most 0.00772032.
Values are sent between devices in bfloat16 or wider.
A program may use at most 768 MiB of HBM per device.

v0:
```python
import jax
import jax.numpy as jnp
from jax import lax
from jax.sharding import PartitionSpec as P

MASK_VALUE = -1e30


def solution(mesh):
    def local_step(query, k_cache, v_cache, k_new, v_new, lens):
        batch, seq_len, head_dim = k_cache.shape[0], k_cache.shape[1], k_cache.shape[3]
        positions = lax.broadcasted_iota(jnp.int32, (1, seq_len, 1, 1), 1)
        new_slot = positions == lens[:, None, None, None]
        k_upd = jnp.where(new_slot, k_new[:, None], k_cache)
        v_upd = jnp.where(new_slot, v_new[:, None], v_cache)
        k_seq = lax.all_to_all(k_upd, "tp", 1, 2, tiled=True)
        v_seq = lax.all_to_all(v_upd, "tp", 1, 2, tiled=True)
        q_all = lax.all_gather(query, "tp", axis=1, tiled=True)
        seq_local, kv_heads = k_seq.shape[1], k_seq.shape[2]
        q_heads = q_all.shape[1]
        q_grp = q_all.reshape(batch, kv_heads, q_heads // kv_heads, head_dim)
        scores = jnp.einsum("bhgd,bthd->bhgt", q_grp, k_seq, preferred_element_type=jnp.float32) * (head_dim ** -0.5)
        tok_pos = lax.axis_index("tp") * seq_local + lax.broadcasted_iota(jnp.int32, (1, 1, 1, seq_local), 3)
        valid = tok_pos <= lens[:, None, None, None]
        scores = jnp.where(valid, scores, MASK_VALUE)
        part_max = jnp.max(scores, axis=-1)
        weights = jnp.where(valid, jnp.exp(scores - part_max[..., None]), 0.0)
        part_sum = jnp.sum(weights, axis=-1)
        part_out = jnp.einsum("bhgt,bthd->bhgd", weights.astype(jnp.bfloat16), v_seq, preferred_element_type=jnp.float32)
        glob_max = lax.pmax(part_max, "tp")
        factor = jnp.exp(part_max - glob_max)
        stacked = jnp.concatenate([part_out * factor[..., None], (part_sum * factor)[..., None]], axis=-1)
        stacked = stacked.reshape(batch, q_heads, head_dim + 1)
        own_heads = lax.psum_scatter(stacked, "tp", scatter_dimension=1, tiled=True)
        attn_out = (own_heads[..., :head_dim] / own_heads[..., head_dim:]).astype(jnp.bfloat16)
        return attn_out, k_seq, v_seq

    head_spec = P("dp", "tp")
    entry_spec = P("dp", None, "tp")
    return jax.shard_map(local_step, mesh=mesh, in_specs=(head_spec, entry_spec, entry_spec, head_spec, head_spec, P("dp")), out_specs=(head_spec, P("dp", "tp"), P("dp", "tp")), check_vma=False)
```

profile of v0, /device:TPU:113, one launch (start us, length us, event | category | flops | bytes accessed | tf_op | source)
XLA Modules:
  0.0 582.2 jit_solution(2543007647335509637)
XLA Ops:
  7.2 0.7 iota_compare_fusion
  7.9 68.6 %copy_select_fusion = (bf16[64,1024,1,128]{3,0,2,1:T(8,128)(2,1)}, bf16[64,1024,1,128]{3,0,2,1:T(8,128)(2,1)S(1)}) fusion(bf16[64,1024,1,128]{3,1,2,0:T(8,128)(2,1)} %param.8, pred[64,1024]{0,1:T(8,128)(4,1)S(1)} %iota_compare_fusion, bf16[64,128]{1,0:T(8,128)(2,1)} %bitcast.28, bf16[64,1024,1,128]{3,1,2,0:T(8,128)(2,1)} %param.7, bf16[64,128]{1,0:T(8,128)(2,1)} %bitcast.29), kind=kLoop, calls=%fused_computation | loop fusion | flops 16777216 | bytes 67207168 | tf_op jit(solution)/shard_map/jit(_where)/select_n | solution.py:15
  76.5 189.3 %all_to_all.36 = bf16[64,1024,1,128]{3,0,2,1:T(8,128)(2,1)} all-to-all(bf16[64,1024,1,128]{3,0,2,1:T(8,128)(2,1)S(1)} %get-tuple-element.18), channel_id=1, replica_groups=mesh['dp'=2,'tp'=8] {'tp'}, dimensions={1} | all-to-all | bytes 33554432 | tf_op jit(solution)/shard_map/all_to_all | solution.py:16
  265.9 6.8 %all-to-all-start.1 = ((bf16[64,1024,1,128]{3,0,2,1:T(8,128)(2,1)}), bf16[64,1024,1,128]{3,0,2,1:T(8,128)(2,1)}, u32[]{:S(2)}, u32[]{:S(2)}) async-start(bf16[64,1024,1,128]{3,0,2,1:T(8,128)(2,1)} %get-tuple-element.17), calls=%async_computation.1 | async-start | bytes 33554432 | tf_op jit(solution)/shard_map/all_to_all | solution.py:17
  272.7 195.4 %all_gather.3 = bf16[64,32,128]{2,0,1:T(8,128)(2,1)S(1)} all-gather(bf16[64,4,128]{2,0,1:T(8,128)(2,1)S(1)} %copy.32), channel_id=1, replica_groups=mesh['dp'=2,'tp'=8] {'tp'}, dimensions={1}, use_global_device_ids=true | all-gather | bytes 589824 | tf_op jit(solution)/shard_map/all_gather | solution.py:18
  468.1 0.3 copy.33
  468.5 0.1 broadcast_compare_fusion
  468.6 9.7 %copy.31 = bf16[64,1024,1,128]{3,1,0,2:T(8,128)(2,1)S(1)} copy(bf16[64,1024,1,128]{3,0,2,1:T(8,128)(2,1)} %all_to_all.36) | data formatting | bytes 33554432 | tf_op jit(solution)/shard_map/all_to_all | solution.py:16
  478.3 9.8 %fusion.11 = (f32[64,8,4]{2,1,0:T(8,128)S(1)}, f32[64,8,4,128]{3,2,1,0:T(4,128)}) fusion(bf16[64,128,8,128]{3,1,2,0:T(8,128)(2,1)S(1)} %bitcast.23, bf16[64,8,4,128]{3,2,1,0:T(4,128)(2,1)S(1)} %bitcast.25, pred[64,128]{1,0:T(8,128)(4,1)S(1)} %broadcast_compare_fusion), kind=kOutput, calls=%fused_computation.22 | convolution fusion | flops 67893248 | bytes 18366464 | tf_op jit(solution)/shard_map/bhgd,bthd->bhgt/dot_general | solution.py:22
  488.0 27.9 %pmax.7 = f32[64,8,4]{2,1,0:T(8,128)S(1)} all-reduce(f32[64,8,4]{2,1,0:T(8,128)S(1)} %get-tuple-element.19), channel_id=1, replica_groups=mesh['dp'=2,'tp'=8] {'tp'}, use_global_device_ids=true, to_apply=%region_1.2 | all-reduce | flops 2048 | bytes 16384 | tf_op jit(solution)/shard_map/pmax | solution.py:30
  515.9 2.4 fusion.2
  518.3 0.1 fusion.10
  518.4 9.8 %copy.35 = bf16[64,1024,1,128]{3,1,0,2:T(8,128)(2,1)S(1)} copy(bf16[64,1024,1,128]{3,0,2,1:T(8,128)(2,1)} %all-to-all-done.1) | data formatting | bytes 33554432 | tf_op jit(solution)/shard_map/all_to_all | solution.py:17
  528.2 4.6 convolution_multiply_fusion
  532.8 0.6 copy.37
  533.4 0.1 copy.36
  533.6 0.4 copy.38
  534.0 1.5 pad_maximum_fusion
  535.5 0.1 reduce-scatter.2.cloned.1.call-update
  535.6 18.5 %copy.40 = bf16[64,128,8,128]{3,2,1,0:T(8,128)(2,1)} copy(bf16[64,128,8,128]{3,0,1,2:T(8,128)(2,1)} %bitcast.22) | data formatting | bytes 33554432
  554.1 18.5 %copy.41 = bf16[64,128,8,128]{3,2,1,0:T(8,128)(2,1)} copy(bf16[64,128,8,128]{3,0,1,2:T(8,128)(2,1)} %bitcast.17) | data formatting | bytes 33554432
  572.6 1.0 slice_reduce_fusion
  573.6 1.0 fusion.8
  574.7 0.7 copy.39
  (11 shorter events, 0.0 us)
Async XLA Ops:
  265.9 6.8 %copy-start.1 = (bf16[64,4,128]{2,1,0:T(4,128)(2,1)S(1)}, bf16[64,4,128]{2,1,0:T(4,128)(2,1)}, u32[]{:S(2)}) copy-start(bf16[64,4,128]{2,1,0:T(4,128)(2,1)} %param.6) | copy-start | bytes 196612
  265.9 202.6 %copy-start.2 = (s32[64]{0:T(128)S(1)}, s32[64]{0:T(128)}, u32[]{:S(2)}) copy-start(s32[64]{0:T(128)} %param.11) | copy-start | bytes 772
  265.9 252.5 %all-to-all-start.1 = ((bf16[64,1024,1,128]{3,0,2,1:T(8,128)(2,1)}), bf16[64,1024,1,128]{3,0,2,1:T(8,128)(2,1)}, u32[]{:S(2)}, u32[]{:S(2)}) async-start(bf16[64,1024,1,128]{3,0,2,1:T(8,128)(2,1)} %get-tuple-element.17), calls=%async_computation.1 | async-start | bytes 33554432 | tf_op jit(solution)/shard_map/all_to_all | solution.py:17
  272.7 299.9 %reduce-scatter.2.cloned.1.call-start = ((), (), s32[]{:S(2)}) async-start(), calls=%async_computation.3 | async-start | bytes 2359296 | tf_op jit(solution)/shard_map/reduce_scatter | solution.py:34
  518.4 9.8 %copy-start = (f32[64,8,4,128]{3,2,1,0:T(4,128)S(1)}, f32[64,8,4,128]{3,2,1,0:T(4,128)}, u32[]{:S(2)}) copy-start(f32[64,8,4,128]{3,2,1,0:T(4,128)} %get-tuple-element.20) | copy-start | bytes 3145732
Sparse Core Ops, SparseCore 0:
  535.7 28.7 reduce-scatter.1
where the time goes:
time: 586 us; the launch traced here: 582 us
  blocking collectives  413 us (70%)
  other arithmetic  74.4 us (13%)
  local copies, waits for them, and re-layouts  59.8 us (10%)
  matrix products  14.3 us (2%)
  between operations  14.2 us (2%)
  starting transfers between devices  6.82 us (1%)
    all_gather x1, blocking collectives, local_step(): q_all = lax.all_gather(query, 'tp', axis=1, tiled=True)  195 us
    all_to_all x1, blocking collectives, local_step(): k_seq = lax.all_to_all(k_upd, 'tp', 1, 2, tiled=True)  189 us
    select_n x1, other arithmetic, local_step(): v_upd = jnp.where(new_slot, v_new[:, None], v_cache)  68.6 us
    unnamed x10, local copies, waits for them, and re-layouts  37.8 us
    pmax x1, blocking collectives, local_step(): glob_max = lax.pmax(part_max, 'tp')  27.9 us
  transfers between devices with their start and end apart: 2, of which 0 were waited for; matrix products, arithmetic and copies ran while one was open for 10% of the time, Pallas kernels for 0%

commit v1 on v0

v1 whole, which is shorter than its diff:
```python
import functools

import jax
import jax.numpy as jnp
from jax import lax
from jax.experimental import pallas as pl
from jax.experimental.pallas import tpu as pltpu
from jax.sharding import PartitionSpec as P

MESH = pl.DeviceIdType.MESH
MASK_VALUE = -1e30


def exchange_kernel(n, q_ref, k_ref, v_ref, kn_ref, vn_ref, lens_ref,
                    out_ref, kx_ref, vx_ref, knx_ref, vnx_ref,
                    kbuf, vbuf, kn32, vn32, send_sem, recv_sem, small_send, small_recv, load_sem, keep_sem):
    dp, me = lax.axis_index("dp"), lax.axis_index("tp")
    batch, seq_len, head_dim = k_ref.shape
    seq_local = seq_len // n

    barrier = pltpu.get_barrier_semaphore()
    for step in range(1, n):
        pl.semaphore_signal(barrier, inc=1, device_id=(dp, lax.rem(me + step, n)), device_id_type=MESH)
    pl.semaphore_wait(barrier, n - 1)

    def rows(peer):
        return pl.ds(pl.multiple_of(peer * seq_local, seq_local), seq_local)

    copies = []
    for a, (src, dst) in enumerate(((k_ref, kx_ref), (v_ref, vx_ref))):
        for slot, step in enumerate(STEPS):
            peer = lax.rem(me + step, n)
            copy = pltpu.make_async_remote_copy(
                src_ref=src.at[:, rows(peer)], dst_ref=dst.at[me],
                send_sem=send_sem.at[a, slot], recv_sem=recv_sem.at[a, slot],
                device_id=(dp, peer), device_id_type=MESH)
            copy.start()
            copies.append(copy)
    for a, (src, dst) in enumerate(((kn_ref, knx_ref), (vn_ref, vnx_ref))):
        for slot, step in enumerate(STEPS):
            copy = pltpu.make_async_remote_copy(
                src_ref=src, dst_ref=dst.at[me],
                send_sem=small_send.at[a, slot], recv_sem=small_recv.at[a, slot],
                device_id=(dp, lax.rem(me + step, n)), device_id_type=MESH)
            copy.start()
            copies.append(copy)
    own_new = [pltpu.make_async_copy(kn_ref, knx_ref.at[me], keep_sem.at[0, 2]),
               pltpu.make_async_copy(vn_ref, vnx_ref.at[me], keep_sem.at[1, 2])]
    for copy in own_new:
        copy.start()

    kn32[...] = kn_ref[...].astype(jnp.float32)
    vn32[...] = vn_ref[...].astype(jnp.float32)

    def load(a, b, slot):
        src, dst = ((k_ref, kbuf), (v_ref, vbuf))[a]
        return pltpu.make_async_copy(src.at[b], dst.at[slot], load_sem.at[a, slot])

    def keep(a, b, slot):
        src, dst = ((kbuf, kx_ref), (vbuf, vx_ref))[a]
        return pltpu.make_async_copy(src.at[slot, rows(me)], dst.at[me, b], keep_sem.at[a, slot])

    for a in range(2):
        load(a, 0, 0).start()
    scale = head_dim ** -0.5
    positions = lax.broadcasted_iota(jnp.int32, (1, seq_len), 1)

    def attend(b, carry):
        slot = lax.rem(b, 2)
        for a in range(2):
            load(a, b, slot).wait()
            keep(a, b, slot).start()

        @pl.when(b > 0)
        def _():
            for a in range(2):
                keep(a, b - 1, 1 - slot).wait()

        @pl.when(b + 1 < batch)
        def _():
            for a in range(2):
                load(a, b + 1, 1 - slot).start()

        length = lens_ref[b]
        query = q_ref[b]
        new_k, new_v = kn32[pl.ds(b, 1), :], vn32[pl.ds(b, 1), :]
        scores = lax.dot_general(query, kbuf[slot], (((1,), (1,)), ((), ())), preferred_element_type=jnp.float32)
        new_score = jnp.sum(query.astype(jnp.float32) * new_k, axis=-1, keepdims=True)
        is_new = positions == length
        scores = jnp.where(is_new, new_score, scores) * scale
        scores = jnp.where(positions <= length, scores, MASK_VALUE)
        weights = jnp.exp(scores - jnp.max(scores, axis=-1, keepdims=True))
        weights = weights / jnp.sum(weights, axis=-1, keepdims=True)
        probs = weights.astype(jnp.bfloat16)
        old = jnp.where(is_new, 0.0, weights).astype(jnp.bfloat16)
        summed = jnp.dot(old, vbuf[slot], preferred_element_type=jnp.float32)
        new_prob = jnp.sum(jnp.where(is_new, probs.astype(jnp.float32), 0.0), axis=-1, keepdims=True)
        out_ref[b] = (summed + new_prob * new_v).astype(jnp.bfloat16)
        return carry

    lax.fori_loop(0, batch, attend, 0)
    for a in range(2):
        keep(a, batch - 1, (batch - 1) % 2).wait()
    for copy in own_new:
        copy.wait()
    for copy in copies:
        copy.wait()


STEPS = (4, 5, 3, 2, 6, 1, 7)


def relayout_kernel(n, lens_ref, kx_ref, vx_ref, knx_ref, vnx_ref, ko_ref, vo_ref, wide, kn32, vn32):
    block, seq_local = ko_ref.shape[0], ko_ref.shape[1]
    batch = knx_ref.shape[1]
    step = pl.program_id(0)
    base = lax.axis_index("tp") * seq_local

    @pl.when(step == 0)
    def _():
        for h in range(n):
            kn32[pl.ds(h, batch, stride=n), :] = knx_ref[h].astype(jnp.float32)
            vn32[pl.ds(h, batch, stride=n), :] = vnx_ref[h].astype(jnp.float32)

    for a, (src, dst, new) in enumerate(((kx_ref, ko_ref, kn32), (vx_ref, vo_ref, vn32))):
        for i in range(block):
            s = (a * block + i) % 2
            for h in range(n):
                wide[s, pl.ds(h, seq_local, stride=n), :] = src[h, i].astype(jnp.float32)
            dst[i] = wide[s].reshape(seq_local, n, -1).astype(jnp.bfloat16)
            b = step * block + i
            row = lens_ref[b] - base

            @pl.when((row >= 0) & (row < seq_local))
            def _():
                dst[i, row] = new[pl.ds(pl.multiple_of(b * n, n), n), :].astype(jnp.bfloat16)


def solution(mesh):
    n = mesh.shape["tp"]

    def local_step(query, k_cache, v_cache, k_new, v_new, lens):
        batch, seq_len, _, head_dim = k_cache.shape
        seq_local = seq_len // n
        k_cache = k_cache.reshape(batch, seq_len, head_dim)
        v_cache = v_cache.reshape(batch, seq_len, head_dim)
        k_new = k_new.reshape(batch, head_dim)
        v_new = v_new.reshape(batch, head_dim)
        dtype = k_cache.dtype
        any_spec = pl.BlockSpec(memory_space=pl.ANY)
        vmem_spec = pl.BlockSpec(memory_space=pltpu.VMEM)
        smem_spec = pl.BlockSpec(memory_space=pltpu.SMEM)
        held = jax.ShapeDtypeStruct((n, batch, seq_local, head_dim), dtype)
        held_new = jax.ShapeDtypeStruct((n, batch, head_dim), dtype)
        attn_out, kx, vx, knx, vnx = pl.pallas_call(
            functools.partial(exchange_kernel, n),
            name="exchange_attend",
            out_shape=[jax.ShapeDtypeStruct(query.shape, dtype), held, held, held_new, held_new],
            in_specs=[vmem_spec, any_spec, any_spec, vmem_spec, vmem_spec, smem_spec],
            out_specs=[vmem_spec, any_spec, any_spec, any_spec, any_spec],
            scratch_shapes=[
                pltpu.VMEM((2, seq_len, head_dim), dtype),
                pltpu.VMEM((2, seq_len, head_dim), dtype),
                pltpu.VMEM((batch, head_dim), jnp.float32),
                pltpu.VMEM((batch, head_dim), jnp.float32),
                pltpu.SemaphoreType.DMA((2, n - 1)),
                pltpu.SemaphoreType.DMA((2, n - 1)),
                pltpu.SemaphoreType.DMA((2, n - 1)),
                pltpu.SemaphoreType.DMA((2, n - 1)),
                pltpu.SemaphoreType.DMA((2, 2)),
                pltpu.SemaphoreType.DMA((2, 3)),
            ],
            compiler_params=pltpu.CompilerParams(collective_id=0, has_side_effects=True),
        )(query, k_cache, v_cache, k_new, v_new, lens)

        block = 2
        moved = jax.ShapeDtypeStruct((batch, seq_local, n, head_dim), dtype)
        in_block = pl.BlockSpec((n, block, seq_local, head_dim), lambda i: (0, i, 0, 0))
        out_block = pl.BlockSpec((block, seq_local, n, head_dim), lambda i: (i, 0, 0, 0))
        new_block = pl.BlockSpec((n, batch, head_dim), lambda i: (0, 0, 0))
        k_out, v_out = pl.pallas_call(
            functools.partial(relayout_kernel, n),
            name="relayout",
            grid=(batch // block,),
            out_shape=[moved, moved],
            in_specs=[smem_spec, in_block, in_block, new_block, new_block],
            out_specs=[out_block, out_block],
            scratch_shapes=[
                pltpu.VMEM((2, seq_local * n, head_dim), jnp.float32),
                pltpu.VMEM((batch * n, head_dim), jnp.float32),
                pltpu.VMEM((batch * n, head_dim), jnp.float32),
            ],
        )(lens, kx, vx, knx, vnx)
        return attn_out, k_out, v_out

    head_spec = P("dp", "tp")
    entry_spec = P("dp", None, "tp")
    return jax.shard_map(local_step, mesh=mesh, in_specs=(head_spec, entry_spec, entry_spec, head_spec, head_spec, P("dp")), out_specs=(head_spec, P("dp", "tp"), P("dp", "tp")), check_vma=False)
```

time: 586 us -> 414 us (0.71)
  blocking collectives: 413 us -> 0 us
  Pallas kernels: 0 us -> 410 us
  other arithmetic: 74.4 us -> 0 us
  local copies, waits for them, and re-layouts: 59.8 us -> 0.63 us
  matrix products: 14.3 us -> 0 us
  between operations: 14.2 us -> 0.65 us
  starting transfers between devices: 6.82 us -> 0 us
    pallas_call x0 -> x2, Pallas kernels: none -> 410 us  [the longest x1 371 us: local_step(): pl.pallas_call(functools.partial(exchange_kernel, n), name='exchange_atte...]
    all_gather x1 -> x0, blocking collectives: 195 us -> none  [local_step(): q_all = lax.all_gather(query, 'tp', axis=1, tiled=True)]
    all_to_all x1 -> x0, blocking collectives: 189 us -> none  [local_step(): k_seq = lax.all_to_all(k_upd, 'tp', 1, 2, tiled=True)]
    select_n x1 -> x0, other arithmetic: 68.6 us -> none  [local_step(): v_upd = jnp.where(new_slot, v_new[:, None], v_cache)]
    unnamed x10 -> x3, local copies, waits for them, and re-layouts: 37.8 us -> 0.63 us
    pmax x1 -> x0, blocking collectives: 27.9 us -> none  [local_step(): glob_max = lax.pmax(part_max, 'tp')]
    all_to_all x2 -> x0, local copies, waits for them, and re-layouts: 19.4 us -> none  [the longest x1 9.76 us: local_step(): v_seq = lax.all_to_all(v_upd, 'tp', 1, 2, tiled=True)]
    dot_general x2 -> x0, matrix products: 14.3 us -> none  [the longest x1 9.76 us: local_step(): jnp.einsum('bhgd,bthd->bhgt', q_grp, k_seq, preferred_element_type=jnp.fl...]
  transfers between devices with their start and end apart: 2 -> 0, of which waited for: 0 -> 0; matrix products, arithmetic and copies ran while one was open for 10% -> 0% of each run, Pallas kernels for 0% -> 0%
where the time goes in v1:
time: 414 us; the launch traced here: 411 us
  Pallas kernels  410 us (99%)
    pallas_call x1, Pallas kernels, local_step(): pl.pallas_call(functools.partial(exchange_kernel, n), name='exchange_atte...  371 us
    pallas_call x1, Pallas kernels, local_step(): pl.pallas_call(functools.partial(relayout_kernel, n), name='relayout', gr...  38.5 us

profile of v1, /device:TPU:113, one launch (start us, length us, event | category | flops | bytes accessed | tf_op | source)
XLA Modules:
  0.0 411.3 jit_solution(4086281341150038105)
XLA Ops:
  0.6 371.5 %exchange_attend.1 = (bf16[64,4,128]{2,1,0:T(4,128)(2,1)}, bf16[8,64,128,128]{3,2,1,0:T(8,128)(2,1)}, bf16[8,64,128,128]{3,2,1,0:T(8,128)(2,1)}, bf16[8,64,128]{2,1,0:T(8,128)(2,1)}, bf16[8,64,128]{2,1,0:T(8,128)(2,1)}) custom-call(bf16[64,4,128]{2,1,0:T(4,128)(2,1)} %q_ref.1, bf16[64,1024,128]{2,1,0:T(8,128)(2,1)} %bitcast.4, ...), custom_call_target="tpu_custom_call" | custom-call | tf_op jit(solution)/shard_map/exchange_attend/pallas_call | solution.py:155
  372.1 0.0 copy-start
  372.1 38.5 %relayout.1 = (bf16[64,128,8,128]{3,2,1,0:T(8,128)(2,1)}, bf16[64,128,8,128]{3,2,1,0:T(8,128)(2,1)}) custom-call(s32[64]{0:T(128)} %lens_ref.3, bf16[8,64,128,128]{3,2,1,0:T(8,128)(2,1)} %get-tuple-element.11.kx_ref, bf16[8,64,128,128]{3,2,1,0:T(8,128)(2,1)} %get-tuple-element.12.vx_ref, bf16[8,64,128]{2,1,0:T(8,128)(2,1)} %get-tuple-element.13.knx_ref, ...), custom_call_target="tpu_custom_call" | custom-call | tf_op jit(solution)/shard_map/relayout/pallas_call | solution.py:181
  410.7 0.0 copy-done
  410.7 0.6 copy.10
Async XLA Ops:
  372.1 38.5 %copy-start = (bf16[64,4,128]{2,1,0:T(4,128)(2,1)S(1)}, bf16[64,4,128]{2,1,0:T(4,128)(2,1)}, u32[]{:S(2)}) copy-start(bf16[64,4,128]{2,1,0:T(4,128)(2,1)} %get-tuple-element.20) | copy-start | bytes 196612

commit v2 on v1

v2 whole, which is shorter than its diff:
```python
import functools

import jax
import jax.numpy as jnp
from jax import lax
from jax.experimental import pallas as pl
from jax.experimental.pallas import tpu as pltpu
from jax.sharding import PartitionSpec as P

MESH = pl.DeviceIdType.MESH
MASK_VALUE = -1e30
TAIL = 8


def exchange_kernel(n, q_hbm, k_ref, v_ref, kn_hbm, vn_hbm, lens_ref,
                    out_hbm, kx_ref, vx_ref, knx_ref, vnx_ref, vt_ref,
                    kbuf, vbuf, q_ref, out_ref, kn_ref, vn_ref, kn32, vn32,
                    send_sem, recv_sem, small_send, small_recv, load_sem, keep_sem, tail_sem, once_sem):
    dp, me = lax.axis_index("dp"), lax.axis_index("tp")
    batch, seq_len, head_dim = k_ref.shape
    seq_local = seq_len // n
    head_part = vx_ref.shape[1]
    chips = n // 2
    chip = me // 2
    core = me - 2 * chip

    def at(hops, other):
        return 2 * lax.rem(chip + hops, chips) + (1 - core if other else core)

    sibling = at(0, True)
    far = chips // 2
    near = [h for h in range(1, chips) if h != far]
    targets = [at(far, False), at(far, True)] + [at(h, False) for h in near] + [at(h, True) for h in near] + [sibling]

    barrier = pltpu.get_barrier_semaphore()
    for step in range(1, n):
        pl.semaphore_signal(barrier, inc=1, device_id=(dp, lax.rem(me + step, n)), device_id_type=MESH)
    pl.semaphore_wait(barrier, n - 1)

    def rows(peer):
        return pl.ds(pl.multiple_of(peer * seq_local, seq_local), seq_local)

    def remote(src, dst, send, recv, peer):
        return pltpu.make_async_remote_copy(src_ref=src, dst_ref=dst, send_sem=send, recv_sem=recv,
                                            device_id=(dp, peer), device_id_type=MESH)

    copies = []
    for a, (src, dst) in enumerate(((kn_hbm, knx_ref), (vn_hbm, vnx_ref))):
        for h in range(1, chips):
            copies.append(remote(src, dst.at[me], small_send.at[a, h], small_recv.at[a, h], at(h, False)))
        copies.append(remote(src, dst.at[me], small_send.at[a, 0], small_recv.at[a, 0], sibling))
    for a, (src, dst) in enumerate(((k_ref, kx_ref), (v_ref, vx_ref))):
        for slot, peer in enumerate(targets):
            copies.append(remote(src.at[pl.ds(0, dst.shape[1]), rows(peer)], dst.at[me],
                                 send_sem.at[a, slot], recv_sem.at[a, slot], peer))
    for copy in copies:
        copy.start()

    def load(a, b, slot):
        src, dst = ((k_ref, kbuf), (v_ref, vbuf))[a]
        return pltpu.make_async_copy(src.at[b], dst.at[slot], load_sem.at[a, slot])

    first = [pltpu.make_async_copy(kn_hbm, kn_ref, once_sem.at[0]),
             pltpu.make_async_copy(vn_hbm, vn_ref, once_sem.at[1]),
             pltpu.make_async_copy(q_hbm, q_ref, once_sem.at[2])]
    for copy in first:
        copy.start()
    for a in range(2):
        load(a, 0, 0).start()
    for copy in first:
        copy.wait()
    own_new = [pltpu.make_async_copy(kn_ref, knx_ref.at[me], once_sem.at[0]),
               pltpu.make_async_copy(vn_ref, vnx_ref.at[me], once_sem.at[1])]
    tail = [pltpu.make_async_copy(v_ref.at[pl.ds(head_part, batch - head_part), pl.ds(p * seq_local, seq_local)],
                                  vt_ref.at[p], tail_sem.at[p]) for p in range(n)]
    for copy in own_new + tail:
        copy.start()
    kn32[...] = kn_ref[...].astype(jnp.float32)
    vn32[...] = vn_ref[...].astype(jnp.float32)

    def keep(b, slot, act):
        act(pltpu.make_async_copy(kbuf.at[slot, rows(me)], kx_ref.at[me, b], keep_sem.at[0, slot]))

        @pl.when(b < head_part)
        def _():
            act(pltpu.make_async_copy(vbuf.at[slot, rows(me)], vx_ref.at[me, b], keep_sem.at[1, slot]))

    scale = head_dim ** -0.5
    positions = lax.broadcasted_iota(jnp.int32, (1, seq_len), 1)

    def attend(b, carry):
        slot = lax.rem(b, 2)
        for a in range(2):
            load(a, b, slot).wait()
        keep(b, slot, lambda copy: copy.start())

        @pl.when(b > 0)
        def _():
            keep(b - 1, 1 - slot, lambda copy: copy.wait())

        @pl.when(b + 1 < batch)
        def _():
            for a in range(2):
                load(a, b + 1, 1 - slot).start()

        length = lens_ref[b]
        query = q_ref[b]
        new_k, new_v = kn32[pl.ds(b, 1), :], vn32[pl.ds(b, 1), :]
        scores = lax.dot_general(query, kbuf[slot], (((1,), (1,)), ((), ())), preferred_element_type=jnp.float32)
        new_score = jnp.sum(query.astype(jnp.float32) * new_k, axis=-1, keepdims=True)
        is_new = positions == length
        scores = jnp.where(is_new, new_score, scores) * scale
        scores = jnp.where(positions <= length, scores, MASK_VALUE)
        weights = jnp.exp(scores - jnp.max(scores, axis=-1, keepdims=True))
        weights = weights / jnp.sum(weights, axis=-1, keepdims=True)
        probs = weights.astype(jnp.bfloat16)
        old = jnp.where(is_new, 0.0, weights).astype(jnp.bfloat16)
        summed = jnp.dot(old, vbuf[slot], preferred_element_type=jnp.float32)
        new_prob = jnp.sum(jnp.where(is_new, probs.astype(jnp.float32), 0.0), axis=-1, keepdims=True)
        out_ref[b] = (summed + new_prob * new_v).astype(jnp.bfloat16)
        return carry

    lax.fori_loop(0, batch, attend, 0)
    keep(batch - 1, (batch - 1) % 2, lambda copy: copy.wait())
    for copy in own_new + tail:
        copy.wait()
    done = pltpu.make_async_copy(out_ref, out_hbm, once_sem.at[2])
    done.start()

    passed = []
    for a, dst in enumerate((knx_ref, vnx_ref)):
        for h in range(1, chips):
            origin = at(chips - h, False)
            remote(dst.at[me], dst.at[me], small_send.at[a, h], small_recv.at[a, h], at(h, False)).wait_recv()
            passed.append(remote(dst.at[origin], dst.at[origin], small_send.at[a, chips + h], small_recv.at[a, chips + h], sibling))
            passed[-1].start()
    for i, copy in enumerate(copies):
        copy.wait_send()
        if not any(i in range(a * chips, a * chips + chips - 1) for a in range(2)):
            copy.wait_recv()
    for copy in passed:
        copy.wait()
    done.wait()


def new_rows(n, new_ref, new32):
    for h in range(n):
        new32[pl.ds(h, new_ref.shape[1], stride=n), :] = new_ref[h].astype(jnp.float32)


def place(n, x_ref, i, o_ref, j, row, b, new32):
    o_ref[j] = jnp.swapaxes(x_ref[:, i], 0, 1)

    @pl.when((row >= 0) & (row < o_ref.shape[1]))
    def _():
        o_ref[j, row] = new32[pl.ds(pl.multiple_of(b * n, n), n), :].astype(o_ref.dtype)


def relayout_kernel(n, lens_ref, out_in, kx_ref, vx_ref, knx_ref, vnx_ref, out_ref, ko_ref, vo_ref, kn32, vn32):
    step = pl.program_id(0)
    base = lax.axis_index("tp") * ko_ref.shape[1]

    @pl.when(step == 0)
    def _():
        out_ref[...] = out_in[...]
        new_rows(n, knx_ref, kn32)
        new_rows(n, vnx_ref, vn32)

    for x_ref, o_ref, new32 in ((kx_ref, ko_ref, kn32), (vx_ref, vo_ref, vn32)):
        block = o_ref.shape[0]
        for i in range(block):
            b = step * block + i
            place(n, x_ref, i, o_ref, i, lens_ref[b] - base, b, new32)


def tail_kernel(n, first, lens_ref, x_ref, new_ref, whole_ref, o_ref, new32):
    step = pl.program_id(0)
    block = o_ref.shape[0]
    base = lax.axis_index("tp") * o_ref.shape[1]

    @pl.when(step == 0)
    def _():
        new_rows(n, new_ref, new32)

    for i in range(block):
        b = first + step * block + i
        place(n, x_ref, step * block + i, o_ref, i, lens_ref[b] - base, b, new32)


def solution(mesh):
    n = mesh.shape["tp"]

    def local_step(query, k_cache, v_cache, k_new, v_new, lens):
        batch, seq_len, _, head_dim = k_cache.shape
        seq_local = seq_len // n
        k_cache = k_cache.reshape(batch, seq_len, head_dim)
        v_cache = v_cache.reshape(batch, seq_len, head_dim)
        k_new = k_new.reshape(batch, head_dim)
        v_new = v_new.reshape(batch, head_dim)
        dtype = k_cache.dtype
        any_spec = pl.BlockSpec(memory_space=pl.ANY)
        vmem_spec = pl.BlockSpec(memory_space=pltpu.VMEM)
        smem_spec = pl.BlockSpec(memory_space=pltpu.SMEM)
        held = lambda count: jax.ShapeDtypeStruct((n, count, seq_local, head_dim), dtype)
        held_new = jax.ShapeDtypeStruct((n, batch, head_dim), dtype)
        head_shape = jax.ShapeDtypeStruct(query.shape, dtype)
        dma = lambda *shape: pltpu.SemaphoreType.DMA(shape)
        attn, kx, vx, knx, vnx, vt = pl.pallas_call(
            functools.partial(exchange_kernel, n),
            name="exchange_attend",
            out_shape=[head_shape, held(batch), held(batch - TAIL), held_new, held_new, held(TAIL)],
            in_specs=[any_spec] * 5 + [smem_spec],
            out_specs=[any_spec] * 6,
            scratch_shapes=[
                pltpu.VMEM((2, seq_len, head_dim), dtype),
                pltpu.VMEM((2, seq_len, head_dim), dtype),
                pltpu.VMEM(query.shape, dtype),
                pltpu.VMEM(query.shape, dtype),
                pltpu.VMEM((batch, head_dim), dtype),
                pltpu.VMEM((batch, head_dim), dtype),
                pltpu.VMEM((batch, head_dim), jnp.float32),
                pltpu.VMEM((batch, head_dim), jnp.float32),
                dma(2, n - 1), dma(2, n - 1), dma(2, n), dma(2, n), dma(2, 2), dma(2, 2), dma(n), dma(3),
            ],
            compiler_params=pltpu.CompilerParams(collective_id=0, has_side_effects=True),
        )(query, k_cache, v_cache, k_new, v_new, lens)

        vr = lax.all_to_all(vt, "tp", 0, 0, tiled=True)

        whole = jax.ShapeDtypeStruct((batch, seq_local, n, head_dim), dtype)
        new_wide = pltpu.VMEM((batch * n, head_dim), jnp.float32)
        steps = 8
        in_block = lambda count: pl.BlockSpec((n, count // steps, seq_local, head_dim), lambda i: (0, i, 0, 0))
        out_block = lambda count: pl.BlockSpec((count // steps, seq_local, n, head_dim), lambda i: (i, 0, 0, 0))
        attn, k_out, v_out = pl.pallas_call(
            functools.partial(relayout_kernel, n),
            name="relayout",
            grid=(steps,),
            out_shape=[head_shape, whole, whole],
            in_specs=[smem_spec, vmem_spec, in_block(batch), in_block(batch - TAIL), vmem_spec, vmem_spec],
            out_specs=[vmem_spec, out_block(batch), out_block(batch - TAIL)],
            scratch_shapes=[new_wide, new_wide],
            cost_estimate=pl.CostEstimate(flops=10**10, bytes_accessed=4 * kx.size + 4 * vx.size, transcendentals=0),
        )(lens, attn, kx, vx, knx, vnx)

        block = 2
        first = batch - TAIL
        v_out = pl.pallas_call(
            functools.partial(tail_kernel, n, first),
            name="relayout_tail",
            grid=(TAIL // block,),
            out_shape=whole,
            in_specs=[smem_spec, vmem_spec, vmem_spec, any_spec],
            out_specs=pl.BlockSpec((block, seq_local, n, head_dim), lambda i: (first // block + i, 0, 0, 0)),
            scratch_shapes=[new_wide],
            input_output_aliases={3: 0},
            compiler_params=pltpu.CompilerParams(vmem_limit_bytes=8 * 2**20),
        )(lens, vr, vnx, v_out)
        return attn, k_out, v_out

    head_spec = P("dp", "tp")
    entry_spec = P("dp", None, "tp")
    return jax.shard_map(local_step, mesh=mesh, in_specs=(head_spec, entry_spec, entry_spec, head_spec, head_spec, P("dp")), out_specs=(head_spec, P("dp", "tp"), P("dp", "tp")), check_vma=False)
```

time: 414 us -> 382 us (0.923)
  Pallas kernels: 410 us -> 376 us
    pallas_call x1, Pallas kernels: 371 us -> 346 us  [local_step(): pl.pallas_call(functools.partial(exchange_kernel, n), name='exchange_atte...]
    pallas_call x1, Pallas kernels: 38.5 us -> 26.6 us  [local_step(): pl.pallas_call(functools.partial(relayout_kernel, n), name='relayout', gr...]
  transfers between devices with their start and end apart: 0 -> 1, of which waited for: 0 -> 0; matrix products, arithmetic and copies ran while one was open for 0% -> 0% of each run, Pallas kernels for 0% -> 7%
where the time goes in v2:
time: 382 us; the launch traced here: 380 us
  Pallas kernels  376 us (98%)
    pallas_call x1, Pallas kernels, local_step(): pl.pallas_call(functools.partial(exchange_kernel, n), name='exchange_atte...  346 us
    pallas_call x1, Pallas kernels, local_step(): pl.pallas_call(functools.partial(relayout_kernel, n), name='relayout', gr...  26.6 us
  transfers between devices with their start and end apart: 1, of which 0 were waited for; matrix products, arithmetic and copies ran while one was open for 0% of the time, Pallas kernels for 7%

profile of v2, /device:TPU:113, one launch (start us, length us, event | category | flops | bytes accessed | tf_op | source)
XLA Modules:
  0.0 380.2 jit_solution(7011523682912265555)
XLA Ops:
  0.6 346.4 %exchange_attend.1 = (bf16[64,4,128]{2,1,0:T(4,128)(2,1)}, bf16[8,64,128,128]{3,2,1,0:T(8,128)(2,1)}, bf16[8,56,128,128]{3,2,1,0:T(8,128)(2,1)}, bf16[8,64,128]{...) custom-call(bf16[64,4,128]{2,1,0:T(4,128)(2,1)} %q_hbm.1, ...), custom_call_target="tpu_custom_call" | custom-call | tf_op jit(solution)/shard_map/exchange_attend/pallas_call | solution.py:208
  347.0 3.7 all-to-all-start
  350.7 0.0 copy-start
  350.7 0.0 copy-start.1
  350.7 26.6 %relayout.1 = (bf16[64,4,128]{2,1,0:T(4,128)(2,1)}, bf16[64,128,8,128]{3,2,1,0:T(8,128)(2,1)}, bf16[64,128,8,128]{3,2,1,0:T(8,128)(2,1)}) custom-call(s32[64]{0:T(128)} %lens_ref.5, bf16[64,4,128]{2,1,0:T(4,128)(2,1)} %get-tuple-element.12.out_in, bf16[8,64,128,128]{3,2,1,0:T(8,128)(2,1)} %get-tuple-element.13.kx_ref, ...), custom_call_target="tpu_custom_call" | custom-call | flops 10000000000 | bytes 62914560 | tf_op jit(solution)/shard_map/relayout/pallas_call | solution.py:235
  377.4 0.0 all-to-all-done.x_ref
  377.4 0.0 copy-done
  377.4 0.0 copy-done.1
  377.4 2.8 relayout_tail.1
Async XLA Ops:
  347.0 30.4 %all-to-all-start = ((bf16[8,8,128,128]{3,2,1,0:T(8,128)(2,1)}), bf16[8,8,128,128]{3,2,1,0:T(8,128)(2,1)S(1)}, u32[]{:S(2)}, u32[]{:S(2)}) async-start(bf16[8,8,128,128]{3,2,1,0:T(8,128)(2,1)} %get-tuple-element.19), calls=%async_computation | async-start | bytes 4194304 | tf_op jit(solution)/shard_map/all_to_all | solution.py:228
  350.7 26.7 %copy-start = (bf16[8,64,128]{2,1,0:T(8,128)(2,1)S(1)}, bf16[8,64,128]{2,1,0:T(8,128)(2,1)}, u32[]{:S(2)}) copy-start(bf16[8,64,128]{2,1,0:T(8,128)(2,1)} %get-tuple-element.16.vnx_ref.new_ref) | copy-start | bytes 393220
  350.7 26.7 %copy-start.1 = (s32[64]{0:T(128)S(1)}, s32[64]{0:T(128)}, u32[]{:S(2)}) copy-start(s32[64]{0:T(128)} %lens_ref.5) | copy-start | bytes 772

commit v3 on v0

v3 whole, which is shorter than its diff:
```python
import functools

import jax
import jax.numpy as jnp
from jax import lax
from jax.experimental import pallas as pl
from jax.experimental.pallas import tpu as pltpu
from jax.sharding import PartitionSpec as P


MASK_VALUE = -1e30
CHUNKS = ((0, 0, 16, 8), (0, 16, 48, 8), (1, 0, 40, 8), (1, 40, 16, 8), (1, 56, 6, 2), (1, 62, 2, 1))


def offsets(n):
    chips = n // 2
    far = chips // 2
    near = [h for h in range(1, chips) if h != far]
    return [(far, False), (far, True)] + [(h, False) for h in near] + [(h, True) for h in near] + [(0, True)]


def pairs(n, hops, other):
    return [(2 * c + k, 2 * ((c + hops) % (n // 2)) + ((1 - k) if other else k)) for c in range(n // 2) for k in range(2)]


def at(n, me, hops, other):
    chip = me // 2
    core = me - 2 * chip
    return 2 * lax.rem(chip + hops, n // 2) + (1 - core if other else core)


def pack_kernel(n, peers, first, pieces, lens_ref, src_ref, new_ref, *refs):
    outs, (buf, new_buf, new32, in_sem, out_sem, new_sem) = refs[:len(peers)], refs[len(peers):]
    count, seq_local = outs[0].shape[0], outs[0].shape[1]
    size = count // pieces
    me = lax.axis_index("tp")
    new_copy = pltpu.make_async_copy(new_ref, new_buf, new_sem)
    new_copy.start()
    slots = buf.shape[0]
    work = [(o, c) for o in range(len(peers)) for c in range(pieces)]

    def base(o):
        return pl.multiple_of(at(n, me, *peers[o]) * seq_local, seq_local)

    def load(w):
        o, c = work[w]
        return pltpu.make_async_copy(src_ref.at[pl.ds(first + c * size, size), pl.ds(base(o), seq_local)],
                                     buf.at[w % slots, pl.ds(0, size)], in_sem.at[w % slots])

    def store(w):
        o, c = work[w]
        return pltpu.make_async_copy(buf.at[w % slots, pl.ds(0, size)], outs[o].at[pl.ds(c * size, size)], out_sem.at[w % slots])

    ahead = slots // 2
    for w in range(min(ahead, len(work))):
        load(w).start()
    new_copy.wait()
    new32[...] = new_buf[...].astype(jnp.float32)
    positions = lax.broadcasted_iota(jnp.int32, (seq_local, 1), 0)
    for w, (o, c) in enumerate(work):
        if w + ahead < len(work):
            if w + ahead >= slots:
                store(w + ahead - slots).wait()
            load(w + ahead).start()
        load(w).wait()
        start = base(o)

        def patch(i, carry):
            b = first + c * size + i
            row = lens_ref[b] - start

            @pl.when((row >= 0) & (row < seq_local))
            def _():
                old = buf[w % slots, i]
                buf[w % slots, i] = jnp.where(positions == row, new32[pl.ds(b, 1), :], old.astype(jnp.float32)).astype(old.dtype)

            return carry

        lax.fori_loop(0, size, patch, 0, unroll=min(size, 8))
        store(w).start()
    for w in range(max(0, len(work) - slots), len(work)):
        store(w).wait()


def pack_first_kernel(n, peer, lens_ref, src_ref, new_ref, out_ref, lens_buf, new_buf, new32, sem):
    count, seq_local = out_ref.shape[0], out_ref.shape[1]
    start = pl.multiple_of(at(n, lax.axis_index("tp"), *peer) * seq_local, seq_local)
    data = pltpu.make_async_copy(src_ref.at[pl.ds(0, count), pl.ds(start, seq_local)], out_ref, sem.at[0])
    lengths = pltpu.make_async_copy(lens_ref, lens_buf, sem.at[1])
    new = pltpu.make_async_copy(new_ref, new_buf, sem.at[2])
    for copy in (lengths, new, data):
        copy.start()
    new.wait()
    new32[...] = new_buf[...].astype(jnp.float32)
    lengths.wait()
    data.wait()
    positions = lax.broadcasted_iota(jnp.int32, (seq_local, 1), 0)
    for b in range(count):
        row = lens_buf[b] - start

        @pl.when((row >= 0) & (row < seq_local))
        def _():
            old = out_ref[b]
            out_ref[b] = jnp.where(positions == row, new32[b:b + 1, :], old.astype(jnp.float32)).astype(old.dtype)


def pack_first(n, lens, src, new, peer, count):
    _, seq_len, head_dim = src.shape
    any_spec = pl.BlockSpec(memory_space=pl.ANY)
    return pl.pallas_call(
        functools.partial(pack_first_kernel, n, peer),
        name="pack_first",
        out_shape=pltpu.VMEM((count, seq_len // n, head_dim), src.dtype),
        in_specs=[any_spec] * 3,
        out_specs=pl.BlockSpec(memory_space=pltpu.VMEM),
        scratch_shapes=[pltpu.SMEM(lens.shape, lens.dtype), pltpu.VMEM(new.shape, new.dtype),
                        pltpu.VMEM(new.shape, jnp.float32), pltpu.SemaphoreType.DMA((3,))],
        cost_estimate=pl.CostEstimate(flops=count * 4_000_000, bytes_accessed=4 * count * seq_len // n * head_dim, transcendentals=0),
    )(lens, src, new)


def pack(n, lens, src, new, peers, first, count, pieces, slots):
    _, seq_len, head_dim = src.shape
    seq_local = seq_len // n
    any_spec = pl.BlockSpec(memory_space=pl.ANY)
    size = count // pieces
    return pl.pallas_call(
        functools.partial(pack_kernel, n, peers, first, pieces),
        out_shape=[jax.ShapeDtypeStruct((count, seq_local, head_dim), src.dtype)] * len(peers),
        in_specs=[pl.BlockSpec(memory_space=pltpu.SMEM), any_spec, any_spec],
        out_specs=[any_spec] * len(peers),
        scratch_shapes=[pltpu.VMEM((slots, size, seq_local, head_dim), src.dtype), pltpu.VMEM(new.shape, new.dtype),
                        pltpu.VMEM(new.shape, jnp.float32), pltpu.SemaphoreType.DMA((slots,)), pltpu.SemaphoreType.DMA((slots,)), pltpu.SemaphoreType.DMA],
        cost_estimate=pl.CostEstimate(flops=len(peers) * count * 4_000_000, bytes_accessed=4 * len(peers) * count * seq_local * head_dim, transcendentals=0),
    )(lens, src, new)


def attend_kernel(lens_ref, q_ref, k_ref, v_ref, kn_ref, vn_ref, out_ref, kn32, vn32):
    step = pl.program_id(0)
    block, seq_len, head_dim = k_ref.shape

    @pl.when(step == 0)
    def _():
        kn32[...] = kn_ref[...].astype(jnp.float32)
        vn32[...] = vn_ref[...].astype(jnp.float32)

    scale = head_dim ** -0.5
    positions = lax.broadcasted_iota(jnp.int32, (1, seq_len), 1)
    for i in range(block):
        b = step * block + i
        length = lens_ref[b]
        query = q_ref[i]
        new_k, new_v = kn32[pl.ds(b, 1), :], vn32[pl.ds(b, 1), :]
        scores = lax.dot_general(query, k_ref[i], (((1,), (1,)), ((), ())), preferred_element_type=jnp.float32)
        new_score = jnp.sum(query.astype(jnp.float32) * new_k, axis=-1, keepdims=True)
        is_new = positions == length
        scores = jnp.where(is_new, new_score, scores) * scale
        scores = jnp.where(positions <= length, scores, MASK_VALUE)
        weights = jnp.exp(scores - jnp.max(scores, axis=-1, keepdims=True))
        weights = weights / jnp.sum(weights, axis=-1, keepdims=True)
        probs = weights.astype(jnp.bfloat16)
        old = jnp.where(is_new, 0.0, weights).astype(jnp.bfloat16)
        summed = jnp.dot(old, v_ref[i], preferred_element_type=jnp.float32)
        new_prob = jnp.sum(jnp.where(is_new, probs.astype(jnp.float32), 0.0), axis=-1, keepdims=True)
        out_ref[i] = (summed + new_prob * new_v).astype(jnp.bfloat16)


def relayout_kernel(n, sources, *refs):
    xs, (o_ref, held) = refs[:n], refs[-2:]
    me = lax.axis_index("tp")
    block = o_ref.shape[0]
    for i in range(block):
        for x_ref, source in zip(xs, sources):
            row = i if x_ref.shape[0] == block else pl.program_id(0) * block + i
            held[i % 2, at(n, me, *source)] = x_ref[row]
        o_ref[i] = jnp.swapaxes(held[i % 2], 0, 1)


def relayout(n, sources, xs, whole, first, batch, block, resident=False):
    count, seq_local, head_dim = xs[0].shape
    return pl.pallas_call(
        functools.partial(relayout_kernel, n, sources),
        grid=(count // block,),
        out_shape=jax.ShapeDtypeStruct((batch, seq_local, n, head_dim), xs[0].dtype),
        in_specs=[pl.BlockSpec(memory_space=pltpu.VMEM) if resident else pl.BlockSpec((block, seq_local, head_dim), lambda i: (i, 0, 0))] * n
        + ([] if whole is None else [pl.BlockSpec(memory_space=pl.ANY)]),
        out_specs=pl.BlockSpec((block, seq_local, n, head_dim), lambda i: (first // block + i, 0, 0, 0)),
        scratch_shapes=[pltpu.VMEM((2, n, seq_local, head_dim), xs[0].dtype)],
        input_output_aliases={} if whole is None else {n: 0},
        compiler_params=pltpu.CompilerParams(vmem_limit_bytes=8 * 2**20) if resident else None,
        cost_estimate=pl.CostEstimate(flops=count * 40_000_000, bytes_accessed=4 * n * xs[0].size, transcendentals=0),
    )(*xs, *([] if whole is None else [whole]))


def solution(mesh):
    n = mesh.shape["tp"]
    peers = offsets(n)
    sources = [((n // 2 - h) % (n // 2), o) for h, o in peers] + [(0, False)]

    def local_step(query, k_cache, v_cache, k_new, v_new, lens):
        batch, seq_len, _, head_dim = k_cache.shape
        k_cache = k_cache.reshape(batch, seq_len, head_dim)
        v_cache = v_cache.reshape(batch, seq_len, head_dim)
        k_new = k_new.reshape(batch, head_dim)
        v_new = v_new.reshape(batch, head_dim)

        caches, news = (k_cache, v_cache), (k_new, v_new)
        own = [(0, False)]
        got = []
        for c, (a, first, count, _) in enumerate(CHUNKS):
            slabs = []
            if c == 0:
                slabs.append(pack_first(n, lens, caches[a], news[a], peers[0], count))
            pieces = 2 if count > 32 else 1
            slabs += pack(n, lens, caches[a], news[a], peers[len(slabs):] + own, first, count, pieces, 4)
            for i, peer in enumerate(peers):
                slabs[i] = lax.ppermute(slabs[i], "tp", pairs(n, *peer))
            got.append(slabs)

        block = 4
        cache_block = pl.BlockSpec((block, seq_len, head_dim), lambda i: (i, 0, 0))
        head_block = pl.BlockSpec((block,) + query.shape[1:], lambda i: (i, 0, 0))
        vmem_spec = pl.BlockSpec(memory_space=pltpu.VMEM)
        attend = pl.pallas_call(
            attend_kernel,
            name="attend",
            grid=(batch // block,),
            out_shape=jax.ShapeDtypeStruct(query.shape, query.dtype),
            in_specs=[pl.BlockSpec(memory_space=pltpu.SMEM), head_block, cache_block, cache_block, vmem_spec, vmem_spec],
            out_specs=head_block,
            scratch_shapes=[pltpu.VMEM((batch, head_dim), jnp.float32)] * 2,
            cost_estimate=pl.CostEstimate(flops=10**11, bytes_accessed=4 * k_cache.size, transcendentals=0),
        )
        attn = attend(lens, query, k_cache, v_cache, k_new, v_new)

        moved = [None, None]
        for c, (a, first, count, size) in enumerate(CHUNKS):
            moved[a] = relayout(n, sources, got[c], moved[a], first, batch, size, resident=c + 1 == len(CHUNKS))
        return attn, *moved


    head_spec = P("dp", "tp")
    entry_spec = P("dp", None, "tp")
    return jax.shard_map(local_step, mesh=mesh, in_specs=(head_spec, entry_spec, entry_spec, head_spec, head_spec, P("dp")), out_specs=(head_spec, P("dp", "tp"), P("dp", "tp")), check_vma=False)
```

time: 586 us -> 436 us (0.74)
  blocking collectives: 413 us -> 0 us
  waiting for transfers between devices: 0.06 us -> 254 us
  Pallas kernels: 0 us -> 117 us
  other arithmetic: 74.4 us -> 0 us
  local copies, waits for them, and re-layouts: 59.8 us -> 5.43 us
  starting transfers between devices: 6.82 us -> 57.1 us
  matrix products: 14.3 us -> 0 us
  between operations: 14.2 us -> 1.09 us
    ppermute x0 -> x42, waiting for transfers between devices: none -> 254 us  [local_step(): slabs[i] = lax.ppermute(slabs[i], 'tp', pairs(n, *peer))]
    all_gather x1 -> x0, blocking collectives: 195 us -> none  [local_step(): q_all = lax.all_gather(query, 'tp', axis=1, tiled=True)]
    all_to_all x1 -> x0, blocking collectives: 189 us -> none  [local_step(): k_seq = lax.all_to_all(k_upd, 'tp', 1, 2, tiled=True)]
    pallas_call x0 -> x14, Pallas kernels: none -> 117 us  [the longest x6 46.8 us: pack(): pl.pallas_call(functools.partial(pack_kernel, n, peers, first, pieces), o...]
    select_n x1 -> x0, other arithmetic: 68.6 us -> none  [local_step(): v_upd = jnp.where(new_slot, v_new[:, None], v_cache)]
    ppermute x0 -> x42, starting transfers between devices: none -> 57.1 us  [local_step(): slabs[i] = lax.ppermute(slabs[i], 'tp', pairs(n, *peer))]
    unnamed x10 -> x78, local copies, waits for them, and re-layouts: 37.8 us -> 5.43 us
    pmax x1 -> x0, blocking collectives: 27.9 us -> none  [local_step(): glob_max = lax.pmax(part_max, 'tp')]
  transfers between devices with their start and end apart: 2 -> 42, of which waited for: 0 -> 11; matrix products, arithmetic and copies ran while one was open for 10% -> 0% of each run, Pallas kernels for 0% -> 23%
where the time goes in v3:
time: 436 us; the launch traced here: 434 us
  waiting for transfers between devices  254 us (58%)
  Pallas kernels  117 us (27%)
  starting transfers between devices  57.1 us (13%)
  local copies, waits for them, and re-layouts  5.43 us (1%)
    ppermute x42, waiting for transfers between devices, local_step(): slabs[i] = lax.ppermute(slabs[i], 'tp', pairs(n, *peer))  254 us
    ppermute x42, starting transfers between devices, local_step(): slabs[i] = lax.ppermute(slabs[i], 'tp', pairs(n, *peer))  57.1 us
    pallas_call x6, Pallas kernels, pack(): pl.pallas_call(functools.partial(pack_kernel, n, peers, first, pieces), o...  46.8 us
    pallas_call x6, Pallas kernels, relayout(): pl.pallas_call(functools.partial(relayout_kernel, n, sources), grid=(coun...  40.1 us
    pallas_call x1, Pallas kernels, local_step(): attn = attend(lens, query, k_cache, v_cache, k_new, v_new)  28.9 us
  transfers between devices with their start and end apart: 42, of which 11 were waited for; matrix products, arithmetic and copies ran while one was open for 0% of the time, Pallas kernels for 23%

profile of v3, /device:TPU:113, one launch (start us, length us, event | category | flops | bytes accessed | tf_op | source)
XLA Modules:
  0.0 434.3 jit_solution(3676197348884254967)
XLA Ops:
  0.6 4.6 %shard_map.89 = (bf16[2,128,128]{2,1,0:T(8,128)(2,1)}, bf16[2,128,128]{2,1,0:T(8,128)(2,1)}, bf16[2,128,128]{2,1,0:T(8,128)(2,1)}, bf16[2,128,128]{2,1,0:T(8,128...) custom-call(s32[64]{0:T(128)} %lens_ref.15, ...), custom_call_target="tpu_custom_call" | custom-call | flops 64000000 | bytes 1048576 | tf_op jit(solution)/shard_map/pallas_call | solution.py:127
  5.3 3.9 collective-permute-start.14
  11.2 5.3 %shard_map.90 = (bf16[6,128,128]{2,1,0:T(8,128)(2,1)}, bf16[6,128,128]{2,1,0:T(8,128)(2,1)}, bf16[6,128,128]{2,1,0:T(8,128)(2,1)}, bf16[6,128,128]{2,1,0:T(8,128...) custom-call(s32[64]{0:T(128)} %lens_ref.15, ...), custom_call_target="tpu_custom_call" | custom-call | flops 192000000 | bytes 3145728 | tf_op jit(solution)/shard_map/pallas_call | solution.py:127
  27.6 5.9 %shard_map.86 = (bf16[16,128,128]{2,1,0:T(8,128)(2,1)}, bf16[16,128,128]{2,1,0:T(8,128)(2,1)}, bf16[16,128,128]{2,1,0:T(8,128)(2,1)}, bf16[16,128,128]{2,1,0:T(8...) custom-call(s32[64]{0:T(128)} %lens_ref.15, ...), custom_call_target="tpu_custom_call" | custom-call | flops 448000000 | bytes 7340032 | tf_op jit(solution)/shard_map/pallas_call | solution.py:127
  41.7 22.7 %collective-permute-done.23.refs_2_ = bf16[6,128,128]{2,1,0:T(8,128)(2,1)S(1)} collective-permute-done((bf16[6,128,128]{2,1,0:T(8,128)(2,1)S(1)}, bf16[6,128,128]{2,1,0:T(8,128)(2,1)S(1)}, u32[]{:S(2)}, u32[]{:S(2)}) %collective-permute-start.23) | collective-permute-done | bytes 196640 | tf_op jit(solution)/shard_map/ppermute | solution.py:217
  65.1 3.4 collective-permute-start.26
  69.1 4.2 collective-permute-done.26.refs_5_
  82.4 6.3 %shard_map.91 = (bf16[16,128,128]{2,1,0:T(8,128)(2,1)}, bf16[16,128,128]{2,1,0:T(8,128)(2,1)}, bf16[16,128,128]{2,1,0:T(8,128)(2,1)}, bf16[16,128,128]{2,1,0:T(8...) custom-call(s32[64]{0:T(128)} %lens_ref.15, ...), custom_call_target="tpu_custom_call" | custom-call | flops 512000000 | bytes 8388608 | tf_op jit(solution)/shard_map/pallas_call | solution.py:127
  92.0 24.2 %collective-permute-done.11.refs_4_ = bf16[16,128,128]{2,1,0:T(8,128)(2,1)S(1)} collective-permute-done((bf16[16,128,128]{2,1,0:T(8,128)(2,1)}, bf16[16,128,128]{2,1,0:T(8,128)(2,1)S(1)}, u32[]{:S(2)}, u32[]{:S(2)}) %collective-permute-start.11) | collective-permute-done | bytes 524320 | tf_op jit(solution)/shard_map/ppermute | solution.py:217
  116.2 5.6 %collective-permute-done.12.refs_5_ = bf16[16,128,128]{2,1,0:T(8,128)(2,1)} collective-permute-done((bf16[16,128,128]{2,1,0:T(8,128)(2,1)}, bf16[16,128,128]{2,1,0:T(8,128)(2,1)}, u32[]{:S(2)}, u32[]{:S(2)}) %collective-permute-start.12) | collective-permute-done | bytes 524320 | tf_op jit(solution)/shard_map/ppermute | solution.py:217
  121.8 4.2 collective-permute-start.31
  126.1 12.0 %shard_map.92 = (bf16[40,128,128]{2,1,0:T(8,128)(2,1)}, bf16[40,128,128]{2,1,0:T(8,128)(2,1)}, bf16[40,128,128]{2,1,0:T(8,128)(2,1)}, bf16[40,128,128]{2,1,0:T(8...) custom-call(s32[64]{0:T(128)} %lens_ref.15, ...), custom_call_target="tpu_custom_call" | custom-call | flops 1280000000 | bytes 20971520 | tf_op jit(solution)/shard_map/pallas_call | solution.py:127
  143.8 55.1 %collective-permute-done.32.refs_4_ = bf16[16,128,128]{2,1,0:T(8,128)(2,1)S(1)} collective-permute-done((bf16[16,128,128]{2,1,0:T(8,128)(2,1)}, bf16[16,128,128]{2,1,0:T(8,128)(2,1)S(1)}, u32[]{:S(2)}, u32[]{:S(2)}) %collective-permute-start.32) | collective-permute-done | bytes 524320 | tf_op jit(solution)/shard_map/ppermute | solution.py:217
  199.0 38.3 %collective-permute-done.33.refs_5_ = bf16[16,128,128]{2,1,0:T(8,128)(2,1)S(1)} collective-permute-done((bf16[16,128,128]{2,1,0:T(8,128)(2,1)}, bf16[16,128,128]{2,1,0:T(8,128)(2,1)S(1)}, u32[]{:S(2)}, u32[]{:S(2)}) %collective-permute-start.33) | collective-permute-done | bytes 524320 | tf_op jit(solution)/shard_map/ppermute | solution.py:217
  237.3 12.6 %shard_map.85 = (bf16[48,128,128]{2,1,0:T(8,128)(2,1)}, bf16[48,128,128]{2,1,0:T(8,128)(2,1)}, bf16[48,128,128]{2,1,0:T(8,128)(2,1)}, bf16[48,128,128]{2,1,0:T(8...) custom-call(s32[64]{0:T(128)} %lens_ref.15, ...), custom_call_target="tpu_custom_call" | custom-call | flops 1536000000 | bytes 25165824 | tf_op jit(solution)/shard_map/pallas_call | solution.py:127
  250.4 3.6 collective-permute-start.1
  257.0 92.8 %collective-permute-done.39.refs_4_ = bf16[40,128,128]{2,1,0:T(8,128)(2,1)S(1)} collective-permute-done((bf16[40,128,128]{2,1,0:T(8,128)(2,1)}, bf16[40,128,128]{2,1,0:T(8,128)(2,1)S(1)}, u32[]{:S(2)}, u32[]{:S(2)}) %collective-permute-start.39) | collective-permute-done | bytes 1310752 | tf_op jit(solution)/shard_map/ppermute | solution.py:217
  356.6 28.9 %attend.1 = bf16[64,4,128]{2,1,0:T(4,128)(2,1)} custom-call(s32[64]{0:T(128)} %lens_ref.15, bf16[64,4,128]{2,1,0:T(4,128)(2,1)} %q_ref.1, bf16[64,1024,128]{2,1,0:T(8,128)(2,1)} %bitcast.12, bf16[64,1024,128]{2,1,0:T(8,128)(2,1)} %bitcast.8, bf16[64,128]{1,0:T(8,128)(2,1)} %bitcast.21, bf16[64,128]{1,0:T(8,128)(2,1)} %bitcast.17), custom_call_target="tpu_custom_call" | custom-call | flops 99999997952 | bytes 33554432 | tf_op jit(solution)/shard_map/attend/pallas_call | solution.py:234
  385.5 5.0 %shard_map.87.refs_8_ = bf16[64,128,8,128]{3,2,1,0:T(8,128)(2,1)} custom-call(bf16[16,128,128]{2,1,0:T(8,128)(2,1)} %copy-done.19, bf16[16,128,128]{2,1,0:T(8,128)(2,1)} %collective-permute-done.8.refs_1_, bf16[16,128,128]{2,1,0:T(8,128)(2,1)} %copy-done.20, bf16[16,128,128]{2,1,0:T(8,128)(2,1)} %copy-done.21, bf16[16,128,128]{2,1,0:T(8,128)(2,1)} %copy-done.22, ...), custom_call_target="tpu_custom_call" | custom-call | flops 640000000 | bytes 8388608 | tf_op jit(solution)/shard_map/pallas_call | solution.py:181
  390.5 12.0 %shard_map.93.refs_8_ = bf16[64,128,8,128]{3,2,1,0:T(8,128)(2,1)} custom-call(bf16[40,128,128]{2,1,0:T(8,128)(2,1)} %collective-permute-done.35.refs_0_, bf16[40,128,128]{2,1,0:T(8,128)(2,1)} %collective-permute-done.36.refs_1_, bf16[40,128,128]{2,1,0:T(8,128)(2,1)} %collective-permute-done.37.refs_2_, ...), custom_call_target="tpu_custom_call" | custom-call | flops 1600000000 | bytes 20971520 | tf_op jit(solution)/shard_map/pallas_call | solution.py:181
  402.5 5.2 %shard_map.94.refs_8_ = bf16[64,128,8,128]{3,2,1,0:T(8,128)(2,1)} custom-call(bf16[16,128,128]{2,1,0:T(8,128)(2,1)} %copy-done.13, bf16[16,128,128]{2,1,0:T(8,128)(2,1)} %copy-done.14, bf16[16,128,128]{2,1,0:T(8,128)(2,1)} %copy-done.15, bf16[16,128,128]{2,1,0:T(8,128)(2,1)} %copy-done.16, ...), custom_call_target="tpu_custom_call", output_to_operand_aliasing={{}: (8, {})} | custom-call | flops 640000000 | bytes 8388608 | tf_op jit(solution)/shard_map/pallas_call | solution.py:181
  407.7 3.9 shard_map.95.refs_8_
  412.6 8.6 %collective-permute-done.4.refs_4_ = bf16[48,128,128]{2,1,0:T(8,128)(2,1)} collective-permute-done((bf16[48,128,128]{2,1,0:T(8,128)(2,1)}, bf16[48,128,128]{2,1,0:T(8,128)(2,1)}, u32[]{:S(2)}, u32[]{:S(2)}) %collective-permute-start.4) | collective-permute-done | bytes 1572896 | tf_op jit(solution)/shard_map/ppermute | solution.py:217
  421.2 13.1 %shard_map.88 = bf16[64,128,8,128]{3,2,1,0:T(8,128)(2,1)} custom-call(bf16[48,128,128]{2,1,0:T(8,128)(2,1)} %copy-done.9, bf16[48,128,128]{2,1,0:T(8,128)(2,1)} %collective-permute-done.1.refs_1_, bf16[48,128,128]{2,1,0:T(8,128)(2,1)} %collective-permute-done.2.refs_2_, ...), custom_call_target="tpu_custom_call", output_to_operand_aliasing={{}: (8, {})} | custom-call | flops 1920000000 | bytes 25165824 | tf_op jit(solution)/shard_map/pallas_call | solution.py:181
  (152 shorter events, 51.7 us)
Async XLA Ops:
  33.5 44.3 %collective-permute-start.7 = (bf16[16,128,128]{2,1,0:T(8,128)(2,1)S(1)}, bf16[16,128,128]{2,1,0:T(8,128)(2,1)S(1)}, u32[]{:S(2)}, u32[]{:S(2)}) collective-permute-start(bf16[16,128,128]{2,1,0:T(8,128)(2,1)S(1)} %pack_first.1), channel_id=1, source_target_pairs={{0,4},{1,5},{2,6},{3,7},{4,0},{5,1},{6,2},{7,3},{8,12},{9,13},{10,... | collective-permute-start | bytes 1572872 | tf_op jit(solution)/shard_map/ppermute | solution.py:217
  33.6 48.0 %collective-permute-start.8 = (bf16[16,128,128]{2,1,0:T(8,128)(2,1)}, bf16[16,128,128]{2,1,0:T(8,128)(2,1)}, u32[]{:S(2)}, u32[]{:S(2)}) collective-permute-start(bf16[16,128,128]{2,1,0:T(8,128)(2,1)} %get-tuple-element.58), channel_id=1, source_target_pairs={{0,5},{1,4},{2,7},{3,6},{4,1},{5,0},{6,3},{7,2},{8,13},{9,12},{10,... | collective-permute-start | bytes 1572872 | tf_op jit(solution)/shard_map/ppermute | solution.py:217
  41.6 27.0 %collective-permute-start.25 = (bf16[6,128,128]{2,1,0:T(8,128)(2,1)S(1)}, bf16[6,128,128]{2,1,0:T(8,128)(2,1)S(1)}, u32[]{:S(2)}, u32[]{:S(2)}) collective-permute-start(bf16[6,128,128]{2,1,0:T(8,128)(2,1)S(1)} %copy-done.32), channel_id=1, source_target_pairs={{0,3},{1,2},{2,5},{3,4},{4,7},{5,6},{6,1},{7,0},{8,11},{9,10},{10,... | collective-permute-start | bytes 589832 | tf_op jit(solution)/shard_map/ppermute | solution.py:217
  77.9 38.3 %collective-permute-start.11 = (bf16[16,128,128]{2,1,0:T(8,128)(2,1)}, bf16[16,128,128]{2,1,0:T(8,128)(2,1)S(1)}, u32[]{:S(2)}, u32[]{:S(2)}) collective-permute-start(bf16[16,128,128]{2,1,0:T(8,128)(2,1)} %get-tuple-element.61), channel_id=1, source_target_pairs={{0,3},{1,2},{2,5},{3,4},{4,7},{5,6},{6,1},{7,0},{8,11},{9,10},{10,... | collective-permute-start | bytes 1572872 | tf_op jit(solution)/shard_map/ppermute | solution.py:217
  78.7 43.2 %collective-permute-start.12 = (bf16[16,128,128]{2,1,0:T(8,128)(2,1)}, bf16[16,128,128]{2,1,0:T(8,128)(2,1)}, u32[]{:S(2)}, u32[]{:S(2)}) collective-permute-start(bf16[16,128,128]{2,1,0:T(8,128)(2,1)} %get-tuple-element.62), channel_id=1, source_target_pairs={{0,7},{1,6},{2,1},{3,0},{4,3},{5,2},{6,5},{7,4},{8,15},{9,14},{10,... | collective-permute-start | bytes 1572872 | tf_op jit(solution)/shard_map/ppermute | solution.py:217
  81.6 44.4 %collective-permute-start.13 = (bf16[16,128,128]{2,1,0:T(8,128)(2,1)}, bf16[16,128,128]{2,1,0:T(8,128)(2,1)}, u32[]{:S(2)}, u32[]{:S(2)}) collective-permute-start(bf16[16,128,128]{2,1,0:T(8,128)(2,1)} %get-tuple-element.63), channel_id=1, source_target_pairs={{0,1},{1,0},{2,3},{3,2},{4,5},{5,4},{6,7},{7,6},{8,9},{9,8},{10,11... | collective-permute-start | bytes 1572872 | tf_op jit(solution)/shard_map/ppermute | solution.py:217
  88.7 49.4 %collective-permute-start.28 = (bf16[16,128,128]{2,1,0:T(8,128)(2,1)}, bf16[16,128,128]{2,1,0:T(8,128)(2,1)S(1)}, u32[]{:S(2)}, u32[]{:S(2)}) collective-permute-start(bf16[16,128,128]{2,1,0:T(8,128)(2,1)} %get-tuple-element.81), channel_id=1, source_target_pairs={{0,4},{1,5},{2,6},{3,7},{4,0},{5,1},{6,2},{7,3},{8,12},{9,13},{10,... | collective-permute-start | bytes 1572872 | tf_op jit(solution)/shard_map/ppermute | solution.py:217
  88.9 49.7 %collective-permute-start.29 = (bf16[16,128,128]{2,1,0:T(8,128)(2,1)}, bf16[16,128,128]{2,1,0:T(8,128)(2,1)S(1)}, u32[]{:S(2)}, u32[]{:S(2)}) collective-permute-start(bf16[16,128,128]{2,1,0:T(8,128)(2,1)} %get-tuple-element.82), channel_id=1, source_target_pairs={{0,5},{1,4},{2,7},{3,6},{4,1},{5,0},{6,3},{7,2},{8,13},{9,12},{10,... | collective-permute-start | bytes 1572872 | tf_op jit(solution)/shard_map/ppermute | solution.py:217
  126.0 72.9 %collective-permute-start.32 = (bf16[16,128,128]{2,1,0:T(8,128)(2,1)}, bf16[16,128,128]{2,1,0:T(8,128)(2,1)S(1)}, u32[]{:S(2)}, u32[]{:S(2)}) collective-permute-start(bf16[16,128,128]{2,1,0:T(8,128)(2,1)} %get-tuple-element.85), channel_id=1, source_target_pairs={{0,3},{1,2},{2,5},{3,4},{4,7},{5,6},{6,1},{7,0},{8,11},{9,10},{10,... | collective-permute-start | bytes 1572872 | tf_op jit(solution)/shard_map/ppermute | solution.py:217
  138.1 112.3 %collective-permute-start.35 = (bf16[40,128,128]{2,1,0:T(8,128)(2,1)}, bf16[40,128,128]{2,1,0:T(8,128)(2,1)}, u32[]{:S(2)}, u32[]{:S(2)}) collective-permute-start(bf16[40,128,128]{2,1,0:T(8,128)(2,1)} %get-tuple-element.89), channel_id=1, source_target_pairs={{0,4},{1,5},{2,6},{3,7},{4,0},{5,1},{6,2},{7,3},{8,12},{9,13},{10,... | collective-permute-start | bytes 3932168 | tf_op jit(solution)/shard_map/ppermute | solution.py:217
  138.6 115.5 %collective-permute-start.36 = (bf16[40,128,128]{2,1,0:T(8,128)(2,1)}, bf16[40,128,128]{2,1,0:T(8,128)(2,1)}, u32[]{:S(2)}, u32[]{:S(2)}) collective-permute-start(bf16[40,128,128]{2,1,0:T(8,128)(2,1)} %get-tuple-element.90), channel_id=1, source_target_pairs={{0,5},{1,4},{2,7},{3,6},{4,1},{5,0},{6,3},{7,2},{8,13},{9,12},{10,... | collective-permute-start | bytes 3932168 | tf_op jit(solution)/shard_map/ppermute | solution.py:217
  140.7 113.4 %collective-permute-start.37 = (bf16[40,128,128]{2,1,0:T(8,128)(2,1)}, bf16[40,128,128]{2,1,0:T(8,128)(2,1)}, u32[]{:S(2)}, u32[]{:S(2)}) collective-permute-start(bf16[40,128,128]{2,1,0:T(8,128)(2,1)} %get-tuple-element.91), channel_id=1, source_target_pairs={{0,2},{1,3},{2,4},{3,5},{4,6},{5,7},{6,0},{7,1},{8,10},{9,11},{10,... | collective-permute-start | bytes 3932168 | tf_op jit(solution)/shard_map/ppermute | solution.py:217
  141.1 115.9 %collective-permute-start.38 = (bf16[40,128,128]{2,1,0:T(8,128)(2,1)}, bf16[40,128,128]{2,1,0:T(8,128)(2,1)}, u32[]{:S(2)}, u32[]{:S(2)}) collective-permute-start(bf16[40,128,128]{2,1,0:T(8,128)(2,1)} %get-tuple-element.92), channel_id=1, source_target_pairs={{0,6},{1,7},{2,0},{3,1},{4,2},{5,3},{6,4},{7,5},{8,14},{9,15},{10,... | collective-permute-start | bytes 3932168 | tf_op jit(solution)/shard_map/ppermute | solution.py:217
  199.0 38.3 %collective-permute-start.33 = (bf16[16,128,128]{2,1,0:T(8,128)(2,1)}, bf16[16,128,128]{2,1,0:T(8,128)(2,1)S(1)}, u32[]{:S(2)}, u32[]{:S(2)}) collective-permute-start(bf16[16,128,128]{2,1,0:T(8,128)(2,1)} %get-tuple-element.86), channel_id=1, source_target_pairs={{0,7},{1,6},{2,1},{3,0},{4,3},{5,2},{6,5},{7,4},{8,15},{9,14},{10,... | collective-permute-start | bytes 1572872 | tf_op jit(solution)/shard_map/ppermute | solution.py:217
  250.0 102.9 %collective-permute-start = (bf16[48,128,128]{2,1,0:T(8,128)(2,1)}, bf16[48,128,128]{2,1,0:T(8,128)(2,1)S(1)}, u32[]{:S(2)}, u32[]{:S(2)}) collective-permute-start(bf16[48,128,128]{2,1,0:T(8,128)(2,1)} %get-tuple-element.50), channel_id=1, source_target_pairs={{0,4},{1,5},{2,6},{3,7},{4,0},{5,1},{6,2},{7,3},{8,12},{9,13},{10,... | collective-permute-start | bytes 4718600 | tf_op jit(solution)/shard_map/ppermute | solution.py:217
  250.4 105.5 %collective-permute-start.1 = (bf16[48,128,128]{2,1,0:T(8,128)(2,1)}, bf16[48,128,128]{2,1,0:T(8,128)(2,1)}, u32[]{:S(2)}, u32[]{:S(2)}) collective-permute-start(bf16[48,128,128]{2,1,0:T(8,128)(2,1)} %get-tuple-element.51), channel_id=1, source_target_pairs={{0,5},{1,4},{2,7},{3,6},{4,1},{5,0},{6,3},{7,2},{8,13},{9,12},{10,... | collective-permute-start | bytes 4718600 | tf_op jit(solution)/shard_map/ppermute | solution.py:217
  254.1 95.8 %collective-permute-start.39 = (bf16[40,128,128]{2,1,0:T(8,128)(2,1)}, bf16[40,128,128]{2,1,0:T(8,128)(2,1)S(1)}, u32[]{:S(2)}, u32[]{:S(2)}) collective-permute-start(bf16[40,128,128]{2,1,0:T(8,128)(2,1)} %get-tuple-element.93), channel_id=1, source_target_pairs={{0,3},{1,2},{2,5},{3,4},{4,7},{5,6},{6,1},{7,0},{8,11},{9,10},{10,... | collective-permute-start | bytes 3932168 | tf_op jit(solution)/shard_map/ppermute | solution.py:217
  254.1 96.4 %collective-permute-start.40 = (bf16[40,128,128]{2,1,0:T(8,128)(2,1)}, bf16[40,128,128]{2,1,0:T(8,128)(2,1)S(1)}, u32[]{:S(2)}, u32[]{:S(2)}) collective-permute-start(bf16[40,128,128]{2,1,0:T(8,128)(2,1)} %get-tuple-element.94), channel_id=1, source_target_pairs={{0,7},{1,6},{2,1},{3,0},{4,3},{5,2},{6,5},{7,4},{8,15},{9,14},{10,... | collective-permute-start | bytes 3932168 | tf_op jit(solution)/shard_map/ppermute | solution.py:217
  257.0 95.8 %collective-permute-start.41 = (bf16[40,128,128]{2,1,0:T(8,128)(2,1)}, bf16[40,128,128]{2,1,0:T(8,128)(2,1)S(1)}, u32[]{:S(2)}, u32[]{:S(2)}) collective-permute-start(bf16[40,128,128]{2,1,0:T(8,128)(2,1)} %get-tuple-element.95), channel_id=1, source_target_pairs={{0,1},{1,0},{2,3},{3,2},{4,5},{5,4},{6,7},{7,6},{8,9},{9,8},{10,11... | collective-permute-start | bytes 3932168 | tf_op jit(solution)/shard_map/ppermute | solution.py:217
  349.9 62.8 %collective-permute-start.2 = (bf16[48,128,128]{2,1,0:T(8,128)(2,1)}, bf16[48,128,128]{2,1,0:T(8,128)(2,1)}, u32[]{:S(2)}, u32[]{:S(2)}) collective-permute-start(bf16[48,128,128]{2,1,0:T(8,128)(2,1)} %get-tuple-element.52), channel_id=1, source_target_pairs={{0,2},{1,3},{2,4},{3,5},{4,6},{5,7},{6,0},{7,1},{8,10},{9,11},{10,... | collective-permute-start | bytes 4718600 | tf_op jit(solution)/shard_map/ppermute | solution.py:217
  350.5 62.1 %collective-permute-start.3 = (bf16[48,128,128]{2,1,0:T(8,128)(2,1)}, bf16[48,128,128]{2,1,0:T(8,128)(2,1)}, u32[]{:S(2)}, u32[]{:S(2)}) collective-permute-start(bf16[48,128,128]{2,1,0:T(8,128)(2,1)} %get-tuple-element.53), channel_id=1, source_target_pairs={{0,6},{1,7},{2,0},{3,1},{4,2},{5,3},{6,4},{7,5},{8,14},{9,15},{10,... | collective-permute-start | bytes 4718600 | tf_op jit(solution)/shard_map/ppermute | solution.py:217
  352.8 68.4 %collective-permute-start.4 = (bf16[48,128,128]{2,1,0:T(8,128)(2,1)}, bf16[48,128,128]{2,1,0:T(8,128)(2,1)}, u32[]{:S(2)}, u32[]{:S(2)}) collective-permute-start(bf16[48,128,128]{2,1,0:T(8,128)(2,1)} %get-tuple-element.54), channel_id=1, source_target_pairs={{0,3},{1,2},{2,5},{3,4},{4,7},{5,6},{6,1},{7,0},{8,11},{9,10},{10,... | collective-permute-start | bytes 4718600 | tf_op jit(solution)/shard_map/ppermute | solution.py:217
  352.9 68.3 %collective-permute-start.5 = (bf16[48,128,128]{2,1,0:T(8,128)(2,1)}, bf16[48,128,128]{2,1,0:T(8,128)(2,1)}, u32[]{:S(2)}, u32[]{:S(2)}) collective-permute-start(bf16[48,128,128]{2,1,0:T(8,128)(2,1)} %get-tuple-element.55), channel_id=1, source_target_pairs={{0,7},{1,6},{2,1},{3,0},{4,3},{5,2},{6,5},{7,4},{8,15},{9,14},{10,... | collective-permute-start | bytes 4718600 | tf_op jit(solution)/shard_map/ppermute | solution.py:217
  355.9 65.3 %collective-permute-start.6 = (bf16[48,128,128]{2,1,0:T(8,128)(2,1)}, bf16[48,128,128]{2,1,0:T(8,128)(2,1)}, u32[]{:S(2)}, u32[]{:S(2)}) collective-permute-start(bf16[48,128,128]{2,1,0:T(8,128)(2,1)} %get-tuple-element.56), channel_id=1, source_target_pairs={{0,1},{1,0},{2,3},{3,2},{4,5},{5,4},{6,7},{7,6},{8,9},{9,8},{10,11... | collective-permute-start | bytes 4718600 | tf_op jit(solution)/shard_map/ppermute | solution.py:217
  (57 other events, 1197.7 us)

commit v4 on v3

--- a/solution.py
+++ b/solution.py
@@ -9,7 +9,8 @@
 
 
 MASK_VALUE = -1e30
-CHUNKS = ((0, 0, 16, 8), (0, 16, 48, 8), (1, 0, 40, 8), (1, 40, 16, 8), (1, 56, 6, 2), (1, 62, 2, 1))
+CHUNKS = ((0, 0, 20, 4), (0, 20, 44, 4), (1, 12, 50, 2), (1, 0, 12, 6), (1, 62, 2, 2))
+ROOM = pltpu.CompilerParams(vmem_limit_bytes=65_900_000)
 
 
 def offsets(n):
@@ -115,6 +116,7 @@
         out_specs=pl.BlockSpec(memory_space=pltpu.VMEM),
         scratch_shapes=[pltpu.SMEM(lens.shape, lens.dtype), pltpu.VMEM(new.shape, new.dtype),
                         pltpu.VMEM(new.shape, jnp.float32), pltpu.SemaphoreType.DMA((3,))],
+        compiler_params=ROOM,
         cost_estimate=pl.CostEstimate(flops=count * 4_000_000, bytes_accessed=4 * count * seq_len // n * head_dim, transcendentals=0),
     )(lens, src, new)
 
@@ -131,6 +133,7 @@
         out_specs=[any_spec] * len(peers),
         scratch_shapes=[pltpu.VMEM((slots, size, seq_local, head_dim), src.dtype), pltpu.VMEM(new.shape, new.dtype),
                         pltpu.VMEM(new.shape, jnp.float32), pltpu.SemaphoreType.DMA((slots,)), pltpu.SemaphoreType.DMA((slots,)), pltpu.SemaphoreType.DMA],
+        compiler_params=ROOM,
         cost_estimate=pl.CostEstimate(flops=len(peers) * count * 4_000_000, bytes_accessed=4 * len(peers) * count * seq_local * head_dim, transcendentals=0),
     )(lens, src, new)
 
@@ -168,28 +171,54 @@
 def relayout_kernel(n, sources, *refs):
     xs, (o_ref, held) = refs[:n], refs[-2:]
     me = lax.axis_index("tp")
-    block = o_ref.shape[0]
-    for i in range(block):
+    for i in range(o_ref.shape[0]):
         for x_ref, source in zip(xs, sources):
-            row = i if x_ref.shape[0] == block else pl.program_id(0) * block + i
-            held[i % 2, at(n, me, *source)] = x_ref[row]
+            held[i % 2, at(n, me, *source)] = x_ref[i]
         o_ref[i] = jnp.swapaxes(held[i % 2], 0, 1)
 
 
-def relayout(n, sources, xs, whole, first, batch, block, resident=False):
+def relayout(n, sources, xs, whole, first, batch, block):
     count, seq_local, head_dim = xs[0].shape
     return pl.pallas_call(
         functools.partial(relayout_kernel, n, sources),
         grid=(count // block,),
         out_shape=jax.ShapeDtypeStruct((batch, seq_local, n, head_dim), xs[0].dtype),
-        in_specs=[pl.BlockSpec(memory_space=pltpu.VMEM) if resident else pl.BlockSpec((block, seq_local, head_dim), lambda i: (i, 0, 0))] * n
+        in_specs=[pl.BlockSpec((block, seq_local, head_dim), lambda i: (i, 0, 0))] * n
         + ([] if whole is None else [pl.BlockSpec(memory_space=pl.ANY)]),
         out_specs=pl.BlockSpec((block, seq_local, n, head_dim), lambda i: (first // block + i, 0, 0, 0)),
         scratch_shapes=[pltpu.VMEM((2, n, seq_local, head_dim), xs[0].dtype)],
         input_output_aliases={} if whole is None else {n: 0},
-        compiler_params=pltpu.CompilerParams(vmem_limit_bytes=8 * 2**20) if resident else None,
+        compiler_params=ROOM,
         cost_estimate=pl.CostEstimate(flops=count * 40_000_000, bytes_accessed=4 * n * xs[0].size, transcendentals=0),
     )(*xs, *([] if whole is None else [whole]))
+
+
+def last_relayout_kernel(n, sources, first, *refs):
+    xs, (o_ref, held, ready, sem) = refs[:n], refs[-4:]
+    me = lax.axis_index("tp")
+    copies = []
+    for i in range(ready.shape[0]):
+        for x_ref, source in zip(xs, sources):
+            held[i, at(n, me, *source)] = x_ref[i]
+        ready[i] = jnp.swapaxes(held[i], 0, 1)
+        copies.append(pltpu.make_async_copy(ready.at[i], o_ref.at[first + i], sem.at[i]))
+        copies[-1].start()
+    for copy in copies:
+        copy.wait()
+
+
+def last_relayout(n, sources, xs, whole, first):
+    count, seq_local, head_dim = xs[0].shape
+    return pl.pallas_call(
+        functools.partial(last_relayout_kernel, n, sources, first),
+        out_shape=jax.ShapeDtypeStruct(whole.shape, whole.dtype),
+        in_specs=[pl.BlockSpec(memory_space=pltpu.VMEM)] * n + [pl.BlockSpec(memory_space=pl.ANY)],
+        out_specs=pl.BlockSpec(memory_space=pl.ANY),
+        scratch_shapes=[pltpu.VMEM((count, n, seq_local, head_dim), whole.dtype), pltpu.VMEM((count, seq_local, n, head_dim), whole.dtype),
+                        pltpu.SemaphoreType.DMA((count,))],
+        input_output_aliases={n: 0},
+        compiler_params=pltpu.CompilerParams(vmem_limit_bytes=8 * 2**20),
+    )(*xs, whole)
 
 
 def solution(mesh):
@@ -229,13 +258,17 @@
             in_specs=[pl.BlockSpec(memory_space=pltpu.SMEM), head_block, cache_block, cache_block, vmem_spec, vmem_spec],
             out_specs=head_block,
             scratch_shapes=[pltpu.VMEM((batch, head_dim), jnp.float32)] * 2,
+            compiler_params=ROOM,
             cost_estimate=pl.CostEstimate(flops=10**11, bytes_accessed=4 * k_cache.size, transcendentals=0),
         )
         attn = attend(lens, query, k_cache, v_cache, k_new, v_new)
 
         moved = [None, None]
         for c, (a, first, count, size) in enumerate(CHUNKS):
-            moved[a] = relayout(n, sources, got[c], moved[a], first, batch, size, resident=c + 1 == len(CHUNKS))
+            if c + 1 < len(CHUNKS):
+                moved[a] = relayout(n, sources, got[c], moved[a], first, batch, size)
+            else:
+                moved[a] = last_relayout(n, sources, got[c], moved[a], first)
         return attn, *moved
 
 

time: 436 us -> 414 us (0.950)
  waiting for transfers between devices: 254 us -> 182 us
  starting transfers between devices: 57.1 us -> 105 us
    ppermute x42 -> x35, waiting for transfers between devices: 254 us -> 182 us  [local_step(): slabs[i] = lax.ppermute(slabs[i], 'tp', pairs(n, *peer))]
    ppermute x42 -> x35, starting transfers between devices: 57.1 us -> 105 us  [local_step(): slabs[i] = lax.ppermute(slabs[i], 'tp', pairs(n, *peer))]
    pallas_call x6 -> x4, Pallas kernels: 40.1 us -> 47.7 us  [relayout(): pl.pallas_call(functools.partial(relayout_kernel, n, sources), grid=(coun...]
    pallas_call x6 -> x5, Pallas kernels: 46.8 us -> 42.6 us  [pack(): pl.pallas_call(functools.partial(pack_kernel, n, peers, first, pieces), o...]
  transfers between devices with their start and end apart: 42 -> 35, of which waited for: 11 -> 10; matrix products, arithmetic and copies ran while one was open for 0% -> 0% of each run, Pallas kernels for 23% -> 28%
where the time goes in v4:
time: 414 us; the launch traced here: 411 us
  waiting for transfers between devices  182 us (44%)
  Pallas kernels  121 us (29%)
  starting transfers between devices  105 us (25%)
    ppermute x35, waiting for transfers between devices, local_step(): slabs[i] = lax.ppermute(slabs[i], 'tp', pairs(n, *peer))  182 us
    ppermute x35, starting transfers between devices, local_step(): slabs[i] = lax.ppermute(slabs[i], 'tp', pairs(n, *peer))  105 us
    pallas_call x4, Pallas kernels, relayout(): pl.pallas_call(functools.partial(relayout_kernel, n, sources), grid=(coun...  47.7 us
    pallas_call x5, Pallas kernels, pack(): pl.pallas_call(functools.partial(pack_kernel, n, peers, first, pieces), o...  42.6 us
    pallas_call x1, Pallas kernels, local_step(): attn = attend(lens, query, k_cache, v_cache, k_new, v_new)  28.9 us
  transfers between devices with their start and end apart: 35, of which 10 were waited for; matrix products, arithmetic and copies ran while one was open for 0% of the time, Pallas kernels for 28%

profile of v4, /device:TPU:113, one launch (start us, length us, event | category | flops | bytes accessed | tf_op | source)
XLA Modules:
  0.0 411.4 jit_solution(9084539776512099190)
XLA Ops:
  0.6 6.0 %shard_map.90 = (bf16[12,128,128]{2,1,0:T(8,128)(2,1)}, bf16[12,128,128]{2,1,0:T(8,128)(2,1)}, bf16[12,128,128]{2,1,0:T(8,128)(2,1)}, bf16[12,128,128]{2,1,0:T(8...) custom-call(s32[64]{0:T(128)} %lens_ref.13, ...), custom_call_target="tpu_custom_call" | custom-call | flops 384000000 | bytes 6291456 | tf_op jit(solution)/shard_map/pallas_call | solution.py:129
  6.7 3.7 collective-permute-start.21
  12.7 4.6 %shard_map.89 = (bf16[2,128,128]{2,1,0:T(8,128)(2,1)}, bf16[2,128,128]{2,1,0:T(8,128)(2,1)}, bf16[2,128,128]{2,1,0:T(8,128)(2,1)}, bf16[2,128,128]{2,1,0:T(8,128...) custom-call(s32[64]{0:T(128)} %lens_ref.13, ...), custom_call_target="tpu_custom_call" | custom-call | flops 64000000 | bytes 1048576 | tf_op jit(solution)/shard_map/pallas_call | solution.py:129
  20.3 17.6 %collective-permute-done.14.refs_0_ = bf16[2,128,128]{2,1,0:T(8,128)(2,1)S(1)} collective-permute-done((bf16[2,128,128]{2,1,0:T(8,128)(2,1)}, bf16[2,128,128]{2,1,0:T(8,128)(2,1)S(1)}, u32[]{:S(2)}, u32[]{:S(2)}) %collective-permute-start.14) | collective-permute-done | bytes 65568 | tf_op jit(solution)/shard_map/ppermute | solution.py:246
  47.8 6.5 %shard_map.86 = (bf16[20,128,128]{2,1,0:T(8,128)(2,1)}, bf16[20,128,128]{2,1,0:T(8,128)(2,1)}, bf16[20,128,128]{2,1,0:T(8,128)(2,1)}, bf16[20,128,128]{2,1,0:T(8...) custom-call(s32[64]{0:T(128)} %lens_ref.13, ...), custom_call_target="tpu_custom_call" | custom-call | flops 560000000 | bytes 9175040 | tf_op jit(solution)/shard_map/pallas_call | solution.py:129
  55.8 24.9 %collective-permute-start.9 = (bf16[20,128,128]{2,1,0:T(8,128)(2,1)}, bf16[20,128,128]{2,1,0:T(8,128)(2,1)}, u32[]{:S(2)}, u32[]{:S(2)}) collective-permute-start(bf16[20,128,128]{2,1,0:T(8,128)(2,1)} %get-tuple-element.51), channel_id=1, source_target_pairs={{0,2},{1,3},{2,4},{3,5},{4,6},{5,7},{6,0},{7,1},{8,10},{9,11},{10,... | collective-permute-start | bytes 1966088 | tf_op jit(solution)/shard_map/ppermute | solution.py:246
  80.8 2.8 collective-permute-start.11
  83.6 12.4 %shard_map.85 = (bf16[44,128,128]{2,1,0:T(8,128)(2,1)}, bf16[44,128,128]{2,1,0:T(8,128)(2,1)}, bf16[44,128,128]{2,1,0:T(8,128)(2,1)}, bf16[44,128,128]{2,1,0:T(8...) custom-call(s32[64]{0:T(128)} %lens_ref.13, ...), custom_call_target="tpu_custom_call" | custom-call | flops 1408000000 | bytes 23068672 | tf_op jit(solution)/shard_map/pallas_call | solution.py:129
  101.9 8.3 %collective-permute-done.11.refs_4_ = bf16[20,128,128]{2,1,0:T(8,128)(2,1)} collective-permute-done((bf16[20,128,128]{2,1,0:T(8,128)(2,1)}, bf16[20,128,128]{2,1,0:T(8,128)(2,1)}, u32[]{:S(2)}, u32[]{:S(2)}) %collective-permute-start.11) | collective-permute-done | bytes 655392 | tf_op jit(solution)/shard_map/ppermute | solution.py:246
  110.2 3.6 collective-permute-start.3
  113.8 33.5 %collective-permute-done.12.refs_5_ = bf16[20,128,128]{2,1,0:T(8,128)(2,1)S(1)} collective-permute-done((bf16[20,128,128]{2,1,0:T(8,128)(2,1)}, bf16[20,128,128]{2,1,0:T(8,128)(2,1)S(1)}, u32[]{:S(2)}, u32[]{:S(2)}) %collective-permute-start.12) | collective-permute-done | bytes 655392 | tf_op jit(solution)/shard_map/ppermute | solution.py:246
  147.3 13.0 %shard_map.91 = (bf16[50,128,128]{2,1,0:T(8,128)(2,1)}, bf16[50,128,128]{2,1,0:T(8,128)(2,1)}, bf16[50,128,128]{2,1,0:T(8,128)(2,1)}, bf16[50,128,128]{2,1,0:T(8...) custom-call(s32[64]{0:T(128)} %lens_ref.13, ...), custom_call_target="tpu_custom_call" | custom-call | flops 1600000000 | bytes 26214400 | tf_op jit(solution)/shard_map/pallas_call | solution.py:129
  160.3 29.7 %collective-permute-start.28 = (bf16[50,128,128]{2,1,0:T(8,128)(2,1)}, bf16[50,128,128]{2,1,0:T(8,128)(2,1)}, u32[]{:S(2)}, u32[]{:S(2)}) collective-permute-start(bf16[50,128,128]{2,1,0:T(8,128)(2,1)} %get-tuple-element.73), channel_id=1, source_target_pairs={{0,4},{1,5},{2,6},{3,7},{4,0},{5,1},{6,2},{7,3},{8,12},{9,13},{10,... | collective-permute-start | bytes 4915208 | tf_op jit(solution)/shard_map/ppermute | solution.py:246
  191.7 11.1 %collective-permute-done.2.refs_2_ = bf16[44,128,128]{2,1,0:T(8,128)(2,1)} collective-permute-done((bf16[44,128,128]{2,1,0:T(8,128)(2,1)}, bf16[44,128,128]{2,1,0:T(8,128)(2,1)}, u32[]{:S(2)}, u32[]{:S(2)}) %collective-permute-start.2) | collective-permute-done | bytes 1441824 | tf_op jit(solution)/shard_map/ppermute | solution.py:246
  202.9 3.9 collective-permute-start.5
  209.5 94.5 %collective-permute-done.4.refs_4_ = bf16[44,128,128]{2,1,0:T(8,128)(2,1)} collective-permute-done((bf16[44,128,128]{2,1,0:T(8,128)(2,1)}, bf16[44,128,128]{2,1,0:T(8,128)(2,1)}, u32[]{:S(2)}, u32[]{:S(2)}) %collective-permute-start.4) | collective-permute-done | bytes 1441824 | tf_op jit(solution)/shard_map/ppermute | solution.py:246
  310.8 3.0 collective-permute-start.33
  314.4 28.9 %attend.1 = bf16[64,4,128]{2,1,0:T(4,128)(2,1)} custom-call(s32[64]{0:T(128)} %lens_ref.13, bf16[64,4,128]{2,1,0:T(4,128)(2,1)} %q_ref.1, bf16[64,1024,128]{2,1,0:T(8,128)(2,1)} %bitcast.7, bf16[64,1024,128]{2,1,0:T(8,128)(2,1)} %bitcast.11, bf16[64,128]{1,0:T(8,128)(2,1)} %bitcast.15, bf16[64,128]{1,0:T(8,128)(2,1)} %bitcast.19), custom_call_target="tpu_custom_call" | custom-call | flops 99999997952 | bytes 33554432 | tf_op jit(solution)/shard_map/attend/pallas_call | solution.py:264
  343.3 7.9 %shard_map.87.refs_8_ = bf16[64,128,8,128]{3,2,1,0:T(8,128)(2,1)} custom-call(bf16[20,128,128]{2,1,0:T(8,128)(2,1)} %collective-permute-done.7.refs_0_, bf16[20,128,128]{2,1,0:T(8,128)(2,1)} %collective-permute-done.8.refs_1_, bf16[20,128,128]{2,1,0:T(8,128)(2,1)} %collective-permute-done.9.refs_2_, bf16[20,128,128]{2,1,0:T(8,128)(2,1)} %collective-permute-done.10.refs_3_, ...), custom_call_target="tpu_custom_call" | custom-call | flops 800000000 | bytes 10485760 | tf_op jit(solution)/shard_map/pallas_call | solution.py:182
  351.2 15.7 %shard_map.88 = bf16[64,128,8,128]{3,2,1,0:T(8,128)(2,1)} custom-call(bf16[44,128,128]{2,1,0:T(8,128)(2,1)} %collective-permute-done.refs_0_, bf16[44,128,128]{2,1,0:T(8,128)(2,1)} %collective-permute-done.1.refs_1_, bf16[44,128,128]{2,1,0:T(8,128)(2,1)} %collective-permute-done.2.refs_2_, ...), custom_call_target="tpu_custom_call", output_to_operand_aliasing={{}: (8, {})} | custom-call | flops 1760000000 | bytes 23068672 | tf_op jit(solution)/shard_map/pallas_call | solution.py:182
  369.6 9.4 %collective-permute-done.32.refs_4_ = bf16[50,128,128]{2,1,0:T(8,128)(2,1)} collective-permute-done((bf16[50,128,128]{2,1,0:T(8,128)(2,1)}, bf16[50,128,128]{2,1,0:T(8,128)(2,1)}, u32[]{:S(2)}, u32[]{:S(2)}) %collective-permute-start.32) | collective-permute-done | bytes 1638432 | tf_op jit(solution)/shard_map/ppermute | solution.py:246
  379.2 3.0 collective-permute-done.33.refs_5_
  386.0 19.9 %shard_map.92.refs_8_ = bf16[64,128,8,128]{3,2,1,0:T(8,128)(2,1)} custom-call(bf16[50,128,128]{2,1,0:T(8,128)(2,1)} %collective-permute-done.28.refs_0_, bf16[50,128,128]{2,1,0:T(8,128)(2,1)} %collective-permute-done.29.refs_1_, bf16[50,128,128]{2,1,0:T(8,128)(2,1)} %collective-permute-done.30.refs_2_, ...), custom_call_target="tpu_custom_call" | custom-call | flops 2000000000 | bytes 26214400 | tf_op jit(solution)/shard_map/pallas_call | solution.py:182
  405.9 4.3 %shard_map.93.refs_8_ = bf16[64,128,8,128]{3,2,1,0:T(8,128)(2,1)} custom-call(bf16[12,128,128]{2,1,0:T(8,128)(2,1)} %copy-done.6, bf16[12,128,128]{2,1,0:T(8,128)(2,1)} %copy-done.7, bf16[12,128,128]{2,1,0:T(8,128)(2,1)} %collective-permute-done.23.refs_2_, bf16[12,128,128]{2,1,0:T(8,128)(2,1)} %collective-permute-done.24.refs_3_, ...), custom_call_target="tpu_custom_call", output_to_operand_aliasing={{}: (8, {})} | custom-call | flops 480000000 | bytes 6291456 | tf_op jit(solution)/shard_map/pallas_call | solution.py:182
  (84 shorter events, 42.1 us)
Async XLA Ops:
  6.7 35.9 %collective-permute-start.21 = (bf16[12,128,128]{2,1,0:T(8,128)(2,1)}, bf16[12,128,128]{2,1,0:T(8,128)(2,1)S(1)}, u32[]{:S(2)}, u32[]{:S(2)}) collective-permute-start(bf16[12,128,128]{2,1,0:T(8,128)(2,1)} %get-tuple-element.65), channel_id=1, source_target_pairs={{0,4},{1,5},{2,6},{3,7},{4,0},{5,1},{6,2},{7,3},{8,12},{9,13},{10,... | collective-permute-start | bytes 1179656 | tf_op jit(solution)/shard_map/ppermute | solution.py:246
  10.8 35.7 %collective-permute-start.23 = (bf16[12,128,128]{2,1,0:T(8,128)(2,1)}, bf16[12,128,128]{2,1,0:T(8,128)(2,1)}, u32[]{:S(2)}, u32[]{:S(2)}) collective-permute-start(bf16[12,128,128]{2,1,0:T(8,128)(2,1)} %get-tuple-element.67), channel_id=1, source_target_pairs={{0,2},{1,3},{2,4},{3,5},{4,6},{5,7},{6,0},{7,1},{8,10},{9,11},{10,... | collective-permute-start | bytes 1179656 | tf_op jit(solution)/shard_map/ppermute | solution.py:246
  42.5 38.2 %collective-permute-start.26 = (bf16[12,128,128]{2,1,0:T(8,128)(2,1)}, bf16[12,128,128]{2,1,0:T(8,128)(2,1)}, u32[]{:S(2)}, u32[]{:S(2)}) collective-permute-start(bf16[12,128,128]{2,1,0:T(8,128)(2,1)} %get-tuple-element.70), channel_id=1, source_target_pairs={{0,7},{1,6},{2,1},{3,0},{4,3},{5,2},{6,5},{7,4},{8,15},{9,14},{10,... | collective-permute-start | bytes 1179656 | tf_op jit(solution)/shard_map/ppermute | solution.py:246
  44.5 36.3 %collective-permute-start.27 = (bf16[12,128,128]{2,1,0:T(8,128)(2,1)}, bf16[12,128,128]{2,1,0:T(8,128)(2,1)}, u32[]{:S(2)}, u32[]{:S(2)}) collective-permute-start(bf16[12,128,128]{2,1,0:T(8,128)(2,1)} %get-tuple-element.71), channel_id=1, source_target_pairs={{0,1},{1,0},{2,3},{3,2},{4,5},{5,4},{6,7},{7,6},{8,9},{9,8},{10,11... | collective-permute-start | bytes 1179656 | tf_op jit(solution)/shard_map/ppermute | solution.py:246
  46.5 49.5 %collective-permute-start.7 = (bf16[20,128,128]{2,1,0:T(8,128)(2,1)S(1)}, bf16[20,128,128]{2,1,0:T(8,128)(2,1)}, u32[]{:S(2)}, u32[]{:S(2)}) collective-permute-start(bf16[20,128,128]{2,1,0:T(8,128)(2,1)S(1)} %pack_first.1), channel_id=1, source_target_pairs={{0,4},{1,5},{2,6},{3,7},{4,0},{5,1},{6,2},{7,3},{8,12},{9,13},{10,... | collective-permute-start | bytes 1966088 | tf_op jit(solution)/shard_map/ppermute | solution.py:246
  54.3 43.4 %collective-permute-start.8 = (bf16[20,128,128]{2,1,0:T(8,128)(2,1)}, bf16[20,128,128]{2,1,0:T(8,128)(2,1)}, u32[]{:S(2)}, u32[]{:S(2)}) collective-permute-start(bf16[20,128,128]{2,1,0:T(8,128)(2,1)} %get-tuple-element.50), channel_id=1, source_target_pairs={{0,5},{1,4},{2,7},{3,6},{4,1},{5,0},{6,3},{7,2},{8,13},{9,12},{10,... | collective-permute-start | bytes 1966088 | tf_op jit(solution)/shard_map/ppermute | solution.py:246
  55.8 43.4 %collective-permute-start.9 = (bf16[20,128,128]{2,1,0:T(8,128)(2,1)}, bf16[20,128,128]{2,1,0:T(8,128)(2,1)}, u32[]{:S(2)}, u32[]{:S(2)}) collective-permute-start(bf16[20,128,128]{2,1,0:T(8,128)(2,1)} %get-tuple-element.51), channel_id=1, source_target_pairs={{0,2},{1,3},{2,4},{3,5},{4,6},{5,7},{6,0},{7,1},{8,10},{9,11},{10,... | collective-permute-start | bytes 1966088 | tf_op jit(solution)/shard_map/ppermute | solution.py:246
  96.1 94.0 %collective-permute-start = (bf16[44,128,128]{2,1,0:T(8,128)(2,1)}, bf16[44,128,128]{2,1,0:T(8,128)(2,1)}, u32[]{:S(2)}, u32[]{:S(2)}) collective-permute-start(bf16[44,128,128]{2,1,0:T(8,128)(2,1)} %get-tuple-element.42), channel_id=1, source_target_pairs={{0,4},{1,5},{2,6},{3,7},{4,0},{5,1},{6,2},{7,3},{8,12},{9,13},{10,... | collective-permute-start | bytes 4325384 | tf_op jit(solution)/shard_map/ppermute | solution.py:246
  97.8 49.5 %collective-permute-start.12 = (bf16[20,128,128]{2,1,0:T(8,128)(2,1)}, bf16[20,128,128]{2,1,0:T(8,128)(2,1)S(1)}, u32[]{:S(2)}, u32[]{:S(2)}) collective-permute-start(bf16[20,128,128]{2,1,0:T(8,128)(2,1)} %get-tuple-element.54), channel_id=1, source_target_pairs={{0,7},{1,6},{2,1},{3,0},{4,3},{5,2},{6,5},{7,4},{8,15},{9,14},{10,... | collective-permute-start | bytes 1966088 | tf_op jit(solution)/shard_map/ppermute | solution.py:246
  99.2 91.1 %collective-permute-start.1 = (bf16[44,128,128]{2,1,0:T(8,128)(2,1)}, bf16[44,128,128]{2,1,0:T(8,128)(2,1)}, u32[]{:S(2)}, u32[]{:S(2)}) collective-permute-start(bf16[44,128,128]{2,1,0:T(8,128)(2,1)} %get-tuple-element.43), channel_id=1, source_target_pairs={{0,5},{1,4},{2,7},{3,6},{4,1},{5,0},{6,3},{7,2},{8,13},{9,12},{10,... | collective-permute-start | bytes 4325384 | tf_op jit(solution)/shard_map/ppermute | solution.py:246
  101.5 101.4 %collective-permute-start.2 = (bf16[44,128,128]{2,1,0:T(8,128)(2,1)}, bf16[44,128,128]{2,1,0:T(8,128)(2,1)}, u32[]{:S(2)}, u32[]{:S(2)}) collective-permute-start(bf16[44,128,128]{2,1,0:T(8,128)(2,1)} %get-tuple-element.44), channel_id=1, source_target_pairs={{0,2},{1,3},{2,4},{3,5},{4,6},{5,7},{6,0},{7,1},{8,10},{9,11},{10,... | collective-permute-start | bytes 4325384 | tf_op jit(solution)/shard_map/ppermute | solution.py:246
  110.2 97.0 %collective-permute-start.3 = (bf16[44,128,128]{2,1,0:T(8,128)(2,1)}, bf16[44,128,128]{2,1,0:T(8,128)(2,1)}, u32[]{:S(2)}, u32[]{:S(2)}) collective-permute-start(bf16[44,128,128]{2,1,0:T(8,128)(2,1)} %get-tuple-element.45), channel_id=1, source_target_pairs={{0,6},{1,7},{2,0},{3,1},{4,2},{5,3},{6,4},{7,5},{8,14},{9,15},{10,... | collective-permute-start | bytes 4325384 | tf_op jit(solution)/shard_map/ppermute | solution.py:246
  160.3 150.5 %collective-permute-start.28 = (bf16[50,128,128]{2,1,0:T(8,128)(2,1)}, bf16[50,128,128]{2,1,0:T(8,128)(2,1)}, u32[]{:S(2)}, u32[]{:S(2)}) collective-permute-start(bf16[50,128,128]{2,1,0:T(8,128)(2,1)} %get-tuple-element.73), channel_id=1, source_target_pairs={{0,4},{1,5},{2,6},{3,7},{4,0},{5,1},{6,2},{7,3},{8,12},{9,13},{10,... | collective-permute-start | bytes 4915208 | tf_op jit(solution)/shard_map/ppermute | solution.py:246
  190.0 123.7 %collective-permute-start.29 = (bf16[50,128,128]{2,1,0:T(8,128)(2,1)}, bf16[50,128,128]{2,1,0:T(8,128)(2,1)}, u32[]{:S(2)}, u32[]{:S(2)}) collective-permute-start(bf16[50,128,128]{2,1,0:T(8,128)(2,1)} %get-tuple-element.74), channel_id=1, source_target_pairs={{0,5},{1,4},{2,7},{3,6},{4,1},{5,0},{6,3},{7,2},{8,13},{9,12},{10,... | collective-permute-start | bytes 4915208 | tf_op jit(solution)/shard_map/ppermute | solution.py:246
  190.3 113.7 %collective-permute-start.4 = (bf16[44,128,128]{2,1,0:T(8,128)(2,1)}, bf16[44,128,128]{2,1,0:T(8,128)(2,1)}, u32[]{:S(2)}, u32[]{:S(2)}) collective-permute-start(bf16[44,128,128]{2,1,0:T(8,128)(2,1)} %get-tuple-element.46), channel_id=1, source_target_pairs={{0,3},{1,2},{2,5},{3,4},{4,7},{5,6},{6,1},{7,0},{8,11},{9,10},{10,... | collective-permute-start | bytes 4325384 | tf_op jit(solution)/shard_map/ppermute | solution.py:246
  202.9 105.4 %collective-permute-start.5 = (bf16[44,128,128]{2,1,0:T(8,128)(2,1)}, bf16[44,128,128]{2,1,0:T(8,128)(2,1)}, u32[]{:S(2)}, u32[]{:S(2)}) collective-permute-start(bf16[44,128,128]{2,1,0:T(8,128)(2,1)} %get-tuple-element.47), channel_id=1, source_target_pairs={{0,7},{1,6},{2,1},{3,0},{4,3},{5,2},{6,5},{7,4},{8,15},{9,14},{10,... | collective-permute-start | bytes 4325384 | tf_op jit(solution)/shard_map/ppermute | solution.py:246
  207.2 103.6 %collective-permute-start.6 = (bf16[44,128,128]{2,1,0:T(8,128)(2,1)}, bf16[44,128,128]{2,1,0:T(8,128)(2,1)}, u32[]{:S(2)}, u32[]{:S(2)}) collective-permute-start(bf16[44,128,128]{2,1,0:T(8,128)(2,1)} %get-tuple-element.48), channel_id=1, source_target_pairs={{0,1},{1,0},{2,3},{3,2},{4,5},{5,4},{6,7},{7,6},{8,9},{9,8},{10,11... | collective-permute-start | bytes 4325384 | tf_op jit(solution)/shard_map/ppermute | solution.py:246
  304.0 62.8 %collective-permute-start.30 = (bf16[50,128,128]{2,1,0:T(8,128)(2,1)}, bf16[50,128,128]{2,1,0:T(8,128)(2,1)}, u32[]{:S(2)}, u32[]{:S(2)}) collective-permute-start(bf16[50,128,128]{2,1,0:T(8,128)(2,1)} %get-tuple-element.75), channel_id=1, source_target_pairs={{0,2},{1,3},{2,4},{3,5},{4,6},{5,7},{6,0},{7,1},{8,10},{9,11},{10,... | collective-permute-start | bytes 4915208 | tf_op jit(solution)/shard_map/ppermute | solution.py:246
  308.3 58.6 %collective-permute-start.31 = (bf16[50,128,128]{2,1,0:T(8,128)(2,1)}, bf16[50,128,128]{2,1,0:T(8,128)(2,1)}, u32[]{:S(2)}, u32[]{:S(2)}) collective-permute-start(bf16[50,128,128]{2,1,0:T(8,128)(2,1)} %get-tuple-element.76), channel_id=1, source_target_pairs={{0,6},{1,7},{2,0},{3,1},{4,2},{5,3},{6,4},{7,5},{8,14},{9,15},{10,... | collective-permute-start | bytes 4915208 | tf_op jit(solution)/shard_map/ppermute | solution.py:246
  310.7 68.3 %collective-permute-start.32 = (bf16[50,128,128]{2,1,0:T(8,128)(2,1)}, bf16[50,128,128]{2,1,0:T(8,128)(2,1)}, u32[]{:S(2)}, u32[]{:S(2)}) collective-permute-start(bf16[50,128,128]{2,1,0:T(8,128)(2,1)} %get-tuple-element.77), channel_id=1, source_target_pairs={{0,3},{1,2},{2,5},{3,4},{4,7},{5,6},{6,1},{7,0},{8,11},{9,10},{10,... | collective-permute-start | bytes 4915208 | tf_op jit(solution)/shard_map/ppermute | solution.py:246
  310.8 71.4 %collective-permute-start.33 = (bf16[50,128,128]{2,1,0:T(8,128)(2,1)}, bf16[50,128,128]{2,1,0:T(8,128)(2,1)}, u32[]{:S(2)}, u32[]{:S(2)}) collective-permute-start(bf16[50,128,128]{2,1,0:T(8,128)(2,1)} %get-tuple-element.78), channel_id=1, source_target_pairs={{0,7},{1,6},{2,1},{3,0},{4,3},{5,2},{6,5},{7,4},{8,15},{9,14},{10,... | collective-permute-start | bytes 4915208 | tf_op jit(solution)/shard_map/ppermute | solution.py:246
  313.7 70.9 %collective-permute-start.34 = (bf16[50,128,128]{2,1,0:T(8,128)(2,1)}, bf16[50,128,128]{2,1,0:T(8,128)(2,1)}, u32[]{:S(2)}, u32[]{:S(2)}) collective-permute-start(bf16[50,128,128]{2,1,0:T(8,128)(2,1)} %get-tuple-element.79), channel_id=1, source_target_pairs={{0,1},{1,0},{2,3},{3,2},{4,5},{5,4},{6,7},{7,6},{8,9},{9,8},{10,11... | collective-permute-start | bytes 4915208 | tf_op jit(solution)/shard_map/ppermute | solution.py:246
  366.9 43.3 %collective-permute-start.16 = (bf16[2,128,128]{2,1,0:T(8,128)(2,1)S(1)}, bf16[2,128,128]{2,1,0:T(8,128)(2,1)S(1)}, u32[]{:S(2)}, u32[]{:S(2)}) collective-permute-start(bf16[2,128,128]{2,1,0:T(8,128)(2,1)S(1)} %copy-done.12), channel_id=1, source_target_pairs={{0,2},{1,3},{2,4},{3,5},{4,6},{5,7},{6,0},{7,1},{8,10},{9,11},{10,... | collective-permute-start | bytes 196616 | tf_op jit(solution)/shard_map/ppermute | solution.py:246
  367.0 43.2 %collective-permute-start.17 = (bf16[2,128,128]{2,1,0:T(8,128)(2,1)S(1)}, bf16[2,128,128]{2,1,0:T(8,128)(2,1)S(1)}, u32[]{:S(2)}, u32[]{:S(2)}) collective-permute-start(bf16[2,128,128]{2,1,0:T(8,128)(2,1)S(1)} %copy-done.11), channel_id=1, source_target_pairs={{0,6},{1,7},{2,0},{3,1},{4,2},{5,3},{6,4},{7,5},{8,14},{9,15},{10,... | collective-permute-start | bytes 196616 | tf_op jit(solution)/shard_map/ppermute | solution.py:246
  (24 other events, 409.4 us)

commit v5 on v4

--- a/solution.py
+++ b/solution.py
@@ -9,8 +9,8 @@
 
 
 MASK_VALUE = -1e30
-CHUNKS = ((0, 0, 20, 4), (0, 20, 44, 4), (1, 12, 50, 2), (1, 0, 12, 6), (1, 62, 2, 2))
-ROOM = pltpu.CompilerParams(vmem_limit_bytes=65_900_000)
+CHUNKS = ((0, 0, 16, 16), (0, 16, 48, 16), (1, 12, 48, 12), (1, 0, 12, 6), (1, 60, 4, 4))
+ROOM = pltpu.CompilerParams(vmem_limit_bytes=65_520_000)
 
 
 def offsets(n):
@@ -240,13 +240,12 @@
             slabs = []
             if c == 0:
                 slabs.append(pack_first(n, lens, caches[a], news[a], peers[0], count))
-            pieces = 2 if count > 32 else 1
-            slabs += pack(n, lens, caches[a], news[a], peers[len(slabs):] + own, first, count, pieces, 4)
+            slabs += pack(n, lens, caches[a], news[a], peers[len(slabs):] + own, first, count, 1, 4)
             for i, peer in enumerate(peers):
                 slabs[i] = lax.ppermute(slabs[i], "tp", pairs(n, *peer))
             got.append(slabs)
 
-        block = 4
+        block = 8
         cache_block = pl.BlockSpec((block, seq_len, head_dim), lambda i: (i, 0, 0))
         head_block = pl.BlockSpec((block,) + query.shape[1:], lambda i: (i, 0, 0))
         vmem_spec = pl.BlockSpec(memory_space=pltpu.VMEM)

time: 414 us -> 392 us (0.947)
  starting transfers between devices: 105 us -> 45.2 us
  waiting for transfers between devices: 182 us -> 237 us
  Pallas kernels: 121 us -> 107 us
    ppermute x35, starting transfers between devices: 105 us -> 45.2 us  [local_step(): slabs[i] = lax.ppermute(slabs[i], 'tp', pairs(n, *peer))]
    ppermute x35, waiting for transfers between devices: 182 us -> 237 us  [local_step(): slabs[i] = lax.ppermute(slabs[i], 'tp', pairs(n, *peer))]
    pallas_call x4, Pallas kernels: 47.7 us -> 36.8 us  [relayout(): pl.pallas_call(functools.partial(relayout_kernel, n, sources), grid=(coun...]
  transfers between devices with their start and end apart: 35 -> 35, of which waited for: 10 -> 14; matrix products, arithmetic and copies ran while one was open for 0% -> 0% of each run, Pallas kernels for 28% -> 26%
where the time goes in v5:
time: 392 us
  waiting for transfers between devices  237 us (60%)
  Pallas kernels  107 us (27%)
  starting transfers between devices  45.2 us (12%)
    ppermute x35, waiting for transfers between devices, local_step(): slabs[i] = lax.ppermute(slabs[i], 'tp', pairs(n, *peer))  237 us
    ppermute x35, starting transfers between devices, local_step(): slabs[i] = lax.ppermute(slabs[i], 'tp', pairs(n, *peer))  45.2 us
    pallas_call x5, Pallas kernels, pack(): pl.pallas_call(functools.partial(pack_kernel, n, peers, first, pieces), o...  39.2 us
    pallas_call x4, Pallas kernels, relayout(): pl.pallas_call(functools.partial(relayout_kernel, n, sources), grid=(coun...  36.8 us
    pallas_call x1, Pallas kernels, local_step(): attn = attend(lens, query, k_cache, v_cache, k_new, v_new)  28.7 us
  transfers between devices with their start and end apart: 35, of which 14 were waited for; matrix products, arithmetic and copies ran while one was open for 0% of the time, Pallas kernels for 26%

profile of v5, /device:TPU:113, one launch (start us, length us, event | category | flops | bytes accessed | tf_op | source)
XLA Modules:
  0.0 391.6 jit_solution(15676037554762199306)
XLA Ops:
  0.6 6.0 %shard_map.90 = (bf16[12,128,128]{2,1,0:T(8,128)(2,1)}, bf16[12,128,128]{2,1,0:T(8,128)(2,1)}, bf16[12,128,128]{2,1,0:T(8,128)(2,1)}, bf16[12,128,128]{2,1,0:T(8...) custom-call(s32[64]{0:T(128)} %lens_ref.13, ...), custom_call_target="tpu_custom_call" | custom-call | flops 384000000 | bytes 6291456 | tf_op jit(solution)/shard_map/pallas_call | solution.py:129
  6.7 3.8 collective-permute-start.21
  10.4 5.0 %shard_map.89 = (bf16[4,128,128]{2,1,0:T(8,128)(2,1)}, bf16[4,128,128]{2,1,0:T(8,128)(2,1)}, bf16[4,128,128]{2,1,0:T(8,128)(2,1)}, bf16[4,128,128]{2,1,0:T(8,128...) custom-call(s32[64]{0:T(128)} %lens_ref.13, ...), custom_call_target="tpu_custom_call" | custom-call | flops 128000000 | bytes 2097152 | tf_op jit(solution)/shard_map/pallas_call | solution.py:129
  15.7 3.6 collective-permute-start.15
  30.5 4.5 %collective-permute-done.22.refs_1_ = bf16[12,128,128]{2,1,0:T(8,128)(2,1)} collective-permute-done((bf16[12,128,128]{2,1,0:T(8,128)(2,1)S(1)}, bf16[12,128,128]{2,1,0:T(8,128)(2,1)}, u32[]{:S(2)}, u32[]{:S(2)}) %collective-permute-start.22) | collective-permute-done | bytes 393248 | tf_op jit(solution)/shard_map/ppermute | solution.py:245
  35.0 5.7 %shard_map.86 = (bf16[16,128,128]{2,1,0:T(8,128)(2,1)}, bf16[16,128,128]{2,1,0:T(8,128)(2,1)}, bf16[16,128,128]{2,1,0:T(8,128)(2,1)}, bf16[16,128,128]{2,1,0:T(8...) custom-call(s32[64]{0:T(128)} %lens_ref.13, ...), custom_call_target="tpu_custom_call" | custom-call | flops 448000000 | bytes 7340032 | tf_op jit(solution)/shard_map/pallas_call | solution.py:129
  42.8 3.0 collective-permute-start.7
  46.7 5.2 %collective-permute-done.25.refs_4_ = bf16[12,128,128]{2,1,0:T(8,128)(2,1)} collective-permute-done((bf16[12,128,128]{2,1,0:T(8,128)(2,1)}, bf16[12,128,128]{2,1,0:T(8,128)(2,1)}, u32[]{:S(2)}, u32[]{:S(2)}) %collective-permute-start.25) | collective-permute-done | bytes 393248 | tf_op jit(solution)/shard_map/ppermute | solution.py:245
  55.2 11.2 %shard_map.85 = (bf16[48,128,128]{2,1,0:T(8,128)(2,1)}, bf16[48,128,128]{2,1,0:T(8,128)(2,1)}, bf16[48,128,128]{2,1,0:T(8,128)(2,1)}, bf16[48,128,128]{2,1,0:T(8...) custom-call(s32[64]{0:T(128)} %lens_ref.13, ...), custom_call_target="tpu_custom_call" | custom-call | flops 1536000000 | bytes 25165824 | tf_op jit(solution)/shard_map/pallas_call | solution.py:129
  66.5 11.3 %shard_map.91 = (bf16[48,128,128]{2,1,0:T(8,128)(2,1)}, bf16[48,128,128]{2,1,0:T(8,128)(2,1)}, bf16[48,128,128]{2,1,0:T(8,128)(2,1)}, bf16[48,128,128]{2,1,0:T(8...) custom-call(s32[64]{0:T(128)} %lens_ref.13, ...), custom_call_target="tpu_custom_call" | custom-call | flops 1536000000 | bytes 25165824 | tf_op jit(solution)/shard_map/pallas_call | solution.py:129
  80.9 4.1 %collective-permute-done.9.refs_2_ = bf16[16,128,128]{2,1,0:T(8,128)(2,1)} collective-permute-done((bf16[16,128,128]{2,1,0:T(8,128)(2,1)}, bf16[16,128,128]{2,1,0:T(8,128)(2,1)}, u32[]{:S(2)}, u32[]{:S(2)}) %collective-permute-start.9) | collective-permute-done | bytes 524320 | tf_op jit(solution)/shard_map/ppermute | solution.py:245
  85.0 3.0 collective-permute-start.28
  88.8 8.0 %collective-permute-done.11.refs_4_ = bf16[16,128,128]{2,1,0:T(8,128)(2,1)} collective-permute-done((bf16[16,128,128]{2,1,0:T(8,128)(2,1)}, bf16[16,128,128]{2,1,0:T(8,128)(2,1)}, u32[]{:S(2)}, u32[]{:S(2)}) %collective-permute-start.11) | collective-permute-done | bytes 524320 | tf_op jit(solution)/shard_map/ppermute | solution.py:245
  96.9 134.4 %collective-permute-done.12.refs_5_ = bf16[16,128,128]{2,1,0:T(8,128)(2,1)S(1)} collective-permute-done((bf16[16,128,128]{2,1,0:T(8,128)(2,1)}, bf16[16,128,128]{2,1,0:T(8,128)(2,1)S(1)}, u32[]{:S(2)}, u32[]{:S(2)}) %collective-permute-start.12) | collective-permute-done | bytes 524320 | tf_op jit(solution)/shard_map/ppermute | solution.py:245
  239.9 31.0 %collective-permute-done.30.refs_2_ = bf16[48,128,128]{2,1,0:T(8,128)(2,1)} collective-permute-done((bf16[48,128,128]{2,1,0:T(8,128)(2,1)}, bf16[48,128,128]{2,1,0:T(8,128)(2,1)}, u32[]{:S(2)}, u32[]{:S(2)}) %collective-permute-start.30) | collective-permute-done | bytes 1572896 | tf_op jit(solution)/shard_map/ppermute | solution.py:245
  270.9 2.7 collective-permute-start.3
  273.6 31.9 %collective-permute-done.32.refs_4_ = bf16[48,128,128]{2,1,0:T(8,128)(2,1)} collective-permute-done((bf16[48,128,128]{2,1,0:T(8,128)(2,1)}, bf16[48,128,128]{2,1,0:T(8,128)(2,1)}, u32[]{:S(2)}, u32[]{:S(2)}) %collective-permute-start.32) | collective-permute-done | bytes 1572896 | tf_op jit(solution)/shard_map/ppermute | solution.py:245
  308.9 28.7 %attend.1 = bf16[64,4,128]{2,1,0:T(4,128)(2,1)} custom-call(s32[64]{0:T(128)} %lens_ref.13, bf16[64,4,128]{2,1,0:T(4,128)(2,1)} %q_ref.1, bf16[64,1024,128]{2,1,0:T(8,128)(2,1)} %bitcast.7, bf16[64,1024,128]{2,1,0:T(8,128)(2,1)} %bitcast.11, bf16[64,128]{1,0:T(8,128)(2,1)} %bitcast.15, bf16[64,128]{1,0:T(8,128)(2,1)} %bitcast.19), custom_call_target="tpu_custom_call" | custom-call | flops 99999997952 | bytes 33554432 | tf_op jit(solution)/shard_map/attend/pallas_call | solution.py:263
  337.5 6.3 %shard_map.87.refs_8_ = bf16[64,128,8,128]{3,2,1,0:T(8,128)(2,1)} custom-call(bf16[16,128,128]{2,1,0:T(8,128)(2,1)} %copy-done.5, bf16[16,128,128]{2,1,0:T(8,128)(2,1)} %collective-permute-done.8.refs_1_, bf16[16,128,128]{2,1,0:T(8,128)(2,1)} %collective-permute-done.9.refs_2_, bf16[16,128,128]{2,1,0:T(8,128)(2,1)} %collective-permute-done.10.refs_3_, ...), custom_call_target="tpu_custom_call" | custom-call | flops 640000000 | bytes 8388608 | tf_op jit(solution)/shard_map/pallas_call | solution.py:182
  343.8 12.4 %shard_map.92.refs_8_ = bf16[64,128,8,128]{3,2,1,0:T(8,128)(2,1)} custom-call(bf16[48,128,128]{2,1,0:T(8,128)(2,1)} %collective-permute-done.28.refs_0_, bf16[48,128,128]{2,1,0:T(8,128)(2,1)} %collective-permute-done.29.refs_1_, bf16[48,128,128]{2,1,0:T(8,128)(2,1)} %collective-permute-done.30.refs_2_, ...), custom_call_target="tpu_custom_call" | custom-call | flops 1920000000 | bytes 25165824 | tf_op jit(solution)/shard_map/pallas_call | solution.py:182
  356.3 4.3 %shard_map.93.refs_8_ = bf16[64,128,8,128]{3,2,1,0:T(8,128)(2,1)} custom-call(bf16[12,128,128]{2,1,0:T(8,128)(2,1)} %copy-done.7, bf16[12,128,128]{2,1,0:T(8,128)(2,1)} %collective-permute-done.22.refs_1_, bf16[12,128,128]{2,1,0:T(8,128)(2,1)} %collective-permute-done.23.refs_2_, ...), custom_call_target="tpu_custom_call", output_to_operand_aliasing={{}: (8, {})} | custom-call | flops 480000000 | bytes 6291456 | tf_op jit(solution)/shard_map/pallas_call | solution.py:182
  360.7 2.6 collective-permute-start.17
  363.3 9.6 %collective-permute-done.4.refs_4_ = bf16[48,128,128]{2,1,0:T(8,128)(2,1)} collective-permute-done((bf16[48,128,128]{2,1,0:T(8,128)(2,1)}, bf16[48,128,128]{2,1,0:T(8,128)(2,1)}, u32[]{:S(2)}, u32[]{:S(2)}) %collective-permute-start.4) | collective-permute-done | bytes 1572896 | tf_op jit(solution)/shard_map/ppermute | solution.py:245
  376.3 13.8 %shard_map.88 = bf16[64,128,8,128]{3,2,1,0:T(8,128)(2,1)} custom-call(bf16[48,128,128]{2,1,0:T(8,128)(2,1)} %collective-permute-done.refs_0_, bf16[48,128,128]{2,1,0:T(8,128)(2,1)} %collective-permute-done.1.refs_1_, bf16[48,128,128]{2,1,0:T(8,128)(2,1)} %collective-permute-done.2.refs_2_, ...), custom_call_target="tpu_custom_call", output_to_operand_aliasing={{}: (8, {})} | custom-call | flops 1920000000 | bytes 25165824 | tf_op jit(solution)/shard_map/pallas_call | solution.py:182
  (84 shorter events, 38.5 us)
Async XLA Ops:
  27.9 25.7 %collective-permute-start.26 = (bf16[12,128,128]{2,1,0:T(8,128)(2,1)}, bf16[12,128,128]{2,1,0:T(8,128)(2,1)}, u32[]{:S(2)}, u32[]{:S(2)}) collective-permute-start(bf16[12,128,128]{2,1,0:T(8,128)(2,1)} %get-tuple-element.70), channel_id=1, source_target_pairs={{0,7},{1,6},{2,1},{3,0},{4,3},{5,2},{6,5},{7,4},{8,15},{9,14},{10,... | collective-permute-start | bytes 1179656 | tf_op jit(solution)/shard_map/ppermute | solution.py:245
  35.0 31.4 %collective-permute-start.27 = (bf16[12,128,128]{2,1,0:T(8,128)(2,1)S(1)}, bf16[12,128,128]{2,1,0:T(8,128)(2,1)}, u32[]{:S(2)}, u32[]{:S(2)}) collective-permute-start(bf16[12,128,128]{2,1,0:T(8,128)(2,1)S(1)} %copy-done.8), channel_id=1, source_target_pairs={{0,1},{1,0},{2,3},{3,2},{4,5},{5,4},{6,7},{7,6},{8,9},{9,8},{10,11... | collective-permute-start | bytes 1179656 | tf_op jit(solution)/shard_map/ppermute | solution.py:245
  42.8 35.0 %collective-permute-start.7 = (bf16[16,128,128]{2,1,0:T(8,128)(2,1)S(1)}, bf16[16,128,128]{2,1,0:T(8,128)(2,1)S(1)}, u32[]{:S(2)}, u32[]{:S(2)}) collective-permute-start(bf16[16,128,128]{2,1,0:T(8,128)(2,1)S(1)} %pack_first.1), channel_id=1, source_target_pairs={{0,4},{1,5},{2,6},{3,7},{4,0},{5,1},{6,2},{7,3},{8,12},{9,13},{10,... | collective-permute-start | bytes 1572872 | tf_op jit(solution)/shard_map/ppermute | solution.py:245
  45.8 33.6 %collective-permute-start.8 = (bf16[16,128,128]{2,1,0:T(8,128)(2,1)}, bf16[16,128,128]{2,1,0:T(8,128)(2,1)}, u32[]{:S(2)}, u32[]{:S(2)}) collective-permute-start(bf16[16,128,128]{2,1,0:T(8,128)(2,1)} %get-tuple-element.50), channel_id=1, source_target_pairs={{0,5},{1,4},{2,7},{3,6},{4,1},{5,0},{6,3},{7,2},{8,13},{9,12},{10,... | collective-permute-start | bytes 1572872 | tf_op jit(solution)/shard_map/ppermute | solution.py:245
  51.8 33.2 %collective-permute-start.9 = (bf16[16,128,128]{2,1,0:T(8,128)(2,1)}, bf16[16,128,128]{2,1,0:T(8,128)(2,1)}, u32[]{:S(2)}, u32[]{:S(2)}) collective-permute-start(bf16[16,128,128]{2,1,0:T(8,128)(2,1)} %get-tuple-element.51), channel_id=1, source_target_pairs={{0,2},{1,3},{2,4},{3,5},{4,6},{5,7},{6,0},{7,1},{8,10},{9,11},{10,... | collective-permute-start | bytes 1572872 | tf_op jit(solution)/shard_map/ppermute | solution.py:245
  53.6 34.3 %collective-permute-start.10 = (bf16[16,128,128]{2,1,0:T(8,128)(2,1)}, bf16[16,128,128]{2,1,0:T(8,128)(2,1)}, u32[]{:S(2)}, u32[]{:S(2)}) collective-permute-start(bf16[16,128,128]{2,1,0:T(8,128)(2,1)} %get-tuple-element.52), channel_id=1, source_target_pairs={{0,6},{1,7},{2,0},{3,1},{4,2},{5,3},{6,4},{7,5},{8,14},{9,15},{10,... | collective-permute-start | bytes 1572872 | tf_op jit(solution)/shard_map/ppermute | solution.py:245
  66.4 30.5 %collective-permute-start.11 = (bf16[16,128,128]{2,1,0:T(8,128)(2,1)}, bf16[16,128,128]{2,1,0:T(8,128)(2,1)}, u32[]{:S(2)}, u32[]{:S(2)}) collective-permute-start(bf16[16,128,128]{2,1,0:T(8,128)(2,1)} %get-tuple-element.53), channel_id=1, source_target_pairs={{0,3},{1,2},{2,5},{3,4},{4,7},{5,6},{6,1},{7,0},{8,11},{9,10},{10,... | collective-permute-start | bytes 1572872 | tf_op jit(solution)/shard_map/ppermute | solution.py:245
  77.8 156.8 %collective-permute-start = (bf16[48,128,128]{2,1,0:T(8,128)(2,1)}, bf16[48,128,128]{2,1,0:T(8,128)(2,1)}, u32[]{:S(2)}, u32[]{:S(2)}) collective-permute-start(bf16[48,128,128]{2,1,0:T(8,128)(2,1)} %get-tuple-element.42), channel_id=1, source_target_pairs={{0,4},{1,5},{2,6},{3,7},{4,0},{5,1},{6,2},{7,3},{8,12},{9,13},{10,... | collective-permute-start | bytes 4718600 | tf_op jit(solution)/shard_map/ppermute | solution.py:245
  79.4 156.8 %collective-permute-start.1 = (bf16[48,128,128]{2,1,0:T(8,128)(2,1)}, bf16[48,128,128]{2,1,0:T(8,128)(2,1)}, u32[]{:S(2)}, u32[]{:S(2)}) collective-permute-start(bf16[48,128,128]{2,1,0:T(8,128)(2,1)} %get-tuple-element.43), channel_id=1, source_target_pairs={{0,5},{1,4},{2,7},{3,6},{4,1},{5,0},{6,3},{7,2},{8,13},{9,12},{10,... | collective-permute-start | bytes 4718600 | tf_op jit(solution)/shard_map/ppermute | solution.py:245
  85.0 151.9 %collective-permute-start.28 = (bf16[48,128,128]{2,1,0:T(8,128)(2,1)}, bf16[48,128,128]{2,1,0:T(8,128)(2,1)}, u32[]{:S(2)}, u32[]{:S(2)}) collective-permute-start(bf16[48,128,128]{2,1,0:T(8,128)(2,1)} %get-tuple-element.73), channel_id=1, source_target_pairs={{0,4},{1,5},{2,6},{3,7},{4,0},{5,1},{6,2},{7,3},{8,12},{9,13},{10,... | collective-permute-start | bytes 4718600 | tf_op jit(solution)/shard_map/ppermute | solution.py:245
  88.0 151.2 %collective-permute-start.29 = (bf16[48,128,128]{2,1,0:T(8,128)(2,1)}, bf16[48,128,128]{2,1,0:T(8,128)(2,1)}, u32[]{:S(2)}, u32[]{:S(2)}) collective-permute-start(bf16[48,128,128]{2,1,0:T(8,128)(2,1)} %get-tuple-element.74), channel_id=1, source_target_pairs={{0,5},{1,4},{2,7},{3,6},{4,1},{5,0},{6,3},{7,2},{8,13},{9,12},{10,... | collective-permute-start | bytes 4718600 | tf_op jit(solution)/shard_map/ppermute | solution.py:245
  96.9 134.4 %collective-permute-start.12 = (bf16[16,128,128]{2,1,0:T(8,128)(2,1)}, bf16[16,128,128]{2,1,0:T(8,128)(2,1)S(1)}, u32[]{:S(2)}, u32[]{:S(2)}) collective-permute-start(bf16[16,128,128]{2,1,0:T(8,128)(2,1)} %get-tuple-element.54), channel_id=1, source_target_pairs={{0,7},{1,6},{2,1},{3,0},{4,3},{5,2},{6,5},{7,4},{8,15},{9,14},{10,... | collective-permute-start | bytes 1572872 | tf_op jit(solution)/shard_map/ppermute | solution.py:245
  233.6 37.3 %collective-permute-start.30 = (bf16[48,128,128]{2,1,0:T(8,128)(2,1)}, bf16[48,128,128]{2,1,0:T(8,128)(2,1)}, u32[]{:S(2)}, u32[]{:S(2)}) collective-permute-start(bf16[48,128,128]{2,1,0:T(8,128)(2,1)} %get-tuple-element.75), channel_id=1, source_target_pairs={{0,2},{1,3},{2,4},{3,5},{4,6},{5,7},{6,0},{7,1},{8,10},{9,11},{10,... | collective-permute-start | bytes 4718600 | tf_op jit(solution)/shard_map/ppermute | solution.py:245
  234.7 36.2 %collective-permute-start.31 = (bf16[48,128,128]{2,1,0:T(8,128)(2,1)}, bf16[48,128,128]{2,1,0:T(8,128)(2,1)}, u32[]{:S(2)}, u32[]{:S(2)}) collective-permute-start(bf16[48,128,128]{2,1,0:T(8,128)(2,1)} %get-tuple-element.76), channel_id=1, source_target_pairs={{0,6},{1,7},{2,0},{3,1},{4,2},{5,3},{6,4},{7,5},{8,14},{9,15},{10,... | collective-permute-start | bytes 4718600 | tf_op jit(solution)/shard_map/ppermute | solution.py:245
  236.2 69.3 %collective-permute-start.32 = (bf16[48,128,128]{2,1,0:T(8,128)(2,1)}, bf16[48,128,128]{2,1,0:T(8,128)(2,1)}, u32[]{:S(2)}, u32[]{:S(2)}) collective-permute-start(bf16[48,128,128]{2,1,0:T(8,128)(2,1)} %get-tuple-element.77), channel_id=1, source_target_pairs={{0,3},{1,2},{2,5},{3,4},{4,7},{5,6},{6,1},{7,0},{8,11},{9,10},{10,... | collective-permute-start | bytes 4718600 | tf_op jit(solution)/shard_map/ppermute | solution.py:245
  237.0 69.3 %collective-permute-start.33 = (bf16[48,128,128]{2,1,0:T(8,128)(2,1)}, bf16[48,128,128]{2,1,0:T(8,128)(2,1)}, u32[]{:S(2)}, u32[]{:S(2)}) collective-permute-start(bf16[48,128,128]{2,1,0:T(8,128)(2,1)} %get-tuple-element.78), channel_id=1, source_target_pairs={{0,7},{1,6},{2,1},{3,0},{4,3},{5,2},{6,5},{7,4},{8,15},{9,14},{10,... | collective-permute-start | bytes 4718600 | tf_op jit(solution)/shard_map/ppermute | solution.py:245
  239.2 69.3 %collective-permute-start.34 = (bf16[48,128,128]{2,1,0:T(8,128)(2,1)}, bf16[48,128,128]{2,1,0:T(8,128)(2,1)}, u32[]{:S(2)}, u32[]{:S(2)}) collective-permute-start(bf16[48,128,128]{2,1,0:T(8,128)(2,1)} %get-tuple-element.79), channel_id=1, source_target_pairs={{0,1},{1,0},{2,3},{3,2},{4,5},{5,4},{6,7},{7,6},{8,9},{9,8},{10,11... | collective-permute-start | bytes 4718600 | tf_op jit(solution)/shard_map/ppermute | solution.py:245
  270.9 89.7 %collective-permute-start.2 = (bf16[48,128,128]{2,1,0:T(8,128)(2,1)}, bf16[48,128,128]{2,1,0:T(8,128)(2,1)}, u32[]{:S(2)}, u32[]{:S(2)}) collective-permute-start(bf16[48,128,128]{2,1,0:T(8,128)(2,1)} %get-tuple-element.44), channel_id=1, source_target_pairs={{0,2},{1,3},{2,4},{3,5},{4,6},{5,7},{6,0},{7,1},{8,10},{9,11},{10,... | collective-permute-start | bytes 4718600 | tf_op jit(solution)/shard_map/ppermute | solution.py:245
  270.9 89.8 %collective-permute-start.3 = (bf16[48,128,128]{2,1,0:T(8,128)(2,1)}, bf16[48,128,128]{2,1,0:T(8,128)(2,1)}, u32[]{:S(2)}, u32[]{:S(2)}) collective-permute-start(bf16[48,128,128]{2,1,0:T(8,128)(2,1)} %get-tuple-element.45), channel_id=1, source_target_pairs={{0,6},{1,7},{2,0},{3,1},{4,2},{5,3},{6,4},{7,5},{8,14},{9,15},{10,... | collective-permute-start | bytes 4718600 | tf_op jit(solution)/shard_map/ppermute | solution.py:245
  305.5 67.4 %collective-permute-start.4 = (bf16[48,128,128]{2,1,0:T(8,128)(2,1)}, bf16[48,128,128]{2,1,0:T(8,128)(2,1)}, u32[]{:S(2)}, u32[]{:S(2)}) collective-permute-start(bf16[48,128,128]{2,1,0:T(8,128)(2,1)} %get-tuple-element.46), channel_id=1, source_target_pairs={{0,3},{1,2},{2,5},{3,4},{4,7},{5,6},{6,1},{7,0},{8,11},{9,10},{10,... | collective-permute-start | bytes 4718600 | tf_op jit(solution)/shard_map/ppermute | solution.py:245
  306.2 67.3 %collective-permute-start.5 = (bf16[48,128,128]{2,1,0:T(8,128)(2,1)}, bf16[48,128,128]{2,1,0:T(8,128)(2,1)}, u32[]{:S(2)}, u32[]{:S(2)}) collective-permute-start(bf16[48,128,128]{2,1,0:T(8,128)(2,1)} %get-tuple-element.47), channel_id=1, source_target_pairs={{0,7},{1,6},{2,1},{3,0},{4,3},{5,2},{6,5},{7,4},{8,15},{9,14},{10,... | collective-permute-start | bytes 4718600 | tf_op jit(solution)/shard_map/ppermute | solution.py:245
  308.5 67.4 %collective-permute-start.6 = (bf16[48,128,128]{2,1,0:T(8,128)(2,1)}, bf16[48,128,128]{2,1,0:T(8,128)(2,1)}, u32[]{:S(2)}, u32[]{:S(2)}) collective-permute-start(bf16[48,128,128]{2,1,0:T(8,128)(2,1)} %get-tuple-element.48), channel_id=1, source_target_pairs={{0,1},{1,0},{2,3},{3,2},{4,5},{5,4},{6,7},{7,6},{8,9},{9,8},{10,11... | collective-permute-start | bytes 4718600 | tf_op jit(solution)/shard_map/ppermute | solution.py:245
  360.6 29.5 %collective-permute-start.16 = (bf16[4,128,128]{2,1,0:T(8,128)(2,1)}, bf16[4,128,128]{2,1,0:T(8,128)(2,1)S(1)}, u32[]{:S(2)}, u32[]{:S(2)}) collective-permute-start(bf16[4,128,128]{2,1,0:T(8,128)(2,1)} %get-tuple-element.59), channel_id=1, source_target_pairs={{0,2},{1,3},{2,4},{3,5},{4,6},{5,7},{6,0},{7,1},{8,10},{9,11},{10,... | collective-permute-start | bytes 393224 | tf_op jit(solution)/shard_map/ppermute | solution.py:245
  360.7 29.4 %collective-permute-start.17 = (bf16[4,128,128]{2,1,0:T(8,128)(2,1)}, bf16[4,128,128]{2,1,0:T(8,128)(2,1)S(1)}, u32[]{:S(2)}, u32[]{:S(2)}) collective-permute-start(bf16[4,128,128]{2,1,0:T(8,128)(2,1)} %get-tuple-element.60), channel_id=1, source_target_pairs={{0,6},{1,7},{2,0},{3,1},{4,2},{5,3},{6,4},{7,5},{8,14},{9,15},{10,... | collective-permute-start | bytes 393224 | tf_op jit(solution)/shard_map/ppermute | solution.py:245
  (24 other events, 692.1 us)

commit v6 on v5

--- a/solution.py
+++ b/solution.py
@@ -9,8 +9,8 @@
 
 
 MASK_VALUE = -1e30
-CHUNKS = ((0, 0, 16, 16), (0, 16, 48, 16), (1, 12, 48, 12), (1, 0, 12, 6), (1, 60, 4, 4))
-ROOM = pltpu.CompilerParams(vmem_limit_bytes=65_520_000)
+CHUNKS = ((0, 0, 16, 16), (0, 16, 48, 24), (1, 0, 50, 25), (1, 50, 12, 6), (1, 62, 2, 2))
+ROOM = pltpu.CompilerParams(vmem_limit_bytes=66_000_000)
 
 
 def offsets(n):
@@ -185,7 +185,7 @@
         out_shape=jax.ShapeDtypeStruct((batch, seq_local, n, head_dim), xs[0].dtype),
         in_specs=[pl.BlockSpec((block, seq_local, head_dim), lambda i: (i, 0, 0))] * n
         + ([] if whole is None else [pl.BlockSpec(memory_space=pl.ANY)]),
-        out_specs=pl.BlockSpec((block, seq_local, n, head_dim), lambda i: (first // block + i, 0, 0, 0)),
+        out_specs=pl.BlockSpec(tuple(map(pl.Element, (block, seq_local, n, head_dim))), lambda i: (first + i * block, 0, 0, 0)),
         scratch_shapes=[pltpu.VMEM((2, n, seq_local, head_dim), xs[0].dtype)],
         input_output_aliases={} if whole is None else {n: 0},
         compiler_params=ROOM,

time: 392 us -> 416 us (1.061)
  starting transfers between devices: 45.2 us -> 68.7 us
    ppermute x35, starting transfers between devices: 45.2 us -> 68.7 us  [local_step(): slabs[i] = lax.ppermute(slabs[i], 'tp', pairs(n, *peer))]
  transfers between devices with their start and end apart: 35 -> 35, of which waited for: 14 -> 7; matrix products, arithmetic and copies ran while one was open for 0% -> 0% of each run, Pallas kernels for 26% -> 24%
where the time goes in v6:
time: 416 us
  waiting for transfers between devices  239 us (57%)
  Pallas kernels  106 us (25%)
  starting transfers between devices  68.7 us (17%)
    ppermute x35, waiting for transfers between devices, local_step(): slabs[i] = lax.ppermute(slabs[i], 'tp', pairs(n, *peer))  239 us
    ppermute x35, starting transfers between devices, local_step(): slabs[i] = lax.ppermute(slabs[i], 'tp', pairs(n, *peer))  68.7 us
    pallas_call x5, Pallas kernels, pack(): pl.pallas_call(functools.partial(pack_kernel, n, peers, first, pieces), o...  39.4 us
    pallas_call x4, Pallas kernels, relayout(): pl.pallas_call(functools.partial(relayout_kernel, n, sources), grid=(coun...  35.3 us
    pallas_call x1, Pallas kernels, local_step(): attn = attend(lens, query, k_cache, v_cache, k_new, v_new)  28.7 us
  transfers between devices with their start and end apart: 35, of which 7 were waited for; matrix products, arithmetic and copies ran while one was open for 0% of the time, Pallas kernels for 24%

profile of v6, /device:TPU:113, one launch (start us, length us, event | category | flops | bytes accessed | tf_op | source)
XLA Modules:
  0.0 415.6 jit_solution(3664539930125915510)
XLA Ops:
  0.6 5.9 %shard_map.90 = (bf16[12,128,128]{2,1,0:T(8,128)(2,1)}, bf16[12,128,128]{2,1,0:T(8,128)(2,1)}, bf16[12,128,128]{2,1,0:T(8,128)(2,1)}, bf16[12,128,128]{2,1,0:T(8...) custom-call(s32[64]{0:T(128)} %lens_ref.13, ...), custom_call_target="tpu_custom_call" | custom-call | flops 384000000 | bytes 6291456 | tf_op jit(solution)/shard_map/pallas_call | solution.py:129
  6.5 4.0 collective-permute-start.21
  10.8 4.6 %shard_map.89 = (bf16[2,128,128]{2,1,0:T(8,128)(2,1)}, bf16[2,128,128]{2,1,0:T(8,128)(2,1)}, bf16[2,128,128]{2,1,0:T(8,128)(2,1)}, bf16[2,128,128]{2,1,0:T(8,128...) custom-call(s32[64]{0:T(128)} %lens_ref.13, ...), custom_call_target="tpu_custom_call" | custom-call | flops 64000000 | bytes 1048576 | tf_op jit(solution)/shard_map/pallas_call | solution.py:129
  15.5 3.2 collective-permute-start.14
  20.0 9.7 %collective-permute-done.14.refs_0_ = bf16[2,128,128]{2,1,0:T(8,128)(2,1)S(1)} collective-permute-done((bf16[2,128,128]{2,1,0:T(8,128)(2,1)}, bf16[2,128,128]{2,1,0:T(8,128)(2,1)S(1)}, u32[]{:S(2)}, u32[]{:S(2)}) %collective-permute-start.14) | collective-permute-done | bytes 65568 | tf_op jit(solution)/shard_map/ppermute | solution.py:245
  40.1 2.9 collective-permute-start.7
  43.0 5.7 %shard_map.86 = (bf16[16,128,128]{2,1,0:T(8,128)(2,1)}, bf16[16,128,128]{2,1,0:T(8,128)(2,1)}, bf16[16,128,128]{2,1,0:T(8,128)(2,1)}, bf16[16,128,128]{2,1,0:T(8...) custom-call(s32[64]{0:T(128)} %lens_ref.13, ...), custom_call_target="tpu_custom_call" | custom-call | flops 448000000 | bytes 7340032 | tf_op jit(solution)/shard_map/pallas_call | solution.py:129
  52.2 21.4 %collective-permute-start.10 = (bf16[16,128,128]{2,1,0:T(8,128)(2,1)}, bf16[16,128,128]{2,1,0:T(8,128)(2,1)}, u32[]{:S(2)}, u32[]{:S(2)}) collective-permute-start(bf16[16,128,128]{2,1,0:T(8,128)(2,1)} %get-tuple-element.52), channel_id=1, source_target_pairs={{0,6},{1,7},{2,0},{3,1},{4,2},{5,3},{6,4},{7,5},{8,14},{9,15},{10,... | collective-permute-start | bytes 1572872 | tf_op jit(solution)/shard_map/ppermute | solution.py:245
  73.6 11.2 %shard_map.85 = (bf16[48,128,128]{2,1,0:T(8,128)(2,1)}, bf16[48,128,128]{2,1,0:T(8,128)(2,1)}, bf16[48,128,128]{2,1,0:T(8,128)(2,1)}, bf16[48,128,128]{2,1,0:T(8...) custom-call(s32[64]{0:T(128)} %lens_ref.13, ...), custom_call_target="tpu_custom_call" | custom-call | flops 1536000000 | bytes 25165824 | tf_op jit(solution)/shard_map/pallas_call | solution.py:129
  88.4 2.7 collective-permute-start.3
  91.1 2.9 collective-permute-done.11.refs_4_
  94.0 105.0 %collective-permute-done.12.refs_5_ = bf16[16,128,128]{2,1,0:T(8,128)(2,1)S(1)} collective-permute-done((bf16[16,128,128]{2,1,0:T(8,128)(2,1)}, bf16[16,128,128]{2,1,0:T(8,128)(2,1)S(1)}, u32[]{:S(2)}, u32[]{:S(2)}) %collective-permute-start.12) | collective-permute-done | bytes 524320 | tf_op jit(solution)/shard_map/ppermute | solution.py:245
  199.0 11.9 %shard_map.91 = (bf16[50,128,128]{2,1,0:T(8,128)(2,1)}, bf16[50,128,128]{2,1,0:T(8,128)(2,1)}, bf16[50,128,128]{2,1,0:T(8,128)(2,1)}, bf16[50,128,128]{2,1,0:T(8...) custom-call(s32[64]{0:T(128)} %lens_ref.13, ...), custom_call_target="tpu_custom_call" | custom-call | flops 1600000000 | bytes 26214400 | tf_op jit(solution)/shard_map/pallas_call | solution.py:129
  217.4 102.1 %collective-permute-done.4.refs_4_ = bf16[48,128,128]{2,1,0:T(8,128)(2,1)} collective-permute-done((bf16[48,128,128]{2,1,0:T(8,128)(2,1)}, bf16[48,128,128]{2,1,0:T(8,128)(2,1)}, u32[]{:S(2)}, u32[]{:S(2)}) %collective-permute-start.4) | collective-permute-done | bytes 1572896 | tf_op jit(solution)/shard_map/ppermute | solution.py:245
  319.5 2.7 collective-permute-start.31
  322.2 3.0 collective-permute-start.33
  326.1 28.7 %attend.1 = bf16[64,4,128]{2,1,0:T(4,128)(2,1)} custom-call(s32[64]{0:T(128)} %lens_ref.13, bf16[64,4,128]{2,1,0:T(4,128)(2,1)} %q_ref.1, bf16[64,1024,128]{2,1,0:T(8,128)(2,1)} %bitcast.7, bf16[64,1024,128]{2,1,0:T(8,128)(2,1)} %bitcast.11, bf16[64,128]{1,0:T(8,128)(2,1)} %bitcast.15, bf16[64,128]{1,0:T(8,128)(2,1)} %bitcast.19), custom_call_target="tpu_custom_call" | custom-call | flops 99999997952 | bytes 33554432 | tf_op jit(solution)/shard_map/attend/pallas_call | solution.py:263
  354.8 6.3 %shard_map.87.refs_8_ = bf16[64,128,8,128]{3,2,1,0:T(8,128)(2,1)} custom-call(bf16[16,128,128]{2,1,0:T(8,128)(2,1)} %collective-permute-done.7.refs_0_, bf16[16,128,128]{2,1,0:T(8,128)(2,1)} %collective-permute-done.8.refs_1_, bf16[16,128,128]{2,1,0:T(8,128)(2,1)} %collective-permute-done.9.refs_2_, bf16[16,128,128]{2,1,0:T(8,128)(2,1)} %collective-permute-done.10.refs_3_, ...), custom_call_target="tpu_custom_call" | custom-call | flops 640000000 | bytes 8388608 | tf_op jit(solution)/shard_map/pallas_call | solution.py:182
  361.1 12.1 %shard_map.88 = bf16[64,128,8,128]{3,2,1,0:T(8,128)(2,1)} custom-call(bf16[48,128,128]{2,1,0:T(8,128)(2,1)} %collective-permute-done.refs_0_, bf16[48,128,128]{2,1,0:T(8,128)(2,1)} %collective-permute-done.1.refs_1_, bf16[48,128,128]{2,1,0:T(8,128)(2,1)} %collective-permute-done.2.refs_2_, ...), custom_call_target="tpu_custom_call", output_to_operand_aliasing={{}: (8, {})} | custom-call | flops 1920000000 | bytes 25165824 | tf_op jit(solution)/shard_map/pallas_call | solution.py:182
  373.4 2.6 collective-permute-start.17
  376.0 18.4 %collective-permute-done.32.refs_4_ = bf16[50,128,128]{2,1,0:T(8,128)(2,1)} collective-permute-done((bf16[50,128,128]{2,1,0:T(8,128)(2,1)}, bf16[50,128,128]{2,1,0:T(8,128)(2,1)}, u32[]{:S(2)}, u32[]{:S(2)}) %collective-permute-start.32) | collective-permute-done | bytes 1638432 | tf_op jit(solution)/shard_map/ppermute | solution.py:245
  394.4 2.9 collective-permute-start.19
  397.4 12.6 %shard_map.92.refs_8_ = bf16[64,128,8,128]{3,2,1,0:T(8,128)(2,1)} custom-call(bf16[50,128,128]{2,1,0:T(8,128)(2,1)} %collective-permute-done.28.refs_0_, bf16[50,128,128]{2,1,0:T(8,128)(2,1)} %collective-permute-done.29.refs_1_, bf16[50,128,128]{2,1,0:T(8,128)(2,1)} %collective-permute-done.30.refs_2_, ...), custom_call_target="tpu_custom_call" | custom-call | flops 2000000000 | bytes 26214400 | tf_op jit(solution)/shard_map/pallas_call | solution.py:182
  410.1 4.3 %shard_map.93.refs_8_ = bf16[64,128,8,128]{3,2,1,0:T(8,128)(2,1)} custom-call(bf16[12,128,128]{2,1,0:T(8,128)(2,1)} %copy-done.6, bf16[12,128,128]{2,1,0:T(8,128)(2,1)} %copy-done.7, bf16[12,128,128]{2,1,0:T(8,128)(2,1)} %collective-permute-done.23.refs_2_, bf16[12,128,128]{2,1,0:T(8,128)(2,1)} %collective-permute-done.24.refs_3_, ...), custom_call_target="tpu_custom_call", output_to_operand_aliasing={{}: (8, {})} | custom-call | flops 480000000 | bytes 6291456 | tf_op jit(solution)/shard_map/pallas_call | solution.py:182
  (84 shorter events, 27.7 us)
Async XLA Ops:
  6.5 27.6 %collective-permute-start.21 = (bf16[12,128,128]{2,1,0:T(8,128)(2,1)}, bf16[12,128,128]{2,1,0:T(8,128)(2,1)S(1)}, u32[]{:S(2)}, u32[]{:S(2)}) collective-permute-start(bf16[12,128,128]{2,1,0:T(8,128)(2,1)} %get-tuple-element.65), channel_id=1, source_target_pairs={{0,4},{1,5},{2,6},{3,7},{4,0},{5,1},{6,2},{7,3},{8,12},{9,13},{10,... | collective-permute-start | bytes 1179656 | tf_op jit(solution)/shard_map/ppermute | solution.py:245
  10.5 25.8 %collective-permute-start.22 = (bf16[12,128,128]{2,1,0:T(8,128)(2,1)}, bf16[12,128,128]{2,1,0:T(8,128)(2,1)S(1)}, u32[]{:S(2)}, u32[]{:S(2)}) collective-permute-start(bf16[12,128,128]{2,1,0:T(8,128)(2,1)} %get-tuple-element.66), channel_id=1, source_target_pairs={{0,5},{1,4},{2,7},{3,6},{4,1},{5,0},{6,3},{7,2},{8,13},{9,12},{10,... | collective-permute-start | bytes 1179656 | tf_op jit(solution)/shard_map/ppermute | solution.py:245
  36.3 37.4 %collective-permute-start.27 = (bf16[12,128,128]{2,1,0:T(8,128)(2,1)}, bf16[12,128,128]{2,1,0:T(8,128)(2,1)}, u32[]{:S(2)}, u32[]{:S(2)}) collective-permute-start(bf16[12,128,128]{2,1,0:T(8,128)(2,1)} %get-tuple-element.71), channel_id=1, source_target_pairs={{0,1},{1,0},{2,3},{3,2},{4,5},{5,4},{6,7},{7,6},{8,9},{9,8},{10,11... | collective-permute-start | bytes 1179656 | tf_op jit(solution)/shard_map/ppermute | solution.py:245
  40.1 44.8 %collective-permute-start.7 = (bf16[16,128,128]{2,1,0:T(8,128)(2,1)S(1)}, bf16[16,128,128]{2,1,0:T(8,128)(2,1)}, u32[]{:S(2)}, u32[]{:S(2)}) collective-permute-start(bf16[16,128,128]{2,1,0:T(8,128)(2,1)S(1)} %pack_first.1), channel_id=1, source_target_pairs={{0,4},{1,5},{2,6},{3,7},{4,0},{5,1},{6,2},{7,3},{8,12},{9,13},{10,... | collective-permute-start | bytes 1572872 | tf_op jit(solution)/shard_map/ppermute | solution.py:245
  48.8 36.2 %collective-permute-start.8 = (bf16[16,128,128]{2,1,0:T(8,128)(2,1)}, bf16[16,128,128]{2,1,0:T(8,128)(2,1)}, u32[]{:S(2)}, u32[]{:S(2)}) collective-permute-start(bf16[16,128,128]{2,1,0:T(8,128)(2,1)} %get-tuple-element.50), channel_id=1, source_target_pairs={{0,5},{1,4},{2,7},{3,6},{4,1},{5,0},{6,3},{7,2},{8,13},{9,12},{10,... | collective-permute-start | bytes 1572872 | tf_op jit(solution)/shard_map/ppermute | solution.py:245
  49.6 36.7 %collective-permute-start.9 = (bf16[16,128,128]{2,1,0:T(8,128)(2,1)}, bf16[16,128,128]{2,1,0:T(8,128)(2,1)}, u32[]{:S(2)}, u32[]{:S(2)}) collective-permute-start(bf16[16,128,128]{2,1,0:T(8,128)(2,1)} %get-tuple-element.51), channel_id=1, source_target_pairs={{0,2},{1,3},{2,4},{3,5},{4,6},{5,7},{6,0},{7,1},{8,10},{9,11},{10,... | collective-permute-start | bytes 1572872 | tf_op jit(solution)/shard_map/ppermute | solution.py:245
  52.2 36.2 %collective-permute-start.10 = (bf16[16,128,128]{2,1,0:T(8,128)(2,1)}, bf16[16,128,128]{2,1,0:T(8,128)(2,1)}, u32[]{:S(2)}, u32[]{:S(2)}) collective-permute-start(bf16[16,128,128]{2,1,0:T(8,128)(2,1)} %get-tuple-element.52), channel_id=1, source_target_pairs={{0,6},{1,7},{2,0},{3,1},{4,2},{5,3},{6,4},{7,5},{8,14},{9,15},{10,... | collective-permute-start | bytes 1572872 | tf_op jit(solution)/shard_map/ppermute | solution.py:245
  84.9 126.4 %collective-permute-start = (bf16[48,128,128]{2,1,0:T(8,128)(2,1)}, bf16[48,128,128]{2,1,0:T(8,128)(2,1)}, u32[]{:S(2)}, u32[]{:S(2)}) collective-permute-start(bf16[48,128,128]{2,1,0:T(8,128)(2,1)} %get-tuple-element.42), channel_id=1, source_target_pairs={{0,4},{1,5},{2,6},{3,7},{4,0},{5,1},{6,2},{7,3},{8,12},{9,13},{10,... | collective-permute-start | bytes 4718600 | tf_op jit(solution)/shard_map/ppermute | solution.py:245
  85.0 128.8 %collective-permute-start.1 = (bf16[48,128,128]{2,1,0:T(8,128)(2,1)}, bf16[48,128,128]{2,1,0:T(8,128)(2,1)}, u32[]{:S(2)}, u32[]{:S(2)}) collective-permute-start(bf16[48,128,128]{2,1,0:T(8,128)(2,1)} %get-tuple-element.43), channel_id=1, source_target_pairs={{0,5},{1,4},{2,7},{3,6},{4,1},{5,0},{6,3},{7,2},{8,13},{9,12},{10,... | collective-permute-start | bytes 4718600 | tf_op jit(solution)/shard_map/ppermute | solution.py:245
  86.3 128.3 %collective-permute-start.2 = (bf16[48,128,128]{2,1,0:T(8,128)(2,1)}, bf16[48,128,128]{2,1,0:T(8,128)(2,1)}, u32[]{:S(2)}, u32[]{:S(2)}) collective-permute-start(bf16[48,128,128]{2,1,0:T(8,128)(2,1)} %get-tuple-element.44), channel_id=1, source_target_pairs={{0,2},{1,3},{2,4},{3,5},{4,6},{5,7},{6,0},{7,1},{8,10},{9,11},{10,... | collective-permute-start | bytes 4718600 | tf_op jit(solution)/shard_map/ppermute | solution.py:245
  88.4 128.4 %collective-permute-start.3 = (bf16[48,128,128]{2,1,0:T(8,128)(2,1)}, bf16[48,128,128]{2,1,0:T(8,128)(2,1)}, u32[]{:S(2)}, u32[]{:S(2)}) collective-permute-start(bf16[48,128,128]{2,1,0:T(8,128)(2,1)} %get-tuple-element.45), channel_id=1, source_target_pairs={{0,6},{1,7},{2,0},{3,1},{4,2},{5,3},{6,4},{7,5},{8,14},{9,15},{10,... | collective-permute-start | bytes 4718600 | tf_op jit(solution)/shard_map/ppermute | solution.py:245
  94.0 105.0 %collective-permute-start.12 = (bf16[16,128,128]{2,1,0:T(8,128)(2,1)}, bf16[16,128,128]{2,1,0:T(8,128)(2,1)S(1)}, u32[]{:S(2)}, u32[]{:S(2)}) collective-permute-start(bf16[16,128,128]{2,1,0:T(8,128)(2,1)} %get-tuple-element.54), channel_id=1, source_target_pairs={{0,7},{1,6},{2,1},{3,0},{4,3},{5,2},{6,5},{7,4},{8,15},{9,14},{10,... | collective-permute-start | bytes 1572872 | tf_op jit(solution)/shard_map/ppermute | solution.py:245
  211.0 111.2 %collective-permute-start.28 = (bf16[50,128,128]{2,1,0:T(8,128)(2,1)}, bf16[50,128,128]{2,1,0:T(8,128)(2,1)}, u32[]{:S(2)}, u32[]{:S(2)}) collective-permute-start(bf16[50,128,128]{2,1,0:T(8,128)(2,1)} %get-tuple-element.73), channel_id=1, source_target_pairs={{0,4},{1,5},{2,6},{3,7},{4,0},{5,1},{6,2},{7,3},{8,12},{9,13},{10,... | collective-permute-start | bytes 4915208 | tf_op jit(solution)/shard_map/ppermute | solution.py:245
  211.3 113.9 %collective-permute-start.29 = (bf16[50,128,128]{2,1,0:T(8,128)(2,1)}, bf16[50,128,128]{2,1,0:T(8,128)(2,1)}, u32[]{:S(2)}, u32[]{:S(2)}) collective-permute-start(bf16[50,128,128]{2,1,0:T(8,128)(2,1)} %get-tuple-element.74), channel_id=1, source_target_pairs={{0,5},{1,4},{2,7},{3,6},{4,1},{5,0},{6,3},{7,2},{8,13},{9,12},{10,... | collective-permute-start | bytes 4915208 | tf_op jit(solution)/shard_map/ppermute | solution.py:245
  213.8 105.7 %collective-permute-start.4 = (bf16[48,128,128]{2,1,0:T(8,128)(2,1)}, bf16[48,128,128]{2,1,0:T(8,128)(2,1)}, u32[]{:S(2)}, u32[]{:S(2)}) collective-permute-start(bf16[48,128,128]{2,1,0:T(8,128)(2,1)} %get-tuple-element.46), channel_id=1, source_target_pairs={{0,3},{1,2},{2,5},{3,4},{4,7},{5,6},{6,1},{7,0},{8,11},{9,10},{10,... | collective-permute-start | bytes 4718600 | tf_op jit(solution)/shard_map/ppermute | solution.py:245
  214.6 104.9 %collective-permute-start.5 = (bf16[48,128,128]{2,1,0:T(8,128)(2,1)}, bf16[48,128,128]{2,1,0:T(8,128)(2,1)}, u32[]{:S(2)}, u32[]{:S(2)}) collective-permute-start(bf16[48,128,128]{2,1,0:T(8,128)(2,1)} %get-tuple-element.47), channel_id=1, source_target_pairs={{0,7},{1,6},{2,1},{3,0},{4,3},{5,2},{6,5},{7,4},{8,15},{9,14},{10,... | collective-permute-start | bytes 4718600 | tf_op jit(solution)/shard_map/ppermute | solution.py:245
  216.8 105.4 %collective-permute-start.6 = (bf16[48,128,128]{2,1,0:T(8,128)(2,1)}, bf16[48,128,128]{2,1,0:T(8,128)(2,1)}, u32[]{:S(2)}, u32[]{:S(2)}) collective-permute-start(bf16[48,128,128]{2,1,0:T(8,128)(2,1)} %get-tuple-element.48), channel_id=1, source_target_pairs={{0,1},{1,0},{2,3},{3,2},{4,5},{5,4},{6,7},{7,6},{8,9},{9,8},{10,11... | collective-permute-start | bytes 4718600 | tf_op jit(solution)/shard_map/ppermute | solution.py:245
  319.5 53.7 %collective-permute-start.30 = (bf16[50,128,128]{2,1,0:T(8,128)(2,1)}, bf16[50,128,128]{2,1,0:T(8,128)(2,1)}, u32[]{:S(2)}, u32[]{:S(2)}) collective-permute-start(bf16[50,128,128]{2,1,0:T(8,128)(2,1)} %get-tuple-element.75), channel_id=1, source_target_pairs={{0,2},{1,3},{2,4},{3,5},{4,6},{5,7},{6,0},{7,1},{8,10},{9,11},{10,... | collective-permute-start | bytes 4915208 | tf_op jit(solution)/shard_map/ppermute | solution.py:245
  319.5 53.8 %collective-permute-start.31 = (bf16[50,128,128]{2,1,0:T(8,128)(2,1)}, bf16[50,128,128]{2,1,0:T(8,128)(2,1)}, u32[]{:S(2)}, u32[]{:S(2)}) collective-permute-start(bf16[50,128,128]{2,1,0:T(8,128)(2,1)} %get-tuple-element.76), channel_id=1, source_target_pairs={{0,6},{1,7},{2,0},{3,1},{4,2},{5,3},{6,4},{7,5},{8,14},{9,15},{10,... | collective-permute-start | bytes 4915208 | tf_op jit(solution)/shard_map/ppermute | solution.py:245
  322.2 72.2 %collective-permute-start.32 = (bf16[50,128,128]{2,1,0:T(8,128)(2,1)}, bf16[50,128,128]{2,1,0:T(8,128)(2,1)}, u32[]{:S(2)}, u32[]{:S(2)}) collective-permute-start(bf16[50,128,128]{2,1,0:T(8,128)(2,1)} %get-tuple-element.77), channel_id=1, source_target_pairs={{0,3},{1,2},{2,5},{3,4},{4,7},{5,6},{6,1},{7,0},{8,11},{9,10},{10,... | collective-permute-start | bytes 4915208 | tf_op jit(solution)/shard_map/ppermute | solution.py:245
  322.2 72.2 %collective-permute-start.33 = (bf16[50,128,128]{2,1,0:T(8,128)(2,1)}, bf16[50,128,128]{2,1,0:T(8,128)(2,1)}, u32[]{:S(2)}, u32[]{:S(2)}) collective-permute-start(bf16[50,128,128]{2,1,0:T(8,128)(2,1)} %get-tuple-element.78), channel_id=1, source_target_pairs={{0,7},{1,6},{2,1},{3,0},{4,3},{5,2},{6,5},{7,4},{8,15},{9,14},{10,... | collective-permute-start | bytes 4915208 | tf_op jit(solution)/shard_map/ppermute | solution.py:245
  325.1 72.2 %collective-permute-start.34 = (bf16[50,128,128]{2,1,0:T(8,128)(2,1)}, bf16[50,128,128]{2,1,0:T(8,128)(2,1)}, u32[]{:S(2)}, u32[]{:S(2)}) collective-permute-start(bf16[50,128,128]{2,1,0:T(8,128)(2,1)} %get-tuple-element.79), channel_id=1, source_target_pairs={{0,1},{1,0},{2,3},{3,2},{4,5},{5,4},{6,7},{7,6},{8,9},{9,8},{10,11... | collective-permute-start | bytes 4915208 | tf_op jit(solution)/shard_map/ppermute | solution.py:245
  373.2 41.1 %collective-permute-start.16 = (bf16[2,128,128]{2,1,0:T(8,128)(2,1)S(1)}, bf16[2,128,128]{2,1,0:T(8,128)(2,1)S(1)}, u32[]{:S(2)}, u32[]{:S(2)}) collective-permute-start(bf16[2,128,128]{2,1,0:T(8,128)(2,1)S(1)} %copy-done.12), channel_id=1, source_target_pairs={{0,2},{1,3},{2,4},{3,5},{4,6},{5,7},{6,0},{7,1},{8,10},{9,11},{10,... | collective-permute-start | bytes 196616 | tf_op jit(solution)/shard_map/ppermute | solution.py:245
  373.4 41.0 %collective-permute-start.17 = (bf16[2,128,128]{2,1,0:T(8,128)(2,1)S(1)}, bf16[2,128,128]{2,1,0:T(8,128)(2,1)S(1)}, u32[]{:S(2)}, u32[]{:S(2)}) collective-permute-start(bf16[2,128,128]{2,1,0:T(8,128)(2,1)S(1)} %copy-done.11), channel_id=1, source_target_pairs={{0,6},{1,7},{2,0},{3,1},{4,2},{5,3},{6,4},{7,5},{8,14},{9,15},{10,... | collective-permute-start | bytes 196616 | tf_op jit(solution)/shard_map/ppermute | solution.py:245
  (24 other events, 352.9 us)

commit v7 on v6

--- a/solution.py
+++ b/solution.py
@@ -52,7 +52,7 @@
         o, c = work[w]
         return pltpu.make_async_copy(buf.at[w % slots, pl.ds(0, size)], outs[o].at[pl.ds(c * size, size)], out_sem.at[w % slots])
 
-    ahead = slots // 2
+    ahead = slots - 1
     for w in range(min(ahead, len(work))):
         load(w).start()
     new_copy.wait()
@@ -73,7 +73,7 @@
             @pl.when((row >= 0) & (row < seq_local))
             def _():
                 old = buf[w % slots, i]
-                buf[w % slots, i] = jnp.where(positions == row, new32[pl.ds(b, 1), :], old.astype(jnp.float32)).astype(old.dtype)
+                buf[w % slots, i] = jnp.where(positions == row, new32[pl.ds(b, 1), :].astype(old.dtype), old)
 
             return carry
 
@@ -102,7 +102,7 @@
         @pl.when((row >= 0) & (row < seq_local))
         def _():
             old = out_ref[b]
-            out_ref[b] = jnp.where(positions == row, new32[b:b + 1, :], old.astype(jnp.float32)).astype(old.dtype)
+            out_ref[b] = jnp.where(positions == row, new32[b:b + 1, :].astype(old.dtype), old)
 
 
 def pack_first(n, lens, src, new, peer, count):
@@ -240,7 +240,7 @@
             slabs = []
             if c == 0:
                 slabs.append(pack_first(n, lens, caches[a], news[a], peers[0], count))
-            slabs += pack(n, lens, caches[a], news[a], peers[len(slabs):] + own, first, count, 1, 4)
+            slabs += pack(n, lens, caches[a], news[a], peers[len(slabs):] + own, first, count, 1, 8)
             for i, peer in enumerate(peers):
                 slabs[i] = lax.ppermute(slabs[i], "tp", pairs(n, *peer))
             got.append(slabs)

time: 416 us -> 413 us (level)
  Pallas kernels: 106 us -> 98.7 us
    pallas_call x5, Pallas kernels: 39.4 us -> 32.4 us  [pack(): pl.pallas_call(functools.partial(pack_kernel, n, peers, first, pieces), o...]
  transfers between devices with their start and end apart: 35 -> 35, of which waited for: 7 -> 8; matrix products, arithmetic and copies ran while one was open for 0% -> 0% of each run, Pallas kernels for 24% -> 23%
where the time goes in v7:
time: 413 us
  waiting for transfers between devices  240 us (58%)
  Pallas kernels  98.7 us (24%)
  starting transfers between devices  72.2 us (17%)
    ppermute x35, waiting for transfers between devices, local_step(): slabs[i] = lax.ppermute(slabs[i], 'tp', pairs(n, *peer))  240 us
    ppermute x35, starting transfers between devices, local_step(): slabs[i] = lax.ppermute(slabs[i], 'tp', pairs(n, *peer))  72.2 us
    pallas_call x4, Pallas kernels, relayout(): pl.pallas_call(functools.partial(relayout_kernel, n, sources), grid=(coun...  35.3 us
    pallas_call x5, Pallas kernels, pack(): pl.pallas_call(functools.partial(pack_kernel, n, peers, first, pieces), o...  32.4 us
    pallas_call x1, Pallas kernels, local_step(): attn = attend(lens, query, k_cache, v_cache, k_new, v_new)  28.7 us
  transfers between devices with their start and end apart: 35, of which 8 were waited for; matrix products, arithmetic and copies ran while one was open for 0% of the time, Pallas kernels for 23%

profile of v7, /device:TPU:113, one launch (start us, length us, event | category | flops | bytes accessed | tf_op | source)
XLA Modules:
  0.0 413.0 jit_solution(18010473151444188676)
XLA Ops:
  0.6 4.2 %shard_map.90 = (bf16[12,128,128]{2,1,0:T(8,128)(2,1)}, bf16[12,128,128]{2,1,0:T(8,128)(2,1)}, bf16[12,128,128]{2,1,0:T(8,128)(2,1)}, bf16[12,128,128]{2,1,0:T(8...) custom-call(s32[64]{0:T(128)} %lens_ref.13, ...), custom_call_target="tpu_custom_call" | custom-call | flops 384000000 | bytes 6291456 | tf_op jit(solution)/shard_map/pallas_call | solution.py:129
  4.8 3.9 collective-permute-start.21
  9.6 3.3 shard_map.89
  12.8 3.2 collective-permute-start.14
  17.0 10.3 %collective-permute-done.14.refs_0_ = bf16[2,128,128]{2,1,0:T(8,128)(2,1)S(1)} collective-permute-done((bf16[2,128,128]{2,1,0:T(8,128)(2,1)}, bf16[2,128,128]{2,1,0:T(8,128)(2,1)S(1)}, u32[]{:S(2)}, u32[]{:S(2)}) %collective-permute-start.14) | collective-permute-done | bytes 65568 | tf_op jit(solution)/shard_map/ppermute | solution.py:245
  27.9 2.8 collective-permute-start.24
  38.6 2.7 collective-permute-start.7
  41.3 4.2 %shard_map.86 = (bf16[16,128,128]{2,1,0:T(8,128)(2,1)}, bf16[16,128,128]{2,1,0:T(8,128)(2,1)}, bf16[16,128,128]{2,1,0:T(8,128)(2,1)}, bf16[16,128,128]{2,1,0:T(8...) custom-call(s32[64]{0:T(128)} %lens_ref.13, ...), custom_call_target="tpu_custom_call" | custom-call | flops 448000000 | bytes 7340032 | tf_op jit(solution)/shard_map/pallas_call | solution.py:129
  50.0 23.4 %collective-permute-start.10 = (bf16[16,128,128]{2,1,0:T(8,128)(2,1)}, bf16[16,128,128]{2,1,0:T(8,128)(2,1)}, u32[]{:S(2)}, u32[]{:S(2)}) collective-permute-start(bf16[16,128,128]{2,1,0:T(8,128)(2,1)} %get-tuple-element.52), channel_id=1, source_target_pairs={{0,6},{1,7},{2,0},{3,1},{4,2},{5,3},{6,4},{7,5},{8,14},{9,15},{10,... | collective-permute-start | bytes 1572872 | tf_op jit(solution)/shard_map/ppermute | solution.py:245
  73.4 10.2 %shard_map.85 = (bf16[48,128,128]{2,1,0:T(8,128)(2,1)}, bf16[48,128,128]{2,1,0:T(8,128)(2,1)}, bf16[48,128,128]{2,1,0:T(8,128)(2,1)}, bf16[48,128,128]{2,1,0:T(8...) custom-call(s32[64]{0:T(128)} %lens_ref.13, ...), custom_call_target="tpu_custom_call" | custom-call | flops 1536000000 | bytes 25165824 | tf_op jit(solution)/shard_map/pallas_call | solution.py:129
  87.1 2.7 collective-permute-start.3
  89.8 3.0 collective-permute-done.11.refs_4_
  92.7 105.2 %collective-permute-done.12.refs_5_ = bf16[16,128,128]{2,1,0:T(8,128)(2,1)S(1)} collective-permute-done((bf16[16,128,128]{2,1,0:T(8,128)(2,1)}, bf16[16,128,128]{2,1,0:T(8,128)(2,1)S(1)}, u32[]{:S(2)}, u32[]{:S(2)}) %collective-permute-start.12) | collective-permute-done | bytes 524320 | tf_op jit(solution)/shard_map/ppermute | solution.py:245
  197.9 10.5 %shard_map.91 = (bf16[50,128,128]{2,1,0:T(8,128)(2,1)}, bf16[50,128,128]{2,1,0:T(8,128)(2,1)}, bf16[50,128,128]{2,1,0:T(8,128)(2,1)}, bf16[50,128,128]{2,1,0:T(8...) custom-call(s32[64]{0:T(128)} %lens_ref.13, ...), custom_call_target="tpu_custom_call" | custom-call | flops 1600000000 | bytes 26214400 | tf_op jit(solution)/shard_map/pallas_call | solution.py:129
  209.1 2.9 collective-permute-start.29
  215.3 101.7 %collective-permute-done.4.refs_4_ = bf16[48,128,128]{2,1,0:T(8,128)(2,1)} collective-permute-done((bf16[48,128,128]{2,1,0:T(8,128)(2,1)}, bf16[48,128,128]{2,1,0:T(8,128)(2,1)}, u32[]{:S(2)}, u32[]{:S(2)}) %collective-permute-start.4) | collective-permute-done | bytes 1572896 | tf_op jit(solution)/shard_map/ppermute | solution.py:245
  319.8 3.0 collective-permute-start.33
  323.5 28.7 %attend.1 = bf16[64,4,128]{2,1,0:T(4,128)(2,1)} custom-call(s32[64]{0:T(128)} %lens_ref.13, bf16[64,4,128]{2,1,0:T(4,128)(2,1)} %q_ref.1, bf16[64,1024,128]{2,1,0:T(8,128)(2,1)} %bitcast.7, bf16[64,1024,128]{2,1,0:T(8,128)(2,1)} %bitcast.11, bf16[64,128]{1,0:T(8,128)(2,1)} %bitcast.15, bf16[64,128]{1,0:T(8,128)(2,1)} %bitcast.19), custom_call_target="tpu_custom_call" | custom-call | flops 99999997952 | bytes 33554432 | tf_op jit(solution)/shard_map/attend/pallas_call | solution.py:263
  352.2 6.3 %shard_map.87.refs_8_ = bf16[64,128,8,128]{3,2,1,0:T(8,128)(2,1)} custom-call(bf16[16,128,128]{2,1,0:T(8,128)(2,1)} %collective-permute-done.7.refs_0_, bf16[16,128,128]{2,1,0:T(8,128)(2,1)} %collective-permute-done.8.refs_1_, bf16[16,128,128]{2,1,0:T(8,128)(2,1)} %collective-permute-done.9.refs_2_, bf16[16,128,128]{2,1,0:T(8,128)(2,1)} %collective-permute-done.10.refs_3_, ...), custom_call_target="tpu_custom_call" | custom-call | flops 640000000 | bytes 8388608 | tf_op jit(solution)/shard_map/pallas_call | solution.py:182
  358.5 12.3 %shard_map.88 = bf16[64,128,8,128]{3,2,1,0:T(8,128)(2,1)} custom-call(bf16[48,128,128]{2,1,0:T(8,128)(2,1)} %collective-permute-done.refs_0_, bf16[48,128,128]{2,1,0:T(8,128)(2,1)} %collective-permute-done.1.refs_1_, bf16[48,128,128]{2,1,0:T(8,128)(2,1)} %collective-permute-done.2.refs_2_, ...), custom_call_target="tpu_custom_call", output_to_operand_aliasing={{}: (8, {})} | custom-call | flops 1920000000 | bytes 25165824 | tf_op jit(solution)/shard_map/pallas_call | solution.py:182
  373.6 18.2 %collective-permute-done.32.refs_4_ = bf16[50,128,128]{2,1,0:T(8,128)(2,1)} collective-permute-done((bf16[50,128,128]{2,1,0:T(8,128)(2,1)}, bf16[50,128,128]{2,1,0:T(8,128)(2,1)}, u32[]{:S(2)}, u32[]{:S(2)}) %collective-permute-start.32) | collective-permute-done | bytes 1638432 | tf_op jit(solution)/shard_map/ppermute | solution.py:245
  391.8 2.9 collective-permute-start.19
  395.0 12.4 %shard_map.92.refs_8_ = bf16[64,128,8,128]{3,2,1,0:T(8,128)(2,1)} custom-call(bf16[50,128,128]{2,1,0:T(8,128)(2,1)} %collective-permute-done.28.refs_0_, bf16[50,128,128]{2,1,0:T(8,128)(2,1)} %collective-permute-done.29.refs_1_, bf16[50,128,128]{2,1,0:T(8,128)(2,1)} %collective-permute-done.30.refs_2_, ...), custom_call_target="tpu_custom_call" | custom-call | flops 2000000000 | bytes 26214400 | tf_op jit(solution)/shard_map/pallas_call | solution.py:182
  407.5 4.3 %shard_map.93.refs_8_ = bf16[64,128,8,128]{3,2,1,0:T(8,128)(2,1)} custom-call(bf16[12,128,128]{2,1,0:T(8,128)(2,1)} %copy-done.6, bf16[12,128,128]{2,1,0:T(8,128)(2,1)} %copy-done.7, bf16[12,128,128]{2,1,0:T(8,128)(2,1)} %collective-permute-done.23.refs_2_, bf16[12,128,128]{2,1,0:T(8,128)(2,1)} %collective-permute-done.24.refs_3_, ...), custom_call_target="tpu_custom_call", output_to_operand_aliasing={{}: (8, {})} | custom-call | flops 480000000 | bytes 6291456 | tf_op jit(solution)/shard_map/pallas_call | solution.py:182
  (84 shorter events, 29.8 us)
Async XLA Ops:
  4.8 28.0 %collective-permute-start.21 = (bf16[12,128,128]{2,1,0:T(8,128)(2,1)}, bf16[12,128,128]{2,1,0:T(8,128)(2,1)S(1)}, u32[]{:S(2)}, u32[]{:S(2)}) collective-permute-start(bf16[12,128,128]{2,1,0:T(8,128)(2,1)} %get-tuple-element.65), channel_id=1, source_target_pairs={{0,4},{1,5},{2,6},{3,7},{4,0},{5,1},{6,2},{7,3},{8,12},{9,13},{10,... | collective-permute-start | bytes 1179656 | tf_op jit(solution)/shard_map/ppermute | solution.py:245
  8.7 26.2 %collective-permute-start.22 = (bf16[12,128,128]{2,1,0:T(8,128)(2,1)}, bf16[12,128,128]{2,1,0:T(8,128)(2,1)S(1)}, u32[]{:S(2)}, u32[]{:S(2)}) collective-permute-start(bf16[12,128,128]{2,1,0:T(8,128)(2,1)} %get-tuple-element.66), channel_id=1, source_target_pairs={{0,5},{1,4},{2,7},{3,6},{4,1},{5,0},{6,3},{7,2},{8,13},{9,12},{10,... | collective-permute-start | bytes 1179656 | tf_op jit(solution)/shard_map/ppermute | solution.py:245
  35.0 38.4 %collective-permute-start.27 = (bf16[12,128,128]{2,1,0:T(8,128)(2,1)}, bf16[12,128,128]{2,1,0:T(8,128)(2,1)}, u32[]{:S(2)}, u32[]{:S(2)}) collective-permute-start(bf16[12,128,128]{2,1,0:T(8,128)(2,1)} %get-tuple-element.71), channel_id=1, source_target_pairs={{0,1},{1,0},{2,3},{3,2},{4,5},{5,4},{6,7},{7,6},{8,9},{9,8},{10,11... | collective-permute-start | bytes 1179656 | tf_op jit(solution)/shard_map/ppermute | solution.py:245
  38.6 45.1 %collective-permute-start.7 = (bf16[16,128,128]{2,1,0:T(8,128)(2,1)S(1)}, bf16[16,128,128]{2,1,0:T(8,128)(2,1)}, u32[]{:S(2)}, u32[]{:S(2)}) collective-permute-start(bf16[16,128,128]{2,1,0:T(8,128)(2,1)S(1)} %pack_first.1), channel_id=1, source_target_pairs={{0,4},{1,5},{2,6},{3,7},{4,0},{5,1},{6,2},{7,3},{8,12},{9,13},{10,... | collective-permute-start | bytes 1572872 | tf_op jit(solution)/shard_map/ppermute | solution.py:245
  45.5 38.3 %collective-permute-start.8 = (bf16[16,128,128]{2,1,0:T(8,128)(2,1)}, bf16[16,128,128]{2,1,0:T(8,128)(2,1)}, u32[]{:S(2)}, u32[]{:S(2)}) collective-permute-start(bf16[16,128,128]{2,1,0:T(8,128)(2,1)} %get-tuple-element.50), channel_id=1, source_target_pairs={{0,5},{1,4},{2,7},{3,6},{4,1},{5,0},{6,3},{7,2},{8,13},{9,12},{10,... | collective-permute-start | bytes 1572872 | tf_op jit(solution)/shard_map/ppermute | solution.py:245
  47.5 37.3 %collective-permute-start.9 = (bf16[16,128,128]{2,1,0:T(8,128)(2,1)}, bf16[16,128,128]{2,1,0:T(8,128)(2,1)}, u32[]{:S(2)}, u32[]{:S(2)}) collective-permute-start(bf16[16,128,128]{2,1,0:T(8,128)(2,1)} %get-tuple-element.51), channel_id=1, source_target_pairs={{0,2},{1,3},{2,4},{3,5},{4,6},{5,7},{6,0},{7,1},{8,10},{9,11},{10,... | collective-permute-start | bytes 1572872 | tf_op jit(solution)/shard_map/ppermute | solution.py:245
  50.0 37.2 %collective-permute-start.10 = (bf16[16,128,128]{2,1,0:T(8,128)(2,1)}, bf16[16,128,128]{2,1,0:T(8,128)(2,1)}, u32[]{:S(2)}, u32[]{:S(2)}) collective-permute-start(bf16[16,128,128]{2,1,0:T(8,128)(2,1)} %get-tuple-element.52), channel_id=1, source_target_pairs={{0,6},{1,7},{2,0},{3,1},{4,2},{5,3},{6,4},{7,5},{8,14},{9,15},{10,... | collective-permute-start | bytes 1572872 | tf_op jit(solution)/shard_map/ppermute | solution.py:245
  83.6 125.5 %collective-permute-start = (bf16[48,128,128]{2,1,0:T(8,128)(2,1)}, bf16[48,128,128]{2,1,0:T(8,128)(2,1)}, u32[]{:S(2)}, u32[]{:S(2)}) collective-permute-start(bf16[48,128,128]{2,1,0:T(8,128)(2,1)} %get-tuple-element.42), channel_id=1, source_target_pairs={{0,4},{1,5},{2,6},{3,7},{4,0},{5,1},{6,2},{7,3},{8,12},{9,13},{10,... | collective-permute-start | bytes 4718600 | tf_op jit(solution)/shard_map/ppermute | solution.py:245
  83.8 128.2 %collective-permute-start.1 = (bf16[48,128,128]{2,1,0:T(8,128)(2,1)}, bf16[48,128,128]{2,1,0:T(8,128)(2,1)}, u32[]{:S(2)}, u32[]{:S(2)}) collective-permute-start(bf16[48,128,128]{2,1,0:T(8,128)(2,1)} %get-tuple-element.43), channel_id=1, source_target_pairs={{0,5},{1,4},{2,7},{3,6},{4,1},{5,0},{6,3},{7,2},{8,13},{9,12},{10,... | collective-permute-start | bytes 4718600 | tf_op jit(solution)/shard_map/ppermute | solution.py:245
  84.8 127.6 %collective-permute-start.2 = (bf16[48,128,128]{2,1,0:T(8,128)(2,1)}, bf16[48,128,128]{2,1,0:T(8,128)(2,1)}, u32[]{:S(2)}, u32[]{:S(2)}) collective-permute-start(bf16[48,128,128]{2,1,0:T(8,128)(2,1)} %get-tuple-element.44), channel_id=1, source_target_pairs={{0,2},{1,3},{2,4},{3,5},{4,6},{5,7},{6,0},{7,1},{8,10},{9,11},{10,... | collective-permute-start | bytes 4718600 | tf_op jit(solution)/shard_map/ppermute | solution.py:245
  87.1 127.8 %collective-permute-start.3 = (bf16[48,128,128]{2,1,0:T(8,128)(2,1)}, bf16[48,128,128]{2,1,0:T(8,128)(2,1)}, u32[]{:S(2)}, u32[]{:S(2)}) collective-permute-start(bf16[48,128,128]{2,1,0:T(8,128)(2,1)} %get-tuple-element.45), channel_id=1, source_target_pairs={{0,6},{1,7},{2,0},{3,1},{4,2},{5,3},{6,4},{7,5},{8,14},{9,15},{10,... | collective-permute-start | bytes 4718600 | tf_op jit(solution)/shard_map/ppermute | solution.py:245
  92.7 105.2 %collective-permute-start.12 = (bf16[16,128,128]{2,1,0:T(8,128)(2,1)}, bf16[16,128,128]{2,1,0:T(8,128)(2,1)S(1)}, u32[]{:S(2)}, u32[]{:S(2)}) collective-permute-start(bf16[16,128,128]{2,1,0:T(8,128)(2,1)} %get-tuple-element.54), channel_id=1, source_target_pairs={{0,7},{1,6},{2,1},{3,0},{4,3},{5,2},{6,5},{7,4},{8,15},{9,14},{10,... | collective-permute-start | bytes 1572872 | tf_op jit(solution)/shard_map/ppermute | solution.py:245
  208.4 111.3 %collective-permute-start.28 = (bf16[50,128,128]{2,1,0:T(8,128)(2,1)}, bf16[50,128,128]{2,1,0:T(8,128)(2,1)}, u32[]{:S(2)}, u32[]{:S(2)}) collective-permute-start(bf16[50,128,128]{2,1,0:T(8,128)(2,1)} %get-tuple-element.73), channel_id=1, source_target_pairs={{0,4},{1,5},{2,6},{3,7},{4,0},{5,1},{6,2},{7,3},{8,12},{9,13},{10,... | collective-permute-start | bytes 4915208 | tf_op jit(solution)/shard_map/ppermute | solution.py:245
  209.1 113.6 %collective-permute-start.29 = (bf16[50,128,128]{2,1,0:T(8,128)(2,1)}, bf16[50,128,128]{2,1,0:T(8,128)(2,1)}, u32[]{:S(2)}, u32[]{:S(2)}) collective-permute-start(bf16[50,128,128]{2,1,0:T(8,128)(2,1)} %get-tuple-element.74), channel_id=1, source_target_pairs={{0,5},{1,4},{2,7},{3,6},{4,1},{5,0},{6,3},{7,2},{8,13},{9,12},{10,... | collective-permute-start | bytes 4915208 | tf_op jit(solution)/shard_map/ppermute | solution.py:245
  212.0 104.9 %collective-permute-start.4 = (bf16[48,128,128]{2,1,0:T(8,128)(2,1)}, bf16[48,128,128]{2,1,0:T(8,128)(2,1)}, u32[]{:S(2)}, u32[]{:S(2)}) collective-permute-start(bf16[48,128,128]{2,1,0:T(8,128)(2,1)} %get-tuple-element.46), channel_id=1, source_target_pairs={{0,3},{1,2},{2,5},{3,4},{4,7},{5,6},{6,1},{7,0},{8,11},{9,10},{10,... | collective-permute-start | bytes 4718600 | tf_op jit(solution)/shard_map/ppermute | solution.py:245
  212.5 104.7 %collective-permute-start.5 = (bf16[48,128,128]{2,1,0:T(8,128)(2,1)}, bf16[48,128,128]{2,1,0:T(8,128)(2,1)}, u32[]{:S(2)}, u32[]{:S(2)}) collective-permute-start(bf16[48,128,128]{2,1,0:T(8,128)(2,1)} %get-tuple-element.47), channel_id=1, source_target_pairs={{0,7},{1,6},{2,1},{3,0},{4,3},{5,2},{6,5},{7,4},{8,15},{9,14},{10,... | collective-permute-start | bytes 4718600 | tf_op jit(solution)/shard_map/ppermute | solution.py:245
  215.0 104.8 %collective-permute-start.6 = (bf16[48,128,128]{2,1,0:T(8,128)(2,1)}, bf16[48,128,128]{2,1,0:T(8,128)(2,1)}, u32[]{:S(2)}, u32[]{:S(2)}) collective-permute-start(bf16[48,128,128]{2,1,0:T(8,128)(2,1)} %get-tuple-element.48), channel_id=1, source_target_pairs={{0,1},{1,0},{2,3},{3,2},{4,5},{5,4},{6,7},{7,6},{8,9},{9,8},{10,11... | collective-permute-start | bytes 4718600 | tf_op jit(solution)/shard_map/ppermute | solution.py:245
  316.9 53.9 %collective-permute-start.30 = (bf16[50,128,128]{2,1,0:T(8,128)(2,1)}, bf16[50,128,128]{2,1,0:T(8,128)(2,1)}, u32[]{:S(2)}, u32[]{:S(2)}) collective-permute-start(bf16[50,128,128]{2,1,0:T(8,128)(2,1)} %get-tuple-element.75), channel_id=1, source_target_pairs={{0,2},{1,3},{2,4},{3,5},{4,6},{5,7},{6,0},{7,1},{8,10},{9,11},{10,... | collective-permute-start | bytes 4915208 | tf_op jit(solution)/shard_map/ppermute | solution.py:245
  317.1 53.8 %collective-permute-start.31 = (bf16[50,128,128]{2,1,0:T(8,128)(2,1)}, bf16[50,128,128]{2,1,0:T(8,128)(2,1)}, u32[]{:S(2)}, u32[]{:S(2)}) collective-permute-start(bf16[50,128,128]{2,1,0:T(8,128)(2,1)} %get-tuple-element.76), channel_id=1, source_target_pairs={{0,6},{1,7},{2,0},{3,1},{4,2},{5,3},{6,4},{7,5},{8,14},{9,15},{10,... | collective-permute-start | bytes 4915208 | tf_op jit(solution)/shard_map/ppermute | solution.py:245
  319.7 72.0 %collective-permute-start.32 = (bf16[50,128,128]{2,1,0:T(8,128)(2,1)}, bf16[50,128,128]{2,1,0:T(8,128)(2,1)}, u32[]{:S(2)}, u32[]{:S(2)}) collective-permute-start(bf16[50,128,128]{2,1,0:T(8,128)(2,1)} %get-tuple-element.77), channel_id=1, source_target_pairs={{0,3},{1,2},{2,5},{3,4},{4,7},{5,6},{6,1},{7,0},{8,11},{9,10},{10,... | collective-permute-start | bytes 4915208 | tf_op jit(solution)/shard_map/ppermute | solution.py:245
  319.8 72.0 %collective-permute-start.33 = (bf16[50,128,128]{2,1,0:T(8,128)(2,1)}, bf16[50,128,128]{2,1,0:T(8,128)(2,1)}, u32[]{:S(2)}, u32[]{:S(2)}) collective-permute-start(bf16[50,128,128]{2,1,0:T(8,128)(2,1)} %get-tuple-element.78), channel_id=1, source_target_pairs={{0,7},{1,6},{2,1},{3,0},{4,3},{5,2},{6,5},{7,4},{8,15},{9,14},{10,... | collective-permute-start | bytes 4915208 | tf_op jit(solution)/shard_map/ppermute | solution.py:245
  322.7 72.1 %collective-permute-start.34 = (bf16[50,128,128]{2,1,0:T(8,128)(2,1)}, bf16[50,128,128]{2,1,0:T(8,128)(2,1)}, u32[]{:S(2)}, u32[]{:S(2)}) collective-permute-start(bf16[50,128,128]{2,1,0:T(8,128)(2,1)} %get-tuple-element.79), channel_id=1, source_target_pairs={{0,1},{1,0},{2,3},{3,2},{4,5},{5,4},{6,7},{7,6},{8,9},{9,8},{10,11... | collective-permute-start | bytes 4915208 | tf_op jit(solution)/shard_map/ppermute | solution.py:245
  370.8 40.9 %collective-permute-start.16 = (bf16[2,128,128]{2,1,0:T(8,128)(2,1)S(1)}, bf16[2,128,128]{2,1,0:T(8,128)(2,1)S(1)}, u32[]{:S(2)}, u32[]{:S(2)}) collective-permute-start(bf16[2,128,128]{2,1,0:T(8,128)(2,1)S(1)} %copy-done.12), channel_id=1, source_target_pairs={{0,2},{1,3},{2,4},{3,5},{4,6},{5,7},{6,0},{7,1},{8,10},{9,11},{10,... | collective-permute-start | bytes 196616 | tf_op jit(solution)/shard_map/ppermute | solution.py:245
  370.9 40.8 %collective-permute-start.17 = (bf16[2,128,128]{2,1,0:T(8,128)(2,1)S(1)}, bf16[2,128,128]{2,1,0:T(8,128)(2,1)S(1)}, u32[]{:S(2)}, u32[]{:S(2)}) collective-permute-start(bf16[2,128,128]{2,1,0:T(8,128)(2,1)S(1)} %copy-done.11), channel_id=1, source_target_pairs={{0,6},{1,7},{2,0},{3,1},{4,2},{5,3},{6,4},{7,5},{8,14},{9,15},{10,... | collective-permute-start | bytes 196616 | tf_op jit(solution)/shard_map/ppermute | solution.py:245
  (24 other events, 349.3 us)
